TPU v7x, 32 devices: a whole 2x2x4 slice. The times are simulated.
32 devices in a mesh: row: 4 (over z), ctx: 4 (over y, core), seq: 2 (over x).
Axes of the slice: x: 2, y: 2, z: 4, core: 2. Of those that a mesh axis runs over, the one named last changes fastest.
Arguments:
- layer_input: bfloat16 [4, 2048, 1536], P('row', ('ctx', 'seq')), may hold values from -6 to 6
- norm_gain1: bfloat16 [1536], P(('row', 'ctx')), may hold values from 0.5 to 1.5
- qkvu_weight: bfloat16 [1536, 6144], P(('row', 'ctx')), may hold values from -0.21875 to 0.21875
- beta_weight: bfloat16 [1536, 12], P(('row', 'ctx')), may hold values from -0.15625 to 0.15625
- conv_kernel: bfloat16 [4, 1536], P(None, ('row', 'ctx')), may hold values from -3 to 3
- out_weight: bfloat16 [1536, 1536], P(('row', 'ctx')), may hold values from -0.875 to 0.875
- norm_gain2: bfloat16 [1536], P(('row', 'ctx')), may hold values from 0.5 to 1.5
- gate_up_weight: bfloat16 [1536, 8192], P(('row', 'ctx')), may hold values from -0.15625 to 0.15625
- down_weight: bfloat16 [4096, 1536], P(('row', 'ctx')), may hold values from -0.09375 to 0.09375
- seq_len: int32 [4], P('row'), may hold values from 512 to 2048, as said below
- out_grad: bfloat16 [4, 2048, 1536], P('row', ('ctx', 'seq')), may hold values from -6 to 6
Outputs:
- layer_output: bfloat16 [4, 2048, 1536], P('row', ('ctx', 'seq'))
- input_grad: bfloat16 [4, 2048, 1536], P('row', ('ctx', 'seq'))
- gain1_grad: float32 [1536], P(('row', 'ctx'))
- qkvu_grad: float32 [1536, 6144], P(('row', 'ctx'))
- beta_grad: float32 [1536, 12], P(('row', 'ctx'))
- kernel_grad: float32 [4, 1536], P(None, ('row', 'ctx'))
- out_weight_grad: float32 [1536, 1536], P(('row', 'ctx'))
- gain2_grad: float32 [1536], P(('row', 'ctx'))
- gate_up_grad: float32 [1536, 8192], P(('row', 'ctx'))
- down_grad: float32 [4096, 1536], P(('row', 'ctx'))
Inputs may be any that keep to these rules, and one draw needn't show every extreme that they name: Each row holds one sequence in its first seq_len slots; one row has exactly 2048 tokens and another exactly 512.
All inputs are finite; a program needn't handle non-finite values.
Results may differ from a plain program's by a relative error of at most 0.015.
The roundings to bfloat16 on the way count: a program that leaves them out, or rounds other values in their place, can miss the bound.
Values may be sent and summed in bfloat16 or wider, within the bound.
A program may use at most 384 MiB of HBM per device.

v0:
```python
import jax
import jax.numpy as jnp
from jax import lax
from jax.sharding import PartitionSpec as P

highest = lax.Precision.HIGHEST
epsilon = 1e-06
negative = -1e30


def passed_along(value, axis, steps):
    count = lax.axis_size(axis)
    leading, last = (max(0, -steps), min(count, count - steps))
    return lax.ppermute(value, axis, [(source, source + steps) for source in range(leading, last)])


def rms_norm(values, gain):
    return values * lax.rsqrt(jnp.mean(values * values, -1, keepdims=True) + epsilon) * gain


def householder_span(scaled, keys, direction, strength):
    count = scaled.shape[0]
    head_size = scaled.shape[2]
    places = jnp.arange(count)
    below = places[:, None] > places[None, :]
    upto = places[:, None] >= places[None, :]
    rates = strength.T
    intersection = jnp.einsum("the,she->hts", direction, direction, precision=highest)
    lower_part = jnp.where(below[None], intersection * rates[:, None, :], 0.0)
    unit_lower = lower_part + jnp.eye(count, dtype=jnp.float32)[None]
    dir_keys = jnp.einsum("she,jhe->hsj", direction, keys, precision=highest)
    right_side = jnp.concatenate(
        [jnp.where(below[None], dir_keys, 0.0), jnp.transpose(direction, (1, 0, 2))], axis=2
    )
    solved = lax.linalg.triangular_solve(
        unit_lower, right_side, left_side=True, lower=True, unit_diagonal=True
    )
    key_coeffs = solved[:, :, :count]
    dir_coeffs = solved[:, :, count:]
    query_dirs = jnp.einsum("ihe,the->hit", scaled, direction, precision=highest)
    weighted = jnp.where(upto[None], query_dirs, 0.0) * rates[:, None, :]
    plain = jnp.einsum("ihe,jhe->hij", scaled, keys, precision=highest)
    intra = plain - jnp.einsum("hit,htj->hij", weighted, key_coeffs, precision=highest)
    query_hat = scaled - jnp.einsum("hit,hte->ihe", weighted, dir_coeffs, precision=highest)
    scaled_dirs = direction * strength[:, :, None]
    key_hat = keys - jnp.einsum("the,htj->jhe", scaled_dirs, key_coeffs, precision=highest)
    transform = jnp.eye(head_size, dtype=jnp.float32)[None] - jnp.einsum(
        "the,htf->hef", scaled_dirs, dir_coeffs, precision=highest
    )
    return (query_hat, key_hat, transform, intra)


def transform_span(queries, keys, raw, rim, logits, kernel):
    taps = kernel.shape[0]
    count = raw.shape[0]
    extended = jnp.concatenate([rim, raw], axis=0)
    conv = jnp.zeros(raw.shape, jnp.float32)
    for lag_index in range(taps):
        conv = (
            conv + kernel[lag_index] * extended[taps - 1 - lag_index : taps - 1 - lag_index + count]
        )
    direction = conv * lax.rsqrt(jnp.sum(conv * conv, -1, keepdims=True) + epsilon)
    strength = 2.0 * jax.nn.sigmoid(logits)
    scaled = queries * queries.shape[-1] ** (-0.5)
    return householder_span(scaled, keys, direction, strength)


def pass_on(block):
    return passed_along(block.astype(jnp.bfloat16), "ctx", 1).astype(block.dtype)


def pass_back(block):
    return passed_along(block.astype(jnp.bfloat16), "ctx", -1).astype(block.dtype)


def per_device(
    layer_input,
    norm_gain1,
    qkvu_weight,
    beta_weight,
    conv_kernel,
    out_weight,
    norm_gain2,
    gate_up_weight,
    down_weight,
    seq_len,
    out_grad,
):
    ctx_size = lax.axis_size("ctx")
    seq_groups = lax.axis_size("seq")
    ctx_index = lax.axis_index("ctx")
    seq_index = lax.axis_index("seq")
    tokens = layer_input[0].astype(jnp.float32)
    tok_count, width = tokens.shape
    heads = beta_weight.shape[1]
    head_size = width // heads
    local_heads = heads // seq_groups
    feature_count = local_heads * head_size
    span = tok_count * seq_groups
    taps = conv_kernel.shape[0]
    length = seq_len[0]
    slot_index = (ctx_index * seq_groups + seq_index) * tok_count + jnp.arange(tok_count)
    valid = (slot_index < length).astype(jnp.float32)[:, None]
    gain_one, wide_qkvu, wide_beta, wide_kernel, wide_out = (
        lax.all_gather(norm_gain1, ("row", "ctx"), axis=0, tiled=True),
        lax.all_gather(qkvu_weight, ("row", "ctx"), axis=0, tiled=True),
        lax.all_gather(beta_weight, ("row", "ctx"), axis=0, tiled=True),
        lax.all_gather(conv_kernel, ("row", "ctx"), axis=1, tiled=True),
        lax.all_gather(out_weight, ("row", "ctx"), axis=0, tiled=True),
    )
    gain_one = gain_one.astype(jnp.float32)
    h_first = rms_norm(tokens, gain_one).astype(jnp.bfloat16)
    projected = (
        jnp.dot(h_first, wide_qkvu, preferred_element_type=jnp.float32)
        .astype(jnp.bfloat16)
        .reshape(tok_count, 4, heads, head_size)
    )
    logit_tokens = (
        jnp.dot(h_first, wide_beta, preferred_element_type=jnp.float32)
        .astype(jnp.bfloat16)
        .reshape(tok_count, 1, heads)
    )
    head_proj, head_logits = (
        lax.all_to_all(projected, "seq", split_axis=2, concat_axis=0, tiled=True),
        lax.all_to_all(logit_tokens, "seq", split_axis=2, concat_axis=0, tiled=True),
    )
    raw_dirs = head_proj[:, 3]
    rim = passed_along(raw_dirs[span - (taps - 1) :], "ctx", 1)
    kernel_local = (
        lax.dynamic_slice_in_dim(wide_kernel, seq_index * feature_count, feature_count, 1)
        .astype(jnp.float32)
        .reshape(taps, local_heads, head_size)
    )
    query_in = head_proj[:, 0].astype(jnp.float32)
    key_in = head_proj[:, 1].astype(jnp.float32)
    value_in = head_proj[:, 2].astype(jnp.float32)
    raw_in = raw_dirs.astype(jnp.float32)
    rim_in = rim.astype(jnp.float32)
    logit_in = head_logits[:, 0].astype(jnp.float32)
    query_hat, key_hat, transform, intra = transform_span(
        query_in, key_in, raw_in, rim_in, logit_in, kernel_local
    )
    columns = jnp.arange(span)
    intra_mask = (columns[None, :] <= columns[:, None]) & (
        ctx_index * span + columns[None, :] < length
    )

    def block_mask(cycle_step):
        key_slots = (ctx_index - cycle_step) * span + columns
        return ((ctx_index >= cycle_step) & (key_slots < length))[None, :]

    first_masked = jnp.where(intra_mask[None], intra, negative)
    first_peak = jnp.max(first_masked, -1)
    first_weights = jnp.where(intra_mask[None], jnp.exp(first_masked - first_peak[:, :, None]), 0.0)
    first_total = jnp.sum(first_weights, -1)
    first_summed = jnp.einsum("hij,jhe->ihe", first_weights, value_in, precision=highest)
    state = (first_peak, first_total, first_summed)
    kept = []
    carried = jnp.stack([key_hat, value_in])
    for cycle_step in range(1, ctx_size):
        received = pass_on(carried)
        kept.append(received)
        mask_now = block_mask(cycle_step)

        def merge_block(state=state, received=received, mask_now=mask_now):
            peak, total, summed = state
            scores = jnp.einsum("ihe,jhe->hij", query_hat, received[0], precision=highest)
            masked = jnp.where(mask_now[None], scores, negative)
            new_peak = jnp.maximum(peak, jnp.max(masked, -1))
            weights = jnp.where(mask_now[None], jnp.exp(masked - new_peak[:, :, None]), 0.0)
            factor = jnp.exp(peak - new_peak)
            total = total * factor + jnp.sum(weights, -1)
            summed = summed * factor.T[:, :, None] + jnp.einsum(
                "hij,jhe->ihe", weights, received[1], precision=highest
            )
            return (new_peak, total, summed)

        state = merge_block()
        if cycle_step < ctx_size - 1:
            moved = jnp.einsum("jhf,hef->jhe", received[0], transform, precision=highest)
            carried = jnp.stack([moved, received[1]])
    peak, total, summed = state
    safe_total = jnp.where(total > 0.0, total, 1.0)
    attn = summed / safe_total.T[:, :, None]
    log_total = peak + jnp.log(safe_total)
    back = lax.all_to_all(
        attn.astype(jnp.bfloat16), "seq", split_axis=0, concat_axis=1, tiled=True
    ).reshape(tok_count, width)
    x_mid = tokens + jnp.dot(back, wide_out, preferred_element_type=jnp.float32)
    gain_two, wide_gate_up, wide_down = (
        lax.all_gather(norm_gain2, ("row", "ctx"), axis=0, tiled=True),
        lax.all_gather(gate_up_weight, ("row", "ctx"), axis=0, tiled=True),
        lax.all_gather(down_weight, ("row", "ctx"), axis=0, tiled=True),
    )
    gain_two = gain_two.astype(jnp.float32)
    h_second = rms_norm(x_mid, gain_two).astype(jnp.bfloat16)
    gate_up = jnp.dot(h_second, wide_gate_up, preferred_element_type=jnp.float32)
    hidden_count = wide_down.shape[0]
    gate_part = gate_up[:, :hidden_count]
    up_part = gate_up[:, hidden_count:]
    sigmoid_gate = jax.nn.sigmoid(gate_part)
    silu_gate = gate_part * sigmoid_gate
    hidden = (silu_gate * up_part).astype(jnp.bfloat16)
    branch = jnp.dot(hidden, wide_down, preferred_element_type=jnp.float32)
    layer_output = (valid * (x_mid + branch)).astype(jnp.bfloat16)[None]
    grad_rows = valid * out_grad[0].astype(jnp.float32)
    grad_low = grad_rows.astype(jnp.bfloat16)
    down_term = jnp.einsum("tf,td->fd", hidden, grad_low, preferred_element_type=jnp.float32)
    d_hidden = jnp.einsum("td,fd->tf", grad_low, wide_down, preferred_element_type=jnp.float32)
    d_gate = d_hidden * up_part * sigmoid_gate * (1.0 + gate_part * (1.0 - sigmoid_gate))
    d_up = d_hidden * silu_gate
    d_gate_up = jnp.concatenate([d_gate, d_up], axis=1).astype(jnp.bfloat16)
    gate_up_term = jnp.einsum("td,tf->df", h_second, d_gate_up, preferred_element_type=jnp.float32)
    d_h_second = jnp.einsum(
        "tf,df->td", d_gate_up, wide_gate_up, preferred_element_type=jnp.float32
    )
    _, pull_second = jax.vjp(rms_norm, x_mid, gain_two)
    mid_norm_grad, gain_two_term = pull_second(d_h_second)
    d_mid = grad_rows + mid_norm_grad
    d_branch = d_mid.astype(jnp.bfloat16)
    out_term = jnp.einsum("td,te->de", back, d_branch, preferred_element_type=jnp.float32)
    d_back = (
        jnp.einsum("te,de->td", d_branch, wide_out, preferred_element_type=jnp.float32)
        .astype(jnp.bfloat16)
        .reshape(tok_count, heads, head_size)
    )
    d_attn = lax.all_to_all(d_back, "seq", split_axis=1, concat_axis=0, tiled=True).astype(
        jnp.float32
    )
    delta = jnp.sum(d_attn * attn, -1).T

    def block_grads(scores, mask_now, block_values):
        probs = jnp.where(
            mask_now[None],
            jnp.exp(jnp.where(mask_now[None], scores - log_total[:, :, None], negative)),
            0.0,
        )
        d_probs = jnp.einsum("ihe,jhe->hij", d_attn, block_values, precision=highest)
        d_scores = probs * (d_probs - delta[:, :, None])
        d_values = jnp.einsum("hij,ihe->jhe", probs, d_attn, precision=highest)
        return (d_scores, d_values)

    d_intra, d_values_own = block_grads(intra, intra_mask, value_in)
    d_query_hat = jnp.zeros(query_hat.shape, jnp.float32)
    d_transform = jnp.zeros(transform.shape, jnp.float32)
    outgoing = jnp.zeros((2, span, local_heads, head_size), jnp.float32)
    for cycle_step in reversed(range(1, ctx_size)):
        received = kept[cycle_step - 1]
        scores = jnp.einsum("ihe,jhe->hij", query_hat, received[0], precision=highest)
        d_scores, d_values_blk = block_grads(scores, block_mask(cycle_step), received[1])
        d_query_hat = d_query_hat + jnp.einsum(
            "hij,jhe->ihe", d_scores, received[0], precision=highest
        )
        d_keys_blk = jnp.einsum("hij,ihe->jhe", d_scores, query_hat, precision=highest)
        if cycle_step < ctx_size - 1:
            incoming = pass_back(outgoing)
            d_keys_blk = d_keys_blk + jnp.einsum(
                "jhe,hef->jhf", incoming[0], transform, precision=highest
            )
            d_transform = d_transform + jnp.einsum(
                "jhe,jhf->hef", incoming[0], received[0], precision=highest
            )
            d_values_blk = d_values_blk + incoming[1]
        outgoing = jnp.stack([d_keys_blk, d_values_blk])
    final = pass_back(outgoing)
    d_key_hat = final[0]
    d_values = d_values_own + final[1]
    _, pull_span = jax.vjp(transform_span, query_in, key_in, raw_in, rim_in, logit_in, kernel_local)
    d_query, d_key, d_raw, d_rim, d_logit, d_kernel = pull_span(
        (d_query_hat, d_key_hat, d_transform, d_intra)
    )
    rim_back = passed_along(d_rim, "ctx", -1)
    d_raw = jnp.concatenate(
        [d_raw[: span - (taps - 1)], d_raw[span - (taps - 1) :] + rim_back], axis=0
    )
    d_projected = jnp.stack([d_query, d_key, d_values, d_raw], axis=1).astype(jnp.bfloat16)
    d_logits = d_logit.astype(jnp.bfloat16)[:, None, :]
    tok_projected, tok_logits = (
        lax.all_to_all(d_projected, "seq", split_axis=0, concat_axis=2, tiled=True),
        lax.all_to_all(d_logits, "seq", split_axis=0, concat_axis=2, tiled=True),
    )
    flat_projected = tok_projected.reshape(tok_count, 4 * width)
    flat_logits = tok_logits.reshape(tok_count, heads)
    qkvu_term = jnp.einsum("td,tn->dn", h_first, flat_projected, preferred_element_type=jnp.float32)
    beta_term = jnp.einsum("td,th->dh", h_first, flat_logits, preferred_element_type=jnp.float32)
    d_h_first = jnp.einsum(
        "tn,dn->td", flat_projected, wide_qkvu, preferred_element_type=jnp.float32
    )
    d_h_first = d_h_first + jnp.einsum(
        "th,dh->td", flat_logits, wide_beta, preferred_element_type=jnp.float32
    )
    _, pull_first = jax.vjp(rms_norm, tokens, gain_one)
    input_norm_grad, gain_one_term = pull_first(d_h_first)
    input_grad = (d_mid + input_norm_grad).astype(jnp.bfloat16)[None]
    kernel_term = lax.dynamic_update_slice_in_dim(
        jnp.zeros((taps, width), jnp.float32),
        d_kernel.reshape(taps, feature_count),
        seq_index * feature_count,
        1,
    )
    terms = (
        gain_one_term,
        qkvu_term,
        beta_term,
        kernel_term,
        out_term,
        gain_two_term,
        gate_up_term,
        down_term,
    )
    shards = (
        lax.psum_scatter(terms[0], ("row", "ctx"), scatter_dimension=0, tiled=True),
        lax.psum_scatter(terms[1], ("row", "ctx"), scatter_dimension=0, tiled=True),
        lax.psum_scatter(terms[2], ("row", "ctx"), scatter_dimension=0, tiled=True),
        lax.psum_scatter(terms[3], ("row", "ctx"), scatter_dimension=1, tiled=True),
        lax.psum_scatter(terms[4], ("row", "ctx"), scatter_dimension=0, tiled=True),
        lax.psum_scatter(terms[5], ("row", "ctx"), scatter_dimension=0, tiled=True),
        lax.psum_scatter(terms[6], ("row", "ctx"), scatter_dimension=0, tiled=True),
        lax.psum_scatter(terms[7], ("row", "ctx"), scatter_dimension=0, tiled=True),
    )
    shards = (
        lax.psum(shards[0].astype(jnp.bfloat16), "seq").astype(jnp.float32),
        lax.psum(shards[1].astype(jnp.bfloat16), "seq").astype(jnp.float32),
        lax.psum(shards[2].astype(jnp.bfloat16), "seq").astype(jnp.float32),
        lax.psum(shards[3].astype(jnp.bfloat16), "seq").astype(jnp.float32),
        lax.psum(shards[4].astype(jnp.bfloat16), "seq").astype(jnp.float32),
        lax.psum(shards[5].astype(jnp.bfloat16), "seq").astype(jnp.float32),
        lax.psum(shards[6].astype(jnp.bfloat16), "seq").astype(jnp.float32),
        lax.psum(shards[7].astype(jnp.bfloat16), "seq").astype(jnp.float32),
    )
    return (
        layer_output,
        input_grad,
        shards[0],
        shards[1],
        shards[2],
        shards[3],
        shards[4],
        shards[5],
        shards[6],
        shards[7],
    )


def solution(mesh):
    return jax.shard_map(
        per_device,
        mesh=mesh,
        in_specs=(
            P("row", ("ctx", "seq"), None),
            P(("row", "ctx")),
            P(("row", "ctx"), None),
            P(("row", "ctx"), None),
            P(None, ("row", "ctx")),
            P(("row", "ctx"), None),
            P(("row", "ctx")),
            P(("row", "ctx"), None),
            P(("row", "ctx"), None),
            P("row"),
            P("row", ("ctx", "seq"), None),
        ),
        out_specs=(
            P("row", ("ctx", "seq"), None),
            P("row", ("ctx", "seq"), None),
            P(("row", "ctx")),
            P(("row", "ctx"), None),
            P(("row", "ctx"), None),
            P(None, ("row", "ctx")),
            P(("row", "ctx"), None),
            P(("row", "ctx")),
            P(("row", "ctx"), None),
            P(("row", "ctx"), None),
        ),
        check_vma=False,
    )
```

profile of v0, /device:TPU:1, one launch (start us, length us, event | category | flops | bytes accessed | tf_op | source)
XLA Modules:
  0.0 2164.8 jit_solution(6833607285970077673)
XLA Ops:
  11.2 32.8 %all-reduce.15 = (bf16[1536]{0:T(1024)(128)(2,1)S(1)}, bf16[1536]{0:T(1024)(128)(2,1)S(1)}) all-reduce(bf16[1536]{0:T(1024)(128)(2,1)S(1)} %dynamic-update-slice.4, bf16[1536]{0:T(1024)(128)(2,1)S(1)} %dynamic-update-slice.5), channel_id=1, replica_groups=mesh['row'=4,'ctx'=4,'seq'=2] {'row','ctx'}, use_global_device_ids=true, to_apply=%add.10 | all-reduce | flops 3072 | bytes 12288
  44.1 22.7 %all-gather.1 = bf16[16,96,12]{1,2,0:T(8,128)(2,1)S(1)} all-gather(bf16[1,96,12]{1,2,0:T(8,128)(2,1)S(1)} %bitcast.629), channel_id=1, replica_groups=mesh['row'=4,'ctx'=4,'seq'=2] {'row','ctx'}, dimensions={0}, use_global_device_ids=true | all-gather | bytes 39168 | tf_op jit(solution)/shard_map/all_gather | solution.py:107
  73.8 38.7 %all-gather.7.cloned.1.call-done = bf16[1536,6144]{1,0:T(8,128)(2,1)} async-done(((bf16[96,6144]{1,0:T(8,128)(2,1)}), bf16[1536,6144]{1,0:T(8,128)(2,1)}) %all-gather.7.cloned.1.call-update) | async-done | bytes 18874384 | tf_op jit(solution)/shard_map/all_gather | solution.py:106
  112.6 13.0 convolution_convert_fusion
  135.4 21.2 all-gather
  192.3 16.0 while.3
  208.3 236.8 %custom-call.9 = f32[6,4,128,128]{2,3,1,0:T(8,128)S(1)} custom-call(f32[6,4,128,128]{3,2,1,0:T(8,128)} %bitcast.631), custom_call_target="InvertDiagBlocksLowerTriangular" | custom-call | tf_op jit(solution)/shard_map/triangular_solve/custom-call.1 | solution.py:35
  583.6 13.1 all-to-all-done.2
  604.4 14.1 fusion.368
  629.6 13.7 multiply_reduce_fusion.2
  650.2 16.8 fusion.295
  766.0 14.3 fusion.382
  780.3 13.1 fusion.381
  896.7 18.6 fusion
  974.9 14.4 fusion.5
  1030.2 34.9 %all_to_all.90 = bf16[512,4,6,128]{3,1,2,0:T(4,128)(2,1)S(1)} all-to-all(bf16[512,4,6,128]{3,1,2,0:T(4,128)(2,1)S(1)} %copy.489), channel_id=1, replica_groups=mesh['row'=4,'ctx'=4,'seq'=2] {'seq'}, dimensions={0} | all-to-all | bytes 6291456 | tf_op jit(solution)/shard_map/all_to_all | solution.py:279
  1072.2 16.8 fusion.301
  1090.4 31.8 %fusion.124 = f32[1536,8192]{1,0:T(8,128)} fusion(bf16[256,4096]{1,0:T(8,128)(2,1)} %get-tuple-element.75, bf16[256,4096]{1,0:T(8,128)(2,1)} %copy-done.85, f32[256,1536]{1,0:T(8,128)S(1)} %copy-done.45, f32[1536]{0:T(1024)S(1)} %copy-done.91, f32[256]{0:T(256)S(1)} %copy-done.108), kind=kOutput, calls=%fused_computation.177 | convolution fusion | flops 6452019200 | bytes 56105984 | tf_op jit(solution)/shard_map/td,tf->df/dot_general | solution.py:213
  1146.0 311.1 %reduce-scatter.11.cloned.1.call-done = f32[96,6144]{1,0:T(8,128)} async-done(((f32[1536,6144]{1,0:T(8,128)}), f32[96,6144]{1,0:T(8,128)}) %reduce-scatter.11.cloned.1.call-update) | async-done | bytes 2359312 | tf_op jit(solution)/shard_map/reduce_scatter | solution.py:313
  1459.9 466.4 %reduce-scatter.15.cloned.1.call-done = f32[96,8192]{1,0:T(8,128)} async-done(((f32[1536,8192]{1,0:T(8,128)}), f32[96,8192]{1,0:T(8,128)}) %reduce-scatter.15.cloned.1.call-update) | async-done | bytes 3145744 | tf_op jit(solution)/shard_map/reduce_scatter | solution.py:318
  1942.0 42.0 %reduce-scatter.21.cloned.1.call-done = f32[96,4]{1,0:T(8,128)} async-done(((f32[1536,4]{1,0:T(8,128)}), f32[96,4]{1,0:T(8,128)}) %reduce-scatter.21.cloned.1.call-update) | async-done | bytes 1552
  1984.8 58.9 %reduce-scatter.19.cloned.1.call-done = f32[96,12]{1,0:T(8,128)} async-done(((f32[1536,12]{1,0:T(8,128)}), f32[96,12]{1,0:T(8,128)}) %reduce-scatter.19.cloned.1.call-update) | async-done | bytes 4624
  2056.0 55.8 %all-reduce.14 = (bf16[1536]{0:T(1024)(128)(2,1)S(1)}, bf16[1536]{0:T(1024)(128)(2,1)S(1)}) all-reduce(f32[1536]{0:T(1024)S(1)} %get-tuple-element.33, f32[1536]{0:T(1024)S(1)} %copy-done.124), channel_id=2, replica_groups=mesh['row'=4,'ctx'=4,'seq'=2] {'row','ctx'}, use_global_device_ids=true, to_apply=%region_19.21.clone | all-reduce | flops 3072 | bytes 18432
  2121.4 27.7 %all-reduce.20.cloned.1.call-done = (bf16[96,6144]{1,0:T(8,128)(2,1)}, bf16[96,1536]{1,0:T(8,128)(2,1)}, bf16[96,8192]{1,0:T(8,128)(2,1)}, bf16[256,1536]{1,0:T(8,128)(2,1)}) async-done(((bf16[96,6144]{1,0:T(8,128)(2,1)}, bf16[96,1536]{1,0:T(8,128)(2,1)}, bf16[96,8192]{1,0:T(8,128)(2,1)}, bf16[256,1536]{1,0:T(8,128)(2,1)}), (bf16[96,6144]{1,0:T(8,128)(2,1)}, bf16[96,1536]{1,0:T(8,128)(2,1)}, ...) | async-done | bytes 3833872 | tf_op jit(solution)/shard_map/psum | solution.py:323
  (585 shorter events, 617.1 us)
Async XLA Ops:
  7.2 105.3 %all-gather.7.cloned.1.call-start = ((), (), s32[]{:S(2)}) async-start(), calls=%async_computation.12 | async-start | bytes 20054016 | tf_op jit(solution)/shard_map/all_gather | solution.py:106
  8.0 591.0 %all-gather.9.cloned.1.call-start = ((), (), s32[]{:S(2)}) async-start(), calls=%async_computation.13 | async-start | bytes 5013504 | tf_op jit(solution)/shard_map/all_gather | solution.py:109
  8.7 595.7 %all-gather.11.cloned.1.call-start = ((), (), s32[]{:S(2)}) async-start(), calls=%async_computation.14 | async-start | bytes 26738688 | tf_op jit(solution)/shard_map/all_gather | solution.py:192
  70.0 60.6 %all-to-all-start.1 = ((bf16[2,2,768]{2,1,0:T(2,128)(2,1)}), bf16[2,2,768]{2,1,0:T(2,128)(2,1)S(1)}, u32[]{:S(2)}, u32[]{:S(2)}) async-start(bf16[2,2,768]{2,1,0:T(2,128)(2,1)} %reshape.482), calls=%async_computation.1 | async-start | bytes 12288 | tf_op jit(solution)/shard_map/all_to_all | solution.py:125
  73.2 545.3 %all-gather.13.cloned.1.call-start = ((), (), s32[]{:S(2)}) async-start(), calls=%async_computation.15 | async-start | bytes 13369344 | tf_op jit(solution)/shard_map/all_gather | solution.py:193
  130.6 40.0 %all-to-all-start = ((bf16[256,4,12,128]{0,3,1,2:T(8,128)(2,1)}), bf16[256,4,12,128]{0,3,1,2:T(8,128)(2,1)S(1)}, u32[]{:S(2)}, u32[]{:S(2)}) async-start(bf16[256,4,12,128]{0,3,1,2:T(8,128)(2,1)} %copy.408), calls=%async_computation | async-start | bytes 6291456 | tf_op jit(solution)/shard_map/all_to_all | solution.py:124
  176.0 4.6 collective-permute-start
  484.6 19.9 collective-permute-start.1
  506.7 22.7 %collective-permute-start.2 = (bf16[2,512,6,128]{3,1,2,0:T(8,128)(2,1)}, bf16[2,512,6,128]{3,1,2,0:T(8,128)(2,1)S(1)}, u32[]{:S(2)}, u32[]{:S(2)}) collective-permute-start(bf16[2,512,6,128]{3,1,2,0:T(8,128)(2,1)} %pad_maximum_fusion.10), channel_id=1, source_target_pairs={{0,2},{2,4},{4,6},{1,3},{3,5},{5,7},{8,10},{10,12},{12,14},{9,11},... | collective-permute-start | bytes 4718600 | tf_op jit(solution)/shard_map/ppermute | solution.py:14
  530.5 21.2 collective-permute-start.3
  579.1 17.6 all-to-all-start.2
  583.5 558.1 %reduce-scatter.13.cloned.1.call-start = ((), (), s32[]{:S(2)}) async-start(), calls=%async_computation.17 | async-start | bytes 10027008 | tf_op jit(solution)/shard_map/reduce_scatter | solution.py:316
  650.1 493.3 %reduce-scatter.17.cloned.1.call-start = ((), (), s32[]{:S(2)}) async-start(), calls=%async_computation.19 | async-start | bytes 26738688 | tf_op jit(solution)/shard_map/reduce_scatter | solution.py:319
  675.1 15.3 all-to-all-start.3
  679.4 777.7 %reduce-scatter.11.cloned.1.call-start = ((), (), s32[]{:S(2)}) async-start(), calls=%async_computation.16 | async-start | bytes 40108032 | tf_op jit(solution)/shard_map/reduce_scatter | solution.py:313
  717.0 99.8 %collective-permute-start.4 = (bf16[2,512,6,128]{3,1,2,0:T(8,128)(2,1)}, bf16[2,512,6,128]{3,1,2,0:T(8,128)(2,1)}, u32[]{:S(2)}, u32[]{:S(2)}) collective-permute-start(bf16[2,512,6,128]{3,1,2,0:T(8,128)(2,1)} %pad_maximum_fusion.12), channel_id=1, source_target_pairs={{2,0},{4,2},{6,4},{3,1},{5,3},{7,5},{10,8},{12,10},{14,12},{11,9},... | collective-permute-start | bytes 4718600 | tf_op jit(solution)/shard_map/ppermute | solution.py:14
  827.4 27.6 %collective-permute-start.5 = (bf16[2,512,6,128]{3,1,2,0:T(8,128)(2,1)}, bf16[2,512,6,128]{3,1,2,0:T(8,128)(2,1)}, u32[]{:S(2)}, u32[]{:S(2)}) collective-permute-start(bf16[2,512,6,128]{3,1,2,0:T(8,128)(2,1)} %pad_maximum_fusion.13), channel_id=1, source_target_pairs={{2,0},{4,2},{6,4},{3,1},{5,3},{7,5},{10,8},{12,10},{14,12},{11,9},... | collective-permute-start | bytes 4718600 | tf_op jit(solution)/shard_map/ppermute | solution.py:14
  864.8 23.0 %collective-permute-start.6 = (bf16[2,512,6,128]{3,1,2,0:T(8,128)(2,1)S(1)}, bf16[2,512,6,128]{3,1,2,0:T(8,128)(2,1)S(1)}, u32[]{:S(2)}, u32[]{:S(2)}) collective-permute-start(bf16[2,512,6,128]{3,1,2,0:T(8,128)(2,1)S(1)} %pad_maximum_fusion.14), channel_id=1, source_target_pairs={{2,0},{4,2},{6,4},{3,1},{5,3},{7,5},{10,8},{12,10},{14,12},{11,9},... | collective-permute-start | bytes 4718600 | tf_op jit(solution)/shard_map/ppermute | solution.py:14
  1004.9 21.2 collective-permute-start.7
  1089.0 837.2 %reduce-scatter.15.cloned.1.call-start = ((), (), s32[]{:S(2)}) async-start(), calls=%async_computation.18 | async-start | bytes 53477376 | tf_op jit(solution)/shard_map/reduce_scatter | solution.py:318
  1133.1 5.9 all-to-all-start.5
  1136.3 847.6 %reduce-scatter.21.cloned.1.call-start = ((), (), s32[]{:S(2)}) async-start(), calls=%async_computation.21 | async-start | bytes 835584
  1137.6 906.1 %reduce-scatter.19.cloned.1.call-start = ((), (), s32[]{:S(2)}) async-start(), calls=%async_computation.20 | async-start | bytes 835584
  1140.8 1008.3 %all-reduce.20.cloned.1.call-start = ((), (), s32[]{:S(2)}) async-start(), calls=%async_computation.22 | async-start | bytes 7667712 | tf_op jit(solution)/shard_map/psum | solution.py:323
  (156 other events, 3722.2 us)
Sparse Core Ops, SparseCore 0:
  9.6 102.8 all-gather.6
  114.8 53.2 all-gather.8
  169.8 127.1 all-gather.10
  299.0 101.1 all-gather.12
  650.2 112.3 reduce-scatter.12
  766.6 243.3 reduce-scatter.16
  1089.1 367.9 reduce-scatter.10
  1461.3 464.8 reduce-scatter.14
  1929.8 54.0 reduce-scatter.20
  1987.9 55.7 reduce-scatter.18
  2047.3 101.7 all-reduce.19
where the time goes:
time: 2170 us; the launch traced here: 2160 us
  waiting for transfers between devices  991 us (46%)
  matrix products  565 us (26%)
  other arithmetic  300 us (14%)
  blocking collectives  172 us (8%)
  local copies, waits for them, and re-layouts  72.7 us (3%)
  starting transfers between devices  45.3 us (2%)
    reduce_scatter x1, waiting for transfers between devices, per_device(): lax.psum_scatter(terms[6], ('row', 'ctx'), scatter_dimension=0, tiled=True)  466 us
    reduce_scatter x1, waiting for transfers between devices, per_device(): lax.psum_scatter(terms[1], ('row', 'ctx'), scatter_dimension=0, tiled=True)  311 us
    another operation x7, other arithmetic, householder_span(): lax.linalg.triangular_solve(unit_lower, right_side, left_side=True, lower...  242 us
    unnamed x13, waiting for transfers between devices  104 us
    unnamed x2, blocking collectives  88.7 us
    another operation x21, matrix products, householder_span(): lax.linalg.triangular_solve(unit_lower, right_side, left_side=True, lower...  67.1 us
  transfers between devices with their start and end apart: 24, of which 13 were waited for; matrix products, arithmetic and copies ran while one was open for 40% of the time, Pallas kernels for 0%

commit v1 on v0

v1 whole, which is shorter than its diff:
```python
import functools
import jax
import jax.numpy as jnp
from jax import lax
from jax.experimental import pallas as pl
from jax.experimental.pallas import tpu as pltpu
from jax.sharding import PartitionSpec as P

f32 = jnp.float32
bf16 = jnp.bfloat16
epsilon = 1e-06
negative = -1e30
CH = 128


def mm(a, b, ca=1, cb=0):
    return lax.dot_general(
        a.astype(bf16), b.astype(bf16), (((ca,), (cb,)), ((), ())), preferred_element_type=f32
    )


def halves(a):
    top = a.astype(bf16)
    return top, (a - top.astype(f32)).astype(bf16)


def mm3(a, b):
    ah, al = halves(a)
    bh, bl = halves(b)
    return mm(ah, bh) + (mm(ah, bl) + mm(al, bh))


def tri(strict):
    rows = lax.broadcasted_iota(jnp.int32, (CH, CH), 0)
    cols = lax.broadcasted_iota(jnp.int32, (CH, CH), 1)
    return rows > cols if strict else rows >= cols


def eye():
    rows = lax.broadcasted_iota(jnp.int32, (CH, CH), 0)
    cols = lax.broadcasted_iota(jnp.int32, (CH, CH), 1)
    return jnp.where(rows == cols, 1.0, 0.0).astype(f32)


def unit_inverses(lowers):
    rows = lax.broadcasted_iota(jnp.int32, (CH, CH), 0)
    cols = lax.broadcasted_iota(jnp.int32, (CH, CH), 1)
    done = None
    shift = 0
    while (1 << shift) < CH:
        parent_row = lax.shift_right_logical(rows, shift)
        parent_col = lax.shift_right_logical(cols, shift)
        link = (parent_row - 1 == parent_col) & (jnp.bitwise_and(parent_row, 1) == 1)
        links = [jnp.where(link, low, 0.0) for low in lowers]
        if done is None:
            unit = eye()
            done = [unit - x for x in links]
        else:
            mids = [mm3(t, x) for t, x in zip(done, links)]
            done = [t - mm3(y, t) for t, y in zip(done, mids)]
        shift += 1
    return done


def rate_forms(logits_ref, head, start):
    pick_rows = lax.broadcasted_iota(jnp.int32, (8, CH), 1) == head
    pick_cols = lax.broadcasted_iota(jnp.int32, (CH, CH), 0) == head
    block = logits_ref[pl.ds(start, CH), :]
    row = mm(jnp.where(pick_rows, 1.0, 0.0), block, 1, 1)[0:1]
    col = mm(block, jnp.where(pick_cols, 1.0, 0.0))
    return 2.0 * jax.nn.sigmoid(row), 2.0 * jax.nn.sigmoid(col)


def convolved(u_ref, rim_ref, kernel_ref, ext_ref):
    count = u_ref.shape[0]
    taps = 4
    ext_ref[0:8] = rim_ref[...].astype(f32)
    ext_ref[pl.ds(8, count)] = u_ref[...].astype(f32)
    conv = kernel_ref[0:1] * ext_ref[pl.ds(8, count)]
    for lag in range(1, taps):
        conv = conv + kernel_ref[lag : lag + 1] * ext_ref[pl.ds(8 - lag, count)]
    scale = lax.rsqrt(jnp.sum(conv * conv, -1, keepdims=True) + epsilon)
    return conv, scale


def prep_kernel(unroll, head, q_ref, k_ref, u_ref, rim_ref, kernel_ref, logits_ref,
                w_ref, t_ref, qh_ref, kh_ref, p_ref, s_ref, kt_ref, ext_ref, mv_ref):
    count = q_ref.shape[0]
    chunks = count // CH
    conv, scale = convolved(u_ref, rim_ref, kernel_ref, ext_ref)
    w_ref[...] = (conv * scale).astype(bf16)
    strict, upto = tri(True), tri(False)

    def step(it, carry):
        starts = [pl.multiple_of((it * unroll + j) * CH, CH) for j in range(unroll)]
        ws = [w_ref[pl.ds(s, CH), :] for s in starts]
        rates = [rate_forms(logits_ref, head, s) for s in starts]
        lowers = [jnp.where(strict, mm(w, w, 1, 1), 0.0) * r[0] for w, r in zip(ws, rates)]
        invs = unit_inverses(lowers)
        for s, w, (row, col), t in zip(starts, ws, rates, invs):
            q = q_ref[pl.ds(s, CH), :]
            k = k_ref[pl.ds(s, CH), :]
            both = jnp.concatenate([w, k], axis=0)
            qs = mm(q, both, 1, 1)
            m = jnp.where(upto, qs[:, :CH], 0.0) * row
            kd = jnp.where(strict, mm(w, k, 1, 1), 0.0).astype(bf16)
            n = mm(m, t).astype(bf16)
            z = mm(t, w.astype(f32) * col, 0, 0).astype(bf16)
            s_ref[pl.ds(s, CH), :] = qs[:, CH:] - mm(n, kd)
            qh_ref[pl.ds(s, CH), :] = (q.astype(f32) - mm(n, w)).astype(bf16)
            kh = (k.astype(f32) - mm(kd, z, 0, 0)).astype(bf16)
            kh_ref[pl.ds(s, CH), :] = kh
            p_ref[pl.ds(s, CH), :] = (eye() - mm(z, w, 0, 0)).astype(bf16)
            t_ref[pl.ds(s, CH), :] = t.astype(bf16)
        return carry

    lax.fori_loop(0, chunks // unroll, step, 0)
    mv_ref[...] = kh_ref[...]
    for m in range(1, chunks):
        mv_ref[0 : m * CH] = mm(mv_ref[0 : m * CH], p_ref[m * CH : (m + 1) * CH], 1, 1).astype(bf16)
    kt_ref[...] = mv_ref[...]


def walk_queries(qh_ref, kh_ref, p_ref, s_in_ref, q_ref, s_ref, save_ref):
    count = qh_ref.shape[0]
    chunks = count // CH
    upto = tri(False)
    q_ref[...] = qh_ref[...]
    for c in range(chunks):
        span = slice(c * CH, (c + 1) * CH)
        s_ref[span, span] = jnp.where(upto, s_in_ref[span, :], negative)
        if c + 1 < chunks:
            s_ref[span, (c + 1) * CH :] = jnp.full((CH, count - (c + 1) * CH), negative, f32)
    for m in range(chunks - 2, -1, -1):
        rows = slice((m + 1) * CH, count)
        span = slice(m * CH, (m + 1) * CH)
        cur = q_ref[rows, :]
        if save_ref is not None:
            save_ref[m, rows, :] = cur
        s_ref[rows, span] = mm(cur, kh_ref[span, :], 1, 1)
        q_ref[rows, :] = mm(cur, p_ref[span, :]).astype(bf16)


def strip_weights(scale, far, begin, q_ref, s_ref, kr_ref):
    local = s_ref[pl.ds(begin, CH), :] * scale
    q = q_ref[pl.ds(begin, CH), :]
    remote = mm(q, kr_ref[...], 1, 1) * scale
    cols = lax.broadcasted_iota(jnp.int32, remote.shape, 1)
    remote = jnp.where(cols < far, remote, negative)
    peak = jnp.maximum(jnp.max(local, -1, keepdims=True), jnp.max(remote, -1, keepdims=True))
    e_local = jnp.exp(local - peak)
    e_remote = jnp.exp(remote - peak)
    total = jnp.sum(e_local, -1, keepdims=True) + jnp.sum(e_remote, -1, keepdims=True)
    return e_local, e_remote, total


def attend_kernel(far_ref, qh_ref, kh_ref, p_ref, s_in_ref, v_ref, kr_ref, vr_ref, o_ref, q_ref, s_ref):
    scale = CH ** -0.5
    far = far_ref[0]
    walk_queries(qh_ref, kh_ref, p_ref, s_in_ref, q_ref, s_ref, None)

    def strip(c, carry):
        begin = pl.multiple_of(c * CH, CH)
        e_local, e_remote, total = strip_weights(scale, far, begin, q_ref, s_ref, kr_ref)
        summed = mm(e_local, v_ref[...]) + mm(e_remote, vr_ref[...])
        o_ref[pl.ds(begin, CH), :] = (summed / total).astype(bf16)
        return carry

    lax.fori_loop(0, qh_ref.shape[0] // CH, strip, 0)


def attend_back_kernel(far_ref, qh_ref, kh_ref, p_ref, s_in_ref, v_ref, kr_ref, vr_ref, do_ref,
                       dqh_ref, dkh_ref, dp_ref, ds_ref, dv_ref, dkr_ref, dvr_ref,
                       q_ref, s_ref, save_ref, pl_ref, pr_ref, dsl_ref, dsr_ref, dq_ref):
    scale = CH ** -0.5
    far = far_ref[0]
    count = qh_ref.shape[0]
    chunks = count // CH
    walk_queries(qh_ref, kh_ref, p_ref, s_in_ref, q_ref, s_ref, save_ref)

    def strip(c, carry):
        begin = pl.multiple_of(c * CH, CH)
        e_local, e_remote, total = strip_weights(scale, far, begin, q_ref, s_ref, kr_ref)
        inverse = 1.0 / total
        p_local, p_remote = e_local * inverse, e_remote * inverse
        do = do_ref[pl.ds(begin, CH), :]
        dp_local = mm(do, v_ref[...], 1, 1)
        dp_remote = mm(do, vr_ref[...], 1, 1)
        delta = jnp.sum(p_local * dp_local, -1, keepdims=True) + jnp.sum(
            p_remote * dp_remote, -1, keepdims=True
        )
        d_local = p_local * (dp_local - delta) * scale
        d_remote = (p_remote * (dp_remote - delta) * scale).astype(bf16)
        pl_ref[pl.ds(begin, CH), :] = p_local.astype(bf16)
        pr_ref[pl.ds(begin, CH), :] = p_remote.astype(bf16)
        dsl_ref[pl.ds(begin, CH), :] = d_local.astype(bf16)
        dsr_ref[pl.ds(begin, CH), :] = d_remote
        dq_ref[pl.ds(begin, CH), :] = mm(d_remote, kr_ref[...])
        return carry

    lax.fori_loop(0, chunks, strip, 0)
    do = do_ref[...]
    far_count = kr_ref.shape[0]
    for b in range(0, far_count, count):
        part = slice(b, b + count)
        dvr_ref[part, :] = mm(pr_ref[:, part], do, 0, 0).astype(bf16)
        dkr_ref[part, :] = mm(dsr_ref[:, part], q_ref[...], 0, 0).astype(bf16)
    dv_ref[...] = mm(pl_ref[...], do, 0, 0)
    for m in range(chunks):
        span = slice(m * CH, (m + 1) * CH)
        ds_ref[span, :] = dsl_ref[span, span]
        if m == chunks - 1:
            dkh_ref[span, :] = jnp.zeros((CH, CH), f32)
            dp_ref[span, :] = jnp.zeros((CH, CH), f32)
            continue
        rows = slice((m + 1) * CH, count)
        cur = save_ref[m, rows, :]
        d_new = dq_ref[rows, :].astype(bf16)
        d_s = dsl_ref[rows, span]
        dkh_ref[span, :] = mm(d_s, cur, 0, 0)
        dp_ref[span, :] = mm(cur, d_new, 0, 0)
        dq_ref[rows, :] = mm(d_s, kh_ref[span, :]) + mm(d_new, p_ref[span, :], 1, 1)
    dqh_ref[...] = dq_ref[...]


def prep_back_kernel(unroll, head, q_ref, k_ref, u_ref, rim_ref, kernel_ref, logits_ref,
                     w_ref, t_ref, kh_ref, p_ref, ds_ref, dqh_ref, dkh_ref, dp_ref, dv_ref,
                     dkt_ref, dvt_ref,
                     gq_ref, gk_ref, gv_ref, gu_ref, glog_ref, gker_ref,
                     ext_ref, mv_ref, save_ref, dk_ref, dps_ref, dw_ref, dc_ref):
    count = q_ref.shape[0]
    chunks = count // CH
    strict, upto = tri(True), tri(False)
    mv_ref[...] = kh_ref[...]
    for m in range(1, chunks):
        rows = slice(0, m * CH)
        cur = mv_ref[rows, :]
        save_ref[m, rows, :] = cur
        if m < chunks - 1:
            mv_ref[rows, :] = mm(cur, p_ref[m * CH : (m + 1) * CH, :], 1, 1).astype(bf16)
    dk_ref[...] = dkt_ref[...].astype(f32)
    dps_ref[...] = dp_ref[...]
    for m in range(chunks - 1, 0, -1):
        rows = slice(0, m * CH)
        span = slice(m * CH, (m + 1) * CH)
        d_new = dk_ref[rows, :].astype(bf16)
        dps_ref[span, :] = dps_ref[span, :] + mm(d_new, save_ref[m, rows, :], 0, 0)
        dk_ref[rows, :] = mm(d_new, p_ref[span, :])
    dk_ref[...] = dk_ref[...] + dkh_ref[...]
    gv_ref[...] = (dv_ref[...] + dvt_ref[...].astype(f32)).astype(bf16)
    ones = jnp.ones((8, CH), f32)

    def chunk(start):
        span = pl.ds(start, CH)
        row, col = rate_forms(logits_ref, head, start)
        q, k, w, t = q_ref[span, :], k_ref[span, :], w_ref[span, :], t_ref[span, :]
        w32 = w.astype(f32)
        ds, dqh, dkh = ds_ref[span, :], dqh_ref[span, :], dk_ref[span, :]
        dqh16, dkh16, dp = dqh.astype(bf16), dkh.astype(bf16), dps_ref[span, :].astype(bf16)
        ww = jnp.where(strict, mm(w, w, 1, 1), 0.0)
        qw = jnp.where(upto, mm(q, w, 1, 1), 0.0)
        kd = jnp.where(strict, mm(w, k, 1, 1), 0.0).astype(bf16)
        n = mm(qw * row, t).astype(bf16)
        z = mm(t, w32 * col, 0, 0).astype(bf16)
        dn = -(mm(ds, kd, 1, 1) + mm(dqh16, w, 1, 1))
        dkd = -(mm(n, ds, 0, 0) + mm(z, dkh16, 1, 1))
        dz = -(mm(kd, dkh16) + mm(w, dp, 1, 1))
        dw = -(mm(n, dqh16, 0, 0) + mm(z, dp))
        dn16, dz16 = dn.astype(bf16), dz.astype(bf16)
        dbw = mm(t, dz16)
        x = mm(n, dn16, 0, 0) + mm(z, dz16, 1, 1)
        da = jnp.where(strict, -mm(x, t, 1, 1), 0.0)
        dm = jnp.where(upto, mm(dn16, t, 1, 1), 0.0)
        dqw = (dm * row).astype(bf16)
        dww = da * row
        dwk = jnp.where(strict, dkd, 0.0).astype(bf16)
        d_rate = jnp.sum(dm * qw + da * ww, 0, keepdims=True)
        high, low = halves(dbw * w32)
        d_rate = d_rate + (mm(ones, high, 1, 1) + mm(ones, low, 1, 1))[0:1]
        gq_ref[span, :] = (mm(ds, k) + mm(dqw, w) + dqh).astype(bf16)
        gk_ref[span, :] = (mm(ds, q, 0, 0) + mm(dwk, w, 0, 0) + dkh).astype(bf16)
        dw = dw + mm(dqw, q, 0, 0) + mm(dwk, k)
        dw = dw + mm(dww, w) + mm(dww, w, 0, 0) + col * dbw
        dw_ref[span, :] = dw
        return d_rate * row * (1.0 - 0.5 * row)

    def step(it, carry):
        for j in range(unroll):
            index = it * unroll + j
            glog_ref[pl.ds(index, 1), :] = chunk(pl.multiple_of(index * CH, CH))
        return carry

    lax.fori_loop(0, chunks // unroll, step, 0)
    conv, scale = convolved(u_ref, rim_ref, kernel_ref, ext_ref)
    unit = conv * scale
    dw = dw_ref[...]
    d_conv = scale * (dw - unit * jnp.sum(unit * dw, -1, keepdims=True))
    dc_ref[0:8] = jnp.zeros((8, CH), f32)
    dc_ref[pl.ds(8, count)] = d_conv
    dc_ref[pl.ds(8 + count, 8)] = jnp.zeros((8, CH), f32)
    total = kernel_ref[0:1] * dc_ref[pl.ds(0, count + 8)]
    gker_ref[...] = jnp.zeros(gker_ref.shape, f32)
    gker_ref[0:1] = jnp.sum(d_conv * ext_ref[pl.ds(8, count)], 0, keepdims=True)
    for lag in range(1, 4):
        total = total + kernel_ref[lag : lag + 1] * dc_ref[pl.ds(lag, count + 8)]
        gker_ref[lag : lag + 1] = jnp.sum(d_conv * ext_ref[pl.ds(8 - lag, count)], 0, keepdims=True)
    gu_ref[...] = total


def params():
    return pltpu.CompilerParams(vmem_limit_bytes=56 * 1024 * 1024)


def whole(shape):
    return pl.BlockSpec(shape, lambda *_: (0,) * len(shape))


def column(rows, index):
    return pl.BlockSpec((rows, CH), lambda *_: (0, index))


def estimate(flops, size):
    return pl.CostEstimate(flops=flops, bytes_accessed=size, transcendentals=0)


def prep(projected, rim, kernel, logits, head, heads):
    count = projected.shape[0]
    sq = jax.ShapeDtypeStruct((count, CH), bf16)
    unroll = 4
    return pl.pallas_call(
        functools.partial(prep_kernel, unroll, head),
        grid=(1,),
        in_specs=[column(count, head), column(count, heads + head), column(count, 3 * heads + head),
                  column(8, head), column(8, head), whole((count, CH))],
        out_specs=[whole((count, CH))] * 7,
        out_shape=[sq, sq, sq, sq, sq, jax.ShapeDtypeStruct((count, CH), f32), sq],
        scratch_shapes=[pltpu.VMEM((count + 8, CH), f32), pltpu.VMEM((count, CH), bf16)],
        compiler_params=params(), name="prep",
        cost_estimate=estimate(count * 10**7, count * 4096),
    )(projected, projected, projected, rim, kernel, logits)


def attend(far, qh, kh, p, s_in, projected, kr, vr, head, heads):
    count = qh.shape[0]
    fc = kr.shape[0]
    c = whole((count, CH))
    return pl.pallas_call(
        attend_kernel,
        grid=(1,),
        in_specs=[pl.BlockSpec(memory_space=pltpu.SMEM), c, c, c, c, column(count, 2 * heads + head),
                  whole((fc, CH)), whole((fc, CH))],
        out_specs=c,
        out_shape=jax.ShapeDtypeStruct((count, CH), bf16),
        scratch_shapes=[pltpu.VMEM((count, CH), bf16), pltpu.VMEM((count, count), f32)],
        compiler_params=params(), name="attend",
        cost_estimate=estimate(count * 10**7, count * 4096),
    )(far, qh, kh, p, s_in, projected, kr, vr)


def attend_back(far, qh, kh, p, s_in, projected, kr, vr, d_attn, head, heads):
    count = qh.shape[0]
    fc = kr.shape[0]
    c = whole((count, CH))
    r = whole((fc, CH))
    w32 = jax.ShapeDtypeStruct((count, CH), f32)
    far16 = jax.ShapeDtypeStruct((fc, CH), bf16)
    return pl.pallas_call(
        attend_back_kernel,
        grid=(1,),
        in_specs=[pl.BlockSpec(memory_space=pltpu.SMEM), c, c, c, c, column(count, 2 * heads + head),
                  r, r, column(count, head)],
        out_specs=[c, c, c, c, c, r, r],
        out_shape=[w32, w32, w32, jax.ShapeDtypeStruct((count, CH), bf16), w32, far16, far16],
        scratch_shapes=[pltpu.VMEM((count, CH), bf16), pltpu.VMEM((count, count), f32),
                        pltpu.VMEM((count // CH - 1, count, CH), bf16),
                        pltpu.VMEM((count, count), bf16), pltpu.VMEM((count, fc), bf16),
                        pltpu.VMEM((count, count), bf16), pltpu.VMEM((count, fc), bf16),
                        pltpu.VMEM((count, CH), f32)],
        compiler_params=params(), name="attend_back",
        cost_estimate=estimate(count * 3 * 10**7, count * 8192),
    )(far, qh, kh, p, s_in, projected, kr, vr, d_attn)


def prep_back(projected, rim, kernel, logits, w, t, kh, p, ds, dqh, dkh, dp, dv, dkt, dvt, head, heads):
    count = projected.shape[0]
    c = whole((count, CH))
    sq = jax.ShapeDtypeStruct((count, CH), bf16)
    chunks = count // CH
    unroll = 2
    return pl.pallas_call(
        functools.partial(prep_back_kernel, unroll, head),
        grid=(1,),
        in_specs=[column(count, head), column(count, heads + head), column(count, 3 * heads + head),
                  column(8, head), column(8, head), c] + [c] * 11,
        out_specs=[c, c, c, whole((count + 8, CH)), whole((chunks, CH)), whole((8, CH))],
        out_shape=[sq, sq, sq, jax.ShapeDtypeStruct((count + 8, CH), f32),
                   jax.ShapeDtypeStruct((chunks, CH), f32), jax.ShapeDtypeStruct((8, CH), f32)],
        scratch_shapes=[pltpu.VMEM((count + 8, CH), f32), pltpu.VMEM((count, CH), bf16),
                        pltpu.VMEM((chunks, count, CH), bf16), pltpu.VMEM((count, CH), f32),
                        pltpu.VMEM((count, CH), f32), pltpu.VMEM((count, CH), f32),
                        pltpu.VMEM((count + 16, CH), f32)],
        compiler_params=params(), name="prep_back",
        cost_estimate=estimate(count * 3 * 10**7, count * 8192),
    )(projected, projected, projected, rim, kernel, logits, w, t, kh, p, ds, dqh, dkh, dp, dv, dkt, dvt)


def swapped(value, axis):
    return lax.ppermute(value, axis, [(0, 1), (1, 0)])


def passed_along(value, axis, steps):
    count = lax.axis_size(axis)
    leading, last = (max(0, -steps), min(count, count - steps))
    return lax.ppermute(value, axis, [(source, source + steps) for source in range(leading, last)])


def in_order(mine, theirs, index, dim=0):
    first = index == 0
    return jnp.concatenate(
        [jnp.where(first, mine, theirs), jnp.where(first, theirs, mine)], axis=dim
    )


def gather_group(value):
    pair = in_order(value, swapped(value, "seq"), lax.axis_index("seq"))
    return in_order(pair, swapped(pair, "cc"), lax.axis_index("cc"))


def reduce_group(partial):
    half = partial.shape[0] // 2
    cc, seq = lax.axis_index("cc"), lax.axis_index("seq")
    mine = lax.dynamic_slice_in_dim(partial, cc * half, half, 0)
    theirs = lax.dynamic_slice_in_dim(partial, (1 - cc) * half, half, 0).astype(bf16)
    mine = mine + swapped(theirs, "cc").astype(f32)
    quarter = half // 2
    own = lax.dynamic_slice_in_dim(mine, seq * quarter, quarter, 0)
    other = lax.dynamic_slice_in_dim(mine, (1 - seq) * quarter, quarter, 0).astype(bf16)
    return own + swapped(other, "seq").astype(f32)


def rms_norm(values, gain):
    return values * lax.rsqrt(jnp.mean(values * values, -1, keepdims=True) + epsilon) * gain


def move_keys(keys, transforms):
    blocks = transforms.reshape(-1, CH, CH)
    for m in range(blocks.shape[0]):
        keys = lax.dot_general(keys, blocks[m], (((1,), (1,)), ((), ())), preferred_element_type=f32)
    return keys


def column_share(shard, parts, group, axis):
    cc, seq = lax.axis_index("cc"), lax.axis_index("seq")
    pair = lax.axis_size("seq")
    mine = lax.dynamic_index_in_dim(shard, cc * pair + seq, axis, keepdims=False)
    theirs = lax.dynamic_index_in_dim(shard, (1 - cc) * pair + seq, axis, keepdims=False)
    return mine, theirs


def share_rows(mine, theirs):
    return in_order(mine, swapped(theirs, "cc"), lax.axis_index("cc"))


def finish(reduced):
    cc, seq = lax.axis_index("cc"), lax.axis_index("seq")
    rows = reduced.shape[0] // 2
    mine = lax.dynamic_slice_in_dim(reduced, cc * rows, rows, 0)
    theirs = swapped(lax.dynamic_slice_in_dim(reduced, (1 - cc) * rows, rows, 0), "cc")
    first = cc == 0
    pair = jnp.stack([jnp.where(first, mine, theirs), jnp.where(first, theirs, mine)])
    other = swapped(pair, "seq")
    first = seq == 0
    return [
        (jnp.where(first, pair[i], other[i]) if j == 0 else jnp.where(first, other[i], pair[i])).astype(f32)
        for i in range(2)
        for j in range(2)
    ]


def per_device(
    layer_input, norm_gain1, qkvu_weight, beta_weight, conv_kernel, out_weight,
    norm_gain2, gate_up_weight, down_weight, seq_len, out_grad,
):
    cy_size = lax.axis_size("cy")
    cy, cc, seq = lax.axis_index("cy"), lax.axis_index("cc"), lax.axis_index("seq")
    group = 2 * lax.axis_size("seq")
    member = cc * lax.axis_size("seq") + seq
    own16 = layer_input[0]
    tok_count, width = own16.shape
    heads = beta_weight.shape[1]
    local = heads // group
    features = local * CH
    taps = conv_kernel.shape[0]
    rows = qkvu_weight.shape[0]
    ff_rows = down_weight.shape[0]
    ff_part = ff_rows // group
    span = group * tok_count
    length = seq_len[0]
    first_slot = cy * span
    valid_span = (first_slot + jnp.arange(span) < length)[:, None]
    valid = (first_slot + member * tok_count + jnp.arange(tok_count) < length)[:, None]
    all_axes = ("row", "cy")

    small = jnp.concatenate(
        [norm_gain1[:, None], norm_gain2[:, None], conv_kernel.T, beta_weight], axis=1
    )
    small = jnp.pad(small, ((0, 0), (0, CH - small.shape[1])))
    mine, theirs = column_share(qkvu_weight.reshape(rows, 4, group, features), 4, group, 2)
    mine = jnp.concatenate([mine.reshape(rows, 4 * features), small], axis=1)
    theirs = jnp.concatenate([theirs.reshape(rows, 4 * features), small], axis=1)
    wide = lax.all_gather(share_rows(mine, theirs), all_axes, axis=0, tiled=True)
    wide_qkvu = wide[:, : 4 * features]
    packed = wide[:, 4 * features :]
    wide_out = lax.all_gather(out_weight, ("row", "cy", "cc"), axis=0, tiled=True)
    shards = width // rows
    mine, theirs = column_share(gate_up_weight.reshape(rows, 2, shards, group, ff_part), 2, group, 3)
    gate_up_pair = share_rows(mine.reshape(rows, -1), theirs.reshape(rows, -1))
    mine, theirs = column_share(down_weight.reshape(group, ff_part, width), 1, group, 0)
    down_pair = share_rows(mine, theirs)
    wide_gate_up = lax.all_gather(gate_up_pair, all_axes, axis=0, tiled=True)
    wide_down = lax.all_gather(down_pair, all_axes, axis=0, tiled=True)

    gain_one = packed[:, 0].astype(f32)
    gain_two = packed[:, 1].astype(f32)
    kernel = lax.dynamic_slice_in_dim(packed[:, 2 : 2 + taps], member * features, features, 0)
    kernel = jnp.pad(kernel.T.astype(f32), ((0, 8 - taps), (0, 0)))
    beta_local = lax.dynamic_slice_in_dim(packed[:, 2 + taps : 2 + taps + heads], member * local, local, 1)
    beta_pad = jnp.pad(beta_local, ((0, 0), (0, CH - local)))

    span_input = gather_group(own16)
    span_grad = jnp.where(valid_span, gather_group(out_grad[0]), 0)
    h_first = rms_norm(span_input.astype(f32), gain_one).astype(bf16)
    projected = jnp.dot(h_first, wide_qkvu, preferred_element_type=f32).astype(bf16)
    logits = jnp.dot(h_first, beta_pad, preferred_element_type=f32).astype(bf16)
    rim = passed_along(projected[span - 8 :, 3 * features :], "cy", 1)
    far = jnp.reshape(cy * span, (1,)).astype(jnp.int32)

    prepared, kept = [], []
    for head in range(local):
        prepared.append(prep(projected, rim, kernel, logits, head, local))
    for head in range(local):
        transforms = prepared[head][4]
        keys = prepared[head][6]
        values = projected[:, (2 * local + head) * CH : (2 * local + head + 1) * CH]
        hops = []
        for hop in range(1, cy_size):
            keys = passed_along(keys, "cy", 1)
            values = passed_along(values, "cy", 1)
            hops.append((keys, values))
            if hop < cy_size - 1:
                keys = move_keys(keys.astype(f32), transforms.astype(f32)).astype(bf16)
        kept.append(hops)
    far_keys = [jnp.concatenate([k for k, _ in hops], 0) for hops in kept]
    far_values = [jnp.concatenate([v for _, v in hops], 0) for hops in kept]
    attn = []
    for head in range(local):
        _, _, qh, kh, p, s_in, _ = prepared[head]
        attn.append(
            attend(far, qh, kh, p, s_in, projected, far_keys[head], far_values[head], head, local)
        )
    attn = jnp.concatenate(attn, axis=1)
    back = lax.all_to_all(attn, ("cc", "seq"), split_axis=0, concat_axis=1, tiled=True)
    tokens = own16.astype(f32)
    x_mid = tokens + jnp.dot(back, wide_out, preferred_element_type=f32)
    h_second = gather_group(rms_norm(x_mid, gain_two).astype(bf16))
    gate_up = jnp.dot(h_second, wide_gate_up, preferred_element_type=f32)
    hidden_count = wide_down.shape[0]
    gate_part, up_part = gate_up[:, :hidden_count], gate_up[:, hidden_count:]
    sigmoid_gate = jax.nn.sigmoid(gate_part)
    silu_gate = gate_part * sigmoid_gate
    hidden = (silu_gate * up_part).astype(bf16)
    branch = reduce_group(jnp.dot(hidden, wide_down, preferred_element_type=f32))
    layer_output = jnp.where(valid, x_mid + branch, 0.0).astype(bf16)[None]

    d_hidden = jnp.einsum("td,fd->tf", span_grad, wide_down, preferred_element_type=f32)
    d_gate = d_hidden * up_part * sigmoid_gate * (1.0 + gate_part * (1.0 - sigmoid_gate))
    d_up = d_hidden * silu_gate
    d_gate_up = jnp.concatenate([d_gate, d_up], axis=1).astype(bf16)
    d_h_second = reduce_group(
        jnp.einsum("tf,df->td", d_gate_up, wide_gate_up, preferred_element_type=f32)
    )
    down_term = jnp.einsum("tf,td->fd", hidden, span_grad, preferred_element_type=f32)
    gate_up_term = jnp.einsum("td,tf->df", h_second, d_gate_up, preferred_element_type=f32)
    down_sum = lax.psum_scatter(down_term.astype(bf16), all_axes, scatter_dimension=0, tiled=True)
    gate_up_sum = lax.psum_scatter(gate_up_term.astype(bf16), all_axes, scatter_dimension=0, tiled=True)
    grad_rows = jnp.where(valid, out_grad[0].astype(f32), 0.0)
    _, pull_second = jax.vjp(rms_norm, x_mid, gain_two)
    mid_norm_grad, gain_two_term = pull_second(d_h_second)
    d_mid = grad_rows + mid_norm_grad
    d_branch = d_mid.astype(bf16)
    out_term = jnp.einsum("td,te->de", back, d_branch, preferred_element_type=f32)
    out_sum = lax.psum_scatter(
        out_term.astype(bf16), ("row", "cy", "cc"), scatter_dimension=0, tiled=True
    )
    d_back = jnp.einsum("te,de->td", d_branch, wide_out, preferred_element_type=f32).astype(bf16)
    d_attn = lax.all_to_all(d_back, ("cc", "seq"), split_axis=1, concat_axis=0, tiled=True)

    backs = []
    for head in range(local):
        _, _, qh, kh, p, s_in, _ = prepared[head]
        backs.append(
            attend_back(
                far, qh, kh, p, s_in, projected, far_keys[head], far_values[head], d_attn, head, local
            )
        )
    pieces, logit_rows, kernel_rows, rims = [], [], [], []
    for head in range(local):
        w, t, _, kh, p, _, _ = prepared[head]
        dqh, dkh, dp, ds, dv, dkr, dvr = backs[head]
        outgoing = None
        for hop in reversed(range(1, cy_size)):
            part = slice((hop - 1) * span, hop * span)
            d_keys, d_values = dkr[part], dvr[part]
            if outgoing is not None:
                incoming = [passed_along(value, "cy", -1) for value in outgoing]
                received = kept[head][hop - 1][0].astype(f32)
                _, pull = jax.vjp(move_keys, received, p.astype(f32))
                extra, d_transform = pull(incoming[0].astype(f32))
                d_keys = (d_keys.astype(f32) + extra).astype(bf16)
                d_values = (d_values.astype(f32) + incoming[1].astype(f32)).astype(bf16)
                dp = dp + d_transform
            outgoing = (d_keys, d_values)
        dkt, dvt = [passed_along(value, "cy", -1) for value in outgoing]
        gq, gk, gv, gu, glog, gker = prep_back(
            projected, rim, kernel, logits, w, t, kh, p, ds, dqh, dkh, dp, dv, dkt, dvt, head, local
        )
        pieces.append((gq, gk, gv, gu))
        logit_rows.append(glog.reshape(1, span))
        kernel_rows.append(gker[:taps])
    d_rim = jnp.concatenate([piece[3][:8] for piece in pieces], axis=1)
    rim_back = passed_along(d_rim, "cy", -1)
    d_raw = jnp.concatenate([piece[3][8:] for piece in pieces], axis=1)
    d_raw = jnp.concatenate([d_raw[: span - 8], d_raw[span - 8 :] + rim_back], axis=0).astype(bf16)
    d_projected = jnp.concatenate(
        [piece[0] for piece in pieces] + [piece[1] for piece in pieces] + [piece[2] for piece in pieces] + [d_raw],
        axis=1,
    )
    d_logits = jnp.concatenate(logit_rows, axis=0).astype(bf16)
    qkvu_term = jnp.einsum("td,tn->dn", h_first, d_projected, preferred_element_type=f32)
    beta_term = jnp.einsum("td,ht->dh", h_first, d_logits, preferred_element_type=f32)
    d_h_first = jnp.einsum("tn,dn->td", d_projected, wide_qkvu, preferred_element_type=f32)
    d_h_first = d_h_first + jnp.einsum("ht,dh->td", d_logits, beta_local, preferred_element_type=f32)
    d_h_first = reduce_group(d_h_first)
    _, pull_first = jax.vjp(rms_norm, tokens, gain_one)
    input_norm_grad, gain_one_term = pull_first(d_h_first)
    input_grad = (d_mid + input_norm_grad).astype(bf16)[None]

    kernel_term = lax.dynamic_update_slice_in_dim(
        jnp.zeros((width, taps), f32), jnp.concatenate(kernel_rows, axis=1).T, member * features, 0
    )
    beta_wide = lax.dynamic_update_slice_in_dim(
        jnp.zeros((width, heads), f32), beta_term, member * local, 1
    )
    small_term = jnp.concatenate(
        [gain_one_term[:, None], gain_two_term[:, None], kernel_term, beta_wide], axis=1
    )
    used = small_term.shape[1]
    small_term = jnp.pad(small_term, ((0, 0), (0, CH - used)))
    qkvu_sum = lax.psum_scatter(
        jnp.concatenate([qkvu_term, small_term], axis=1).astype(bf16),
        all_axes, scatter_dimension=0, tiled=True,
    )
    parts = finish(qkvu_sum)
    qkvu_grad = jnp.stack([part[:, : 4 * features].reshape(rows, 4, features) for part in parts], axis=2)
    qkvu_grad = qkvu_grad.reshape(rows, 4 * width)
    small_grad = sum(part[:, 4 * features :] for part in parts)
    gate_up_grad = jnp.stack(
        [part.reshape(rows, 2, shards, ff_part) for part in finish(gate_up_sum)], axis=3
    ).reshape(rows, -1)
    down_grad = jnp.concatenate(finish(down_sum), axis=0)
    out_grad_own = out_sum.astype(f32) + swapped(out_sum, "seq").astype(f32)
    return (
        layer_output,
        input_grad,
        small_grad[:, 0],
        qkvu_grad,
        small_grad[:, 2 + taps : 2 + taps + heads],
        small_grad[:, 2 : 2 + taps].T,
        out_grad_own,
        small_grad[:, 1],
        gate_up_grad,
        down_grad,
    )


def solution(mesh):
    row, ctx, seq = (mesh.shape[name] for name in ("row", "ctx", "seq"))
    fine = jax.sharding.Mesh(mesh.devices.reshape(row, ctx // 2, 2, seq), ("row", "cy", "cc", "seq"))
    own = ("row", "cy", "cc")
    token = P("row", ("cy", "cc", "seq"), None)
    return jax.shard_map(
        per_device,
        mesh=fine,
        in_specs=(
            token, P(own), P(own, None), P(own, None), P(None, own), P(own, None),
            P(own), P(own, None), P(own, None), P("row"), token,
        ),
        out_specs=(
            token, token, P(own), P(own, None), P(own, None), P(None, own), P(own, None),
            P(own), P(own, None), P(own, None),
        ),
        check_vma=False,
    )
```

time: 2170 us -> 784 us (0.36)
  waiting for transfers between devices: 991 us -> 346 us
  matrix products: 565 us -> 80.5 us
  other arithmetic: 300 us -> 56.1 us
  blocking collectives: 172 us -> 0 us
  Pallas kernels: 0 us -> 146 us
    reduce_scatter x4, waiting for transfers between devices: 777 us -> 118 us  [the longest x1 104 us: per_device(): lax.psum_scatter(jnp.concatenate([qkvu_term, small_term], axis=1).astype(...]
    dot_general x66 -> x15, matrix products: 496 us -> 80.5 us  [the longest x1 11.7 us: per_device(): gate_up = jnp.dot(h_second, wide_gate_up, preferred_element_type=f32)]
    another operation x16 -> x5, other arithmetic: 246 us -> 2.3 us  [the longest x3 1.76 us: finish(): jnp.stack([jnp.where(first, mine, theirs), jnp.where(first, theirs, mine)])]
    pallas_call x0 -> x12, Pallas kernels: none -> 146 us  [the longest x3 44.3 us: prep_back(): pl.pallas_call(functools.partial(prep_back_kernel, unroll, head), grid=(1...]
    unnamed x13 -> x8, waiting for transfers between devices: 104 us -> 0.81 us
    ppermute x0 -> x22, waiting for transfers between devices: none -> 99.2 us  [swapped(): return lax.ppermute(value, axis, [(0, 1), (1, 0)])]
    unnamed x2 -> x0, blocking collectives: 88.7 us -> none
    all_gather x4, waiting for transfers between devices: 38.7 us -> 114 us  [the longest x1 48.8 us: per_device(): lax.all_gather(share_rows(mine, theirs), all_axes, axis=0, tiled=True)]
  transfers between devices with their start and end apart: 24 -> 46, of which waited for: 13 -> 20; matrix products, arithmetic and copies ran while one was open for 40% -> 21% of each run, Pallas kernels for 0% -> 19%
where the time goes in v1:
time: 784 us; the launch traced here: 773 us
  waiting for transfers between devices  346 us (44%)
  Pallas kernels  146 us (19%)
  matrix products  80.5 us (10%)
  local copies, waits for them, and re-layouts  73.7 us (9%)
  other arithmetic  56.1 us (7%)
  starting transfers between devices  53.4 us (7%)
  between operations  16.8 us (2%)
    reduce_scatter x1, waiting for transfers between devices, per_device(): lax.psum_scatter(jnp.concatenate([qkvu_term, small_term], axis=1).astype(...  104 us
    ppermute x22, waiting for transfers between devices, swapped(): return lax.ppermute(value, axis, [(0, 1), (1, 0)])  99.2 us
    all_gather x1, waiting for transfers between devices, per_device(): lax.all_gather(share_rows(mine, theirs), all_axes, axis=0, tiled=True)  48.8 us
    all_gather x1, waiting for transfers between devices, per_device(): wide_down = lax.all_gather(down_pair, all_axes, axis=0, tiled=True)  48.7 us
    pallas_call x3, Pallas kernels, prep_back(): pl.pallas_call(functools.partial(prep_back_kernel, unroll, head), grid=(1...  44.3 us
    pallas_call x3, Pallas kernels, attend_back(): pl.pallas_call(attend_back_kernel, grid=(1,), in_specs=[pl.BlockSpec(memo...  43.6 us
    unnamed x166, local copies, waits for them, and re-layouts  34.9 us
    pallas_call x3, Pallas kernels, prep(): pl.pallas_call(functools.partial(prep_kernel, unroll, head), grid=(1,), i...  32.5 us
  transfers between devices with their start and end apart: 46, of which 20 were waited for; matrix products, arithmetic and copies ran while one was open for 21% of the time, Pallas kernels for 19%

profile of v1, /device:TPU:1, one launch (start us, length us, event | category | flops | bytes accessed | tf_op | source)
XLA Modules:
  0.0 772.9 jit_solution(6225369358950990233)
XLA Ops:
  19.1 17.7 %collective-permute-done = bf16[256,1536]{1,0:T(8,128)(2,1)S(1)} collective-permute-done((bf16[256,1536]{1,0:T(8,128)(2,1)S(1)}, bf16[256,1536]{1,0:T(8,128)(2,1)S(1)}, u32[]{:S(2)}, u32[]{:S(2)}) %collective-permute-start) | collective-permute-done | bytes 786464 | tf_op jit(solution)/shard_map/ppermute | solution.py:408
  52.1 48.8 %all-gather.5.cloned.1.call-done = bf16[1536,1664]{1,0:T(8,128)(2,1)} async-done(((bf16[192,1664]{1,0:T(8,128)(2,1)}), bf16[1536,1664]{1,0:T(8,128)(2,1)}) %all-gather.5.cloned.1.call-update) | async-done | bytes 5111824 | tf_op jit(solution)/shard_map/all_gather | solution.py:511
  123.5 10.8 %prep.3 = (bf16[1024,128]{1,0:T(8,128)(2,1)}, bf16[1024,128]{1,0:T(8,128)(2,1)}, bf16[1024,128]{1,0:T(8,128)(2,1)}, bf16[1024,128]{1,0:T(8,128)(2,1)}, bf16[1024...) custom-call(bf16[1024,1536]{1,0:T(8,128)(2,1)} %copy-done.41, bf16[1024,1536]{1,0:T(8,128)(2,1)} %copy-done.41, ...), custom_call_target="tpu_custom_call" | custom-call | flops 10240000000 | bytes 4194304 | tf_op jit(solution)/shard_map/prep/pallas_call | solution.py:330
  135.6 10.8 %prep.4 = (bf16[1024,128]{1,0:T(8,128)(2,1)}, bf16[1024,128]{1,0:T(8,128)(2,1)}, bf16[1024,128]{1,0:T(8,128)(2,1)}, bf16[1024,128]{1,0:T(8,128)(2,1)}, bf16[1024...) custom-call(bf16[1024,1536]{1,0:T(8,128)(2,1)} %copy-done.41, bf16[1024,1536]{1,0:T(8,128)(2,1)} %copy-done.41, ...), custom_call_target="tpu_custom_call" | custom-call | flops 10240000000 | bytes 4194304 | tf_op jit(solution)/shard_map/prep/pallas_call | solution.py:330
  147.7 10.8 %prep.5 = (bf16[1024,128]{1,0:T(8,128)(2,1)}, bf16[1024,128]{1,0:T(8,128)(2,1)}, bf16[1024,128]{1,0:T(8,128)(2,1)}, bf16[1024,128]{1,0:T(8,128)(2,1)}, bf16[1024...) custom-call(bf16[1024,1536]{1,0:T(8,128)(2,1)} %copy-done.41, bf16[1024,1536]{1,0:T(8,128)(2,1)} %copy-done.41, ...), custom_call_target="tpu_custom_call" | custom-call | flops 10240000000 | bytes 4194304 | tf_op jit(solution)/shard_map/prep/pallas_call | solution.py:330
  215.3 8.8 %collective-permute-done.16 = bf16[256,1536]{1,0:T(8,128)(2,1)} collective-permute-done((bf16[256,1536]{1,0:T(8,128)(2,1)}, bf16[256,1536]{1,0:T(8,128)(2,1)}, u32[]{:S(2)}, u32[]{:S(2)}) %collective-permute-start.16) | collective-permute-done | bytes 786464 | tf_op jit(solution)/shard_map/ppermute | solution.py:408
  224.1 16.9 %collective-permute-done.10 = bf16[256,1536]{1,0:T(8,128)(2,1)S(1)} collective-permute-done((bf16[256,1536]{1,0:T(8,128)(2,1)}, bf16[256,1536]{1,0:T(8,128)(2,1)S(1)}, u32[]{:S(2)}, u32[]{:S(2)}) %collective-permute-start.10) | collective-permute-done | bytes 786464 | tf_op jit(solution)/shard_map/ppermute | solution.py:408
  251.3 16.4 %all-gather.9.cloned.1.call-done = bf16[1536,2048]{1,0:T(8,128)(2,1)} async-done(((bf16[192,2048]{1,0:T(8,128)(2,1)}), bf16[1536,2048]{1,0:T(8,128)(2,1)}) %all-gather.9.cloned.1.call-update) | async-done | bytes 6291472 | tf_op jit(solution)/shard_map/all_gather | solution.py:520
  267.6 11.7 %fusion.11 = f32[1024,2048]{1,0:T(8,128)} fusion(bf16[1536,2048]{1,0:T(8,128)(2,1)} %all-gather.9.cloned.1.call-done, bf16[512,1536]{1,0:T(8,128)(2,1)} %get-tuple-element.186, bf16[512,1536]{1,0:T(8,128)(2,1)} %get-tuple-element.185), kind=kOutput, calls=%fused_computation.41 | convolution fusion | flops 6448742400 | bytes 17825792 | tf_op jit(solution)/shard_map/dot_general | solution.py:566
  279.4 48.7 %all-gather.11.cloned.1.call-done = bf16[1024,1536]{1,0:T(8,128)(2,1)} async-done(((bf16[128,1536]{1,0:T(8,128)(2,1)}), bf16[1024,1536]{1,0:T(8,128)(2,1)}) %all-gather.11.cloned.1.call-update) | async-done | bytes 3145744 | tf_op jit(solution)/shard_map/all_gather | solution.py:521
  328.1 10.5 %multiply_convert_fusion.1 = (bf16[1024,1024]{1,0:T(8,128)(2,1)}, bf16[1024,1024]{1,0:T(8,128)(2,1)}, bf16[1024,1024]{1,0:T(8,128)(2,1)S(1)}) fusion(f32[1024,2048]{1,0:T(8,128)} %fusion.11, bf16[1024,1536]{1,0:T(8,128)(2,1)} %all-gather.11.cloned.1.call-done, bf16[512,1536]{1,0:T(8,128)(2,1)} %get-tuple-element.184, ...), kind=kOutput, calls=%fused_computation.12 | convolution fusion | flops 3244818432 | bytes 20972544 | tf_op jit(solution)/shard_map/td,fd->tf/dot_general | solution.py:575
  345.3 11.4 %convolution_convert_fusion.1 = bf16[1536,2048]{1,0:T(8,128)(2,1)} fusion(bf16[1024,1024]{1,0:T(8,128)(2,1)} %get-tuple-element.181, bf16[1024,1024]{1,0:T(8,128)(2,1)} %get-tuple-element.180, bf16[512,1536]{1,0:T(8,128)(2,1)} %get-tuple-element.186, bf16[512,1536]{1,0:T(8,128)(2,1)} %get-tuple-element.185), kind=kOutput, calls=%fused_computation.3 | convolution fusion | flops 6460276736 | bytes 13631488 | tf_op jit(solution)/shard_map/td,tf->df/dot_general | solution.py:583
  356.7 10.6 %fusion.10 = f32[1024,1536]{1,0:T(8,128)S(1)} fusion(bf16[1536,2048]{1,0:T(8,128)(2,1)} %all-gather.9.cloned.1.call-done, bf16[1024,1024]{1,0:T(8,128)(2,1)} %get-tuple-element.181, bf16[1024,1024]{1,0:T(8,128)(2,1)} %get-tuple-element.180), kind=kOutput, calls=%fused_computation.35 | convolution fusion | flops 6450839552 | bytes 16777216 | tf_op jit(solution)/shard_map/tf,df->td/dot_general | solution.py:580
  391.4 13.1 %collective-permute-done.19 = bf16[256,1536]{1,0:T(8,128)(2,1)S(1)} collective-permute-done((bf16[256,1536]{1,0:T(8,128)(2,1)}, bf16[256,1536]{1,0:T(8,128)(2,1)S(1)}, u32[]{:S(2)}, u32[]{:S(2)}) %collective-permute-start.19) | collective-permute-done | bytes 786464 | tf_op jit(solution)/shard_map/ppermute | solution.py:408
  407.0 14.5 %collective-permute-done.15 = bf16[256,1536]{1,0:T(8,128)(2,1)} collective-permute-done((bf16[256,1536]{1,0:T(8,128)(2,1)}, bf16[256,1536]{1,0:T(8,128)(2,1)}, u32[]{:S(2)}, u32[]{:S(2)}) %collective-permute-start.15) | collective-permute-done | bytes 786464 | tf_op jit(solution)/shard_map/ppermute | solution.py:408
  443.6 14.8 %attend_back.3 = (f32[1024,128]{1,0:T(8,128)}, f32[1024,128]{1,0:T(8,128)}, f32[1024,128]{1,0:T(8,128)}, bf16[1024,128]{1,0:T(8,128)(2,1)}, f32[1024,128]{1,0:T(...) custom-call(s32[1]{0:T(128)} %bitcast.2.far_ref, bf16[1024,128]{1,0:T(8,128)(2,1)} %get-tuple-element.70.qh_ref, ...), custom_call_target="tpu_custom_call" | custom-call | flops 30720000000 | bytes 8388608 | tf_op jit(solution)/shard_map/attend_back/pallas_call | solution.py:367
  461.0 14.3 %attend_back.4 = (f32[1024,128]{1,0:T(8,128)}, f32[1024,128]{1,0:T(8,128)}, f32[1024,128]{1,0:T(8,128)}, bf16[1024,128]{1,0:T(8,128)(2,1)}, f32[1024,128]{1,0:T(...) custom-call(s32[1]{0:T(128)} %bitcast.2.far_ref, bf16[1024,128]{1,0:T(8,128)(2,1)} %get-tuple-element.75.qh_ref, ...), custom_call_target="tpu_custom_call" | custom-call | flops 30720000000 | bytes 8388608 | tf_op jit(solution)/shard_map/attend_back/pallas_call | solution.py:367
  477.8 14.5 %attend_back.5 = (f32[1024,128]{1,0:T(8,128)}, f32[1024,128]{1,0:T(8,128)}, f32[1024,128]{1,0:T(8,128)}, bf16[1024,128]{1,0:T(8,128)(2,1)}, f32[1024,128]{1,0:T(...) custom-call(s32[1]{0:T(128)} %bitcast.2.far_ref, bf16[1024,128]{1,0:T(8,128)(2,1)} %get-tuple-element.80.qh_ref, ...), custom_call_target="tpu_custom_call" | custom-call | flops 30720000000 | bytes 8388608 | tf_op jit(solution)/shard_map/attend_back/pallas_call | solution.py:367
  495.6 14.9 %prep_back.3 = (bf16[1024,128]{1,0:T(8,128)(2,1)}, bf16[1024,128]{1,0:T(8,128)(2,1)}, bf16[1024,128]{1,0:T(8,128)(2,1)}, f32[1032,128]{1,0:T(8,128)}, f32[8,128]{1,0:T(8,128)}, /*index=5*/f32[8,128]{1,0:T(8,128)}) custom-call(bf16[1024,1536]{1,0:T(8,128)(2,1)} %copy-done.41, bf16[1024,1536]{1,0:T(8,128)(2,1)} %copy-done.41, bf16[1024,1536]{1,0:T(8,128)(2,1)} %copy-done.41, ...), custom_call_target="tpu_custom_call" | custom-call | flops 30720000000 | bytes 8388608 | tf_op jit(solution)/shard_map/prep_back/pallas_call | solution.py:390
  511.3 14.7 %prep_back.4 = (bf16[1024,128]{1,0:T(8,128)(2,1)}, bf16[1024,128]{1,0:T(8,128)(2,1)}, bf16[1024,128]{1,0:T(8,128)(2,1)}, f32[1032,128]{1,0:T(8,128)}, f32[8,128]{1,0:T(8,128)}, /*index=5*/f32[8,128]{1,0:T(8,128)}) custom-call(bf16[1024,1536]{1,0:T(8,128)(2,1)} %copy-done.41, bf16[1024,1536]{1,0:T(8,128)(2,1)} %copy-done.41, bf16[1024,1536]{1,0:T(8,128)(2,1)} %copy-done.41, ...), custom_call_target="tpu_custom_call" | custom-call | flops 30720000000 | bytes 8388608 | tf_op jit(solution)/shard_map/prep_back/pallas_call | solution.py:390
  528.7 14.7 %prep_back.5 = (bf16[1024,128]{1,0:T(8,128)(2,1)}, bf16[1024,128]{1,0:T(8,128)(2,1)}, bf16[1024,128]{1,0:T(8,128)(2,1)}, f32[1032,128]{1,0:T(8,128)}, f32[8,128]{1,0:T(8,128)}, /*index=5*/f32[8,128]{1,0:T(8,128)}) custom-call(bf16[1024,1536]{1,0:T(8,128)(2,1)} %copy-done.41, bf16[1024,1536]{1,0:T(8,128)(2,1)} %copy-done.41, bf16[1024,1536]{1,0:T(8,128)(2,1)} %copy-done.41, ...), custom_call_target="tpu_custom_call" | custom-call | flops 30720000000 | bytes 8388608 | tf_op jit(solution)/shard_map/prep_back/pallas_call | solution.py:390
  572.9 12.3 %collective-permute-done.28 = bf16[256,1536]{1,0:T(8,128)(2,1)S(1)} collective-permute-done((bf16[256,1536]{1,0:T(8,128)(2,1)S(1)}, bf16[256,1536]{1,0:T(8,128)(2,1)S(1)}, u32[]{:S(2)}, u32[]{:S(2)}) %collective-permute-start.28) | collective-permute-done | bytes 786464 | tf_op jit(solution)/shard_map/ppermute | solution.py:408
  615.4 13.8 %reduce-scatter.7.cloned.1.call-done = bf16[96,1536]{1,0:T(8,128)(2,1)} async-done(((bf16[1536,1536]{1,0:T(8,128)(2,1)}), bf16[96,1536]{1,0:T(8,128)(2,1)}) %reduce-scatter.7.cloned.1.call-update) | async-done | bytes 294928 | tf_op jit(solution)/shard_map/reduce_scatter | solution.py:592
  630.9 103.7 %reduce-scatter.13.cloned.1.call-done = bf16[192,1664]{1,0:T(8,128)(2,1)} async-done(((bf16[1536,1664]{1,0:T(8,128)(2,1)}), bf16[192,1664]{1,0:T(8,128)(2,1)}) %reduce-scatter.13.cloned.1.call-update) | async-done | bytes 638992 | tf_op jit(solution)/shard_map/reduce_scatter | solution.py:659
  (389 shorter events, 277.0 us)
Async XLA Ops:
  7.2 93.6 %all-gather.5.cloned.1.call-start = ((), (), s32[]{:S(2)}) async-start(), calls=%async_computation.6 | async-start | bytes 5750784 | tf_op jit(solution)/shard_map/all_gather | solution.py:511
  15.9 183.6 %all-gather.7.cloned.1.call-start = ((), (), s32[]{:S(2)}) async-start(), calls=%async_computation.7 | async-start | bytes 5013504 | tf_op jit(solution)/shard_map/all_gather | solution.py:514
  16.6 251.0 %all-gather.9.cloned.1.call-start = ((), (), s32[]{:S(2)}) async-start(), calls=%async_computation.8 | async-start | bytes 7077888 | tf_op jit(solution)/shard_map/all_gather | solution.py:520
  118.5 40.0 %collective-permute-start.5 = (bf16[1024,128]{1,0:T(8,128)(2,1)S(1)}, bf16[1024,128]{1,0:T(8,128)(2,1)S(1)}, u32[]{:S(2)}, u32[]{:S(2)}) collective-permute-start(bf16[1024,128]{1,0:T(8,128)(2,1)S(1)} %get-tuple-element.187), channel_id=1, source_target_pairs={{0,4},{1,5},{2,6},{3,7},{8,12},{9,13},{10,14},{11,15},{16,20},{17,... | collective-permute-start | bytes 786440 | tf_op jit(solution)/shard_map/ppermute | solution.py:414
  120.2 49.3 %collective-permute-start.7 = (bf16[1024,128]{1,0:T(8,128)(2,1)S(1)}, bf16[1024,128]{1,0:T(8,128)(2,1)S(1)}, u32[]{:S(2)}, u32[]{:S(2)}) collective-permute-start(bf16[1024,128]{1,0:T(8,128)(2,1)S(1)} %get-tuple-element.189), channel_id=1, source_target_pairs={{0,4},{1,5},{2,6},{3,7},{8,12},{9,13},{10,14},{11,15},{16,20},{17,... | collective-permute-start | bytes 786440 | tf_op jit(solution)/shard_map/ppermute | solution.py:414
  121.6 57.3 %collective-permute-start.9 = (bf16[1024,128]{1,0:T(8,128)(2,1)S(1)}, bf16[1024,128]{1,0:T(8,128)(2,1)S(1)}, u32[]{:S(2)}, u32[]{:S(2)}) collective-permute-start(bf16[1024,128]{1,0:T(8,128)(2,1)S(1)} %get-tuple-element.188), channel_id=1, source_target_pairs={{0,4},{1,5},{2,6},{3,7},{8,12},{9,13},{10,14},{11,15},{16,20},{17,... | collective-permute-start | bytes 786440 | tf_op jit(solution)/shard_map/ppermute | solution.py:414
  134.3 26.0 %collective-permute-start.4 = (bf16[1024,128]{1,0:T(8,128)(2,1)}, bf16[1024,128]{1,0:T(8,128)(2,1)S(1)}, u32[]{:S(2)}, u32[]{:S(2)}) collective-permute-start(bf16[1024,128]{1,0:T(8,128)(2,1)} %get-tuple-element.74), channel_id=1, source_target_pairs={{0,4},{1,5},{2,6},{3,7},{8,12},{9,13},{10,14},{11,15},{16,20},{17,... | collective-permute-start | bytes 786440 | tf_op jit(solution)/shard_map/ppermute | solution.py:414
  196.5 131.6 %all-gather.11.cloned.1.call-start = ((), (), s32[]{:S(2)}) async-start(), calls=%async_computation.9 | async-start | bytes 3538944 | tf_op jit(solution)/shard_map/all_gather | solution.py:521
  196.5 27.6 %collective-permute-start.16 = (bf16[256,1536]{1,0:T(8,128)(2,1)}, bf16[256,1536]{1,0:T(8,128)(2,1)}, u32[]{:S(2)}, u32[]{:S(2)}) collective-permute-start(bf16[256,1536]{1,0:T(8,128)(2,1)} %bitcast.17), channel_id=1, source_target_pairs={{0,1},{1,0},{2,3},{3,2},{4,5},{5,4},{6,7},{7,6},{8,9},{9,8},{10,11... | collective-permute-start | bytes 2359304 | tf_op jit(solution)/shard_map/ppermute | solution.py:408
  212.2 28.8 %collective-permute-start.10 = (bf16[256,1536]{1,0:T(8,128)(2,1)}, bf16[256,1536]{1,0:T(8,128)(2,1)S(1)}, u32[]{:S(2)}, u32[]{:S(2)}) collective-permute-start(bf16[256,1536]{1,0:T(8,128)(2,1)} %multiply_convert_fusion.3), channel_id=1, source_target_pairs={{0,1},{1,0},{2,3},{3,2},{4,5},{5,4},{6,7},{7,6},{8,9},{9,8},{10,11... | collective-permute-start | bytes 2359304 | tf_op jit(solution)/shard_map/ppermute | solution.py:408
  215.1 381.6 %reduce-scatter.11.cloned.1.call-start = ((), (), s32[]{:S(2)}) async-start(), calls=%async_computation.12 | async-start | bytes 3538944 | tf_op jit(solution)/shard_map/reduce_scatter | solution.py:584
  345.1 260.6 %reduce-scatter.9.cloned.1.call-start = ((), (), s32[]{:S(2)}) async-start(), calls=%async_computation.11 | async-start | bytes 7077888 | tf_op jit(solution)/shard_map/reduce_scatter | solution.py:585
  390.6 30.9 %collective-permute-start.15 = (bf16[256,1536]{1,0:T(8,128)(2,1)}, bf16[256,1536]{1,0:T(8,128)(2,1)}, u32[]{:S(2)}, u32[]{:S(2)}) collective-permute-start(bf16[256,1536]{1,0:T(8,128)(2,1)} %dynamic-slice_convert_fusion.5), channel_id=1, source_target_pairs={{0,1},{1,0},{2,3},{3,2},{4,5},{5,4},{6,7},{7,6},{8,9},{9,8},{10,11... | collective-permute-start | bytes 2359304 | tf_op jit(solution)/shard_map/ppermute | solution.py:408
  431.9 197.2 %reduce-scatter.7.cloned.1.call-start = ((), (), s32[]{:S(2)}) async-start(), calls=%async_computation.10 | async-start | bytes 5013504 | tf_op jit(solution)/shard_map/reduce_scatter | solution.py:592
  435.6 299.1 %reduce-scatter.13.cloned.1.call-start = ((), (), s32[]{:S(2)}) async-start(), calls=%async_computation.13 | async-start | bytes 5750784 | tf_op jit(solution)/shard_map/reduce_scatter | solution.py:659
  458.4 35.2 %collective-permute-start.20 = (bf16[1024,128]{1,0:T(8,128)(2,1)}, bf16[1024,128]{1,0:T(8,128)(2,1)S(1)}, u32[]{:S(2)}, u32[]{:S(2)}) collective-permute-start(bf16[1024,128]{1,0:T(8,128)(2,1)} %get-tuple-element.92), channel_id=1, source_target_pairs={{4,0},{5,1},{6,2},{7,3},{12,8},{13,9},{14,10},{15,11},{20,16},{21,... | collective-permute-start | bytes 786440 | tf_op jit(solution)/shard_map/ppermute | solution.py:414
  459.7 35.3 %collective-permute-start.21 = (bf16[1024,128]{1,0:T(8,128)(2,1)}, bf16[1024,128]{1,0:T(8,128)(2,1)S(1)}, u32[]{:S(2)}, u32[]{:S(2)}) collective-permute-start(bf16[1024,128]{1,0:T(8,128)(2,1)} %get-tuple-element.93), channel_id=1, source_target_pairs={{4,0},{5,1},{6,2},{7,3},{12,8},{13,9},{14,10},{15,11},{20,16},{21,... | collective-permute-start | bytes 786440 | tf_op jit(solution)/shard_map/ppermute | solution.py:414
  475.3 35.3 %collective-permute-start.22 = (bf16[1024,128]{1,0:T(8,128)(2,1)}, bf16[1024,128]{1,0:T(8,128)(2,1)S(1)}, u32[]{:S(2)}, u32[]{:S(2)}) collective-permute-start(bf16[1024,128]{1,0:T(8,128)(2,1)} %get-tuple-element.102), channel_id=1, source_target_pairs={{4,0},{5,1},{6,2},{7,3},{12,8},{13,9},{14,10},{15,11},{20,16},{21,... | collective-permute-start | bytes 786440 | tf_op jit(solution)/shard_map/ppermute | solution.py:414
  476.5 34.0 %collective-permute-start.23 = (bf16[1024,128]{1,0:T(8,128)(2,1)}, bf16[1024,128]{1,0:T(8,128)(2,1)S(1)}, u32[]{:S(2)}, u32[]{:S(2)}) collective-permute-start(bf16[1024,128]{1,0:T(8,128)(2,1)} %get-tuple-element.103), channel_id=1, source_target_pairs={{4,0},{5,1},{6,2},{7,3},{12,8},{13,9},{14,10},{15,11},{20,16},{21,... | collective-permute-start | bytes 786440 | tf_op jit(solution)/shard_map/ppermute | solution.py:414
  492.3 35.6 %collective-permute-start.24 = (bf16[1024,128]{1,0:T(8,128)(2,1)}, bf16[1024,128]{1,0:T(8,128)(2,1)S(1)}, u32[]{:S(2)}, u32[]{:S(2)}) collective-permute-start(bf16[1024,128]{1,0:T(8,128)(2,1)} %get-tuple-element.112), channel_id=1, source_target_pairs={{4,0},{5,1},{6,2},{7,3},{12,8},{13,9},{14,10},{15,11},{20,16},{21,... | collective-permute-start | bytes 786440 | tf_op jit(solution)/shard_map/ppermute | solution.py:414
  493.6 34.3 %collective-permute-start.25 = (bf16[1024,128]{1,0:T(8,128)(2,1)}, bf16[1024,128]{1,0:T(8,128)(2,1)S(1)}, u32[]{:S(2)}, u32[]{:S(2)}) collective-permute-start(bf16[1024,128]{1,0:T(8,128)(2,1)} %get-tuple-element.113), channel_id=1, source_target_pairs={{4,0},{5,1},{6,2},{7,3},{12,8},{13,9},{14,10},{15,11},{20,16},{21,... | collective-permute-start | bytes 786440 | tf_op jit(solution)/shard_map/ppermute | solution.py:414
  606.8 23.5 %collective-permute-start.32 = (bf16[96,2048]{1,0:T(8,128)(2,1)S(1)}, bf16[96,2048]{1,0:T(8,128)(2,1)S(1)}, u32[]{:S(2)}, u32[]{:S(2)}) collective-permute-start(bf16[96,2048]{1,0:T(8,128)(2,1)S(1)} %constant_dynamic-slice_fusion.1), channel_id=1, source_target_pairs={{0,2},{2,0},{1,3},{3,1},{4,6},{6,4},{5,7},{7,5},{8,10},{10,8},{9,1... | collective-permute-start | bytes 1179656 | tf_op jit(solution)/shard_map/ppermute | solution.py:408
  629.1 107.6 %collective-permute-start.31 = (bf16[96,1536]{1,0:T(8,128)(2,1)}, bf16[96,1536]{1,0:T(8,128)(2,1)}, u32[]{:S(2)}, u32[]{:S(2)}) collective-permute-start(bf16[96,1536]{1,0:T(8,128)(2,1)} %reduce-scatter.7.cloned.1.call-done), channel_id=1, source_target_pairs={{0,1},{1,0},{2,3},{3,2},{4,5},{5,4},{6,7},{7,6},{8,9},{9,8},{10,11... | collective-permute-start | bytes 884744 | tf_op jit(solution)/shard_map/ppermute | solution.py:408
  630.6 111.2 %collective-permute-start.33 = (bf16[2,96,2048]{2,1,0:T(8,128)(2,1)S(1)}, bf16[2,96,2048]{2,1,0:T(8,128)(2,1)}, u32[]{:S(2)}, u32[]{:S(2)}) collective-permute-start(bf16[2,96,2048]{2,1,0:T(8,128)(2,1)S(1)} %pad_maximum_fusion.15), channel_id=1, source_target_pairs={{0,1},{1,0},{2,3},{3,2},{4,5},{5,4},{6,7},{7,6},{8,9},{9,8},{10,11... | collective-permute-start | bytes 2359304 | tf_op jit(solution)/shard_map/ppermute | solution.py:408
  (95 other events, 864.2 us)
Sparse Core Ops, SparseCore 0:
  16.0 84.7 all-gather.4
  103.1 53.3 all-gather.6
  159.2 108.3 all-gather.8
  270.2 57.7 all-gather.10
  345.2 74.1 reduce-scatter.10
  422.9 128.5 reduce-scatter.8
  555.3 73.7 reduce-scatter.6
  632.8 101.7 reduce-scatter.12

commit v2 on v1

--- a/solution.py
+++ b/solution.py
@@ -404,6 +404,415 @@
     )(projected, projected, projected, rim, kernel, logits, w, t, kh, p, ds, dqh, dkh, dp, dv, dkt, dvt)
 
 
+MESH = pl.DeviceIdType.MESH
+
+
+def greet(r, row_count, y, y_count):
+    c, q = lax.axis_index("cc"), lax.axis_index("seq")
+    barrier = pltpu.get_barrier_semaphore()
+
+    def tell(where):
+        pl.semaphore_signal(barrier, inc=1, device_id=where, device_id_type=MESH)
+
+    @pl.when(r > 0)
+    def _():
+        tell({"row": r - 1})
+
+    @pl.when(r < row_count - 1)
+    def _():
+        tell({"row": r + 1})
+
+    for step in range(1, y_count):
+        tell({"cy": lax.rem(y + step, y_count)})
+    tell({"cc": 1 - c})
+    tell({"seq": 1 - q})
+    tell({"cc": 1 - c, "seq": 1 - q})
+    edges = jnp.where(r > 0, 1, 0) + jnp.where(r < row_count - 1, 1, 0)
+    pl.semaphore_wait(barrier, edges + (y_count - 1) + 3)
+
+
+def remote(source, target, send, recv, where):
+    return pltpu.make_async_remote_copy(source, target, send, recv, device_id=where, device_id_type=MESH)
+
+
+def gather_kernel(row_count, y_count, features, qkvu_ref, small_ref, out_w_ref, x_ref, g_ref,
+                  wide_ref, packed_ref, wo_ref, xs_ref, gs_ref,
+                  local_sem, cc_send, cc_recv, tok_send, tok_recv, up_send, down_send, z_recv, y_send, y_recv,
+                  wo_y_send, wo_y_recv, wo_x_send, wo_x_recv, wo_c_send, wo_c_recv):
+    r, y = lax.axis_index("row"), lax.axis_index("cy")
+    c, q = lax.axis_index("cc"), lax.axis_index("seq")
+    t, other_t = c * 2 + q, (1 - c) * 2 + q
+    width = wo_ref.shape[-1]
+    half = width // 2
+    middle = wide_ref.shape[-1] // 2
+    columns = pl.ds(pl.multiple_of(q * half, half), half)
+    greet(r, row_count, y, y_count)
+
+    def lanes(block, part):
+        return pl.ds(pl.multiple_of(block * width + part * features, features), features)
+
+    local, cross = [], []
+    for block in range(4):
+        place = wide_ref.at[r, y, c, :, pl.ds(block * features, features)]
+        local.append(pltpu.make_async_copy(qkvu_ref.at[:, lanes(block, t)], place, local_sem.at[block]))
+        cross.append(remote(qkvu_ref.at[:, lanes(block, other_t)], place, cc_send.at[block], cc_recv.at[block], {"cc": 1 - c}))
+    local.append(pltpu.make_async_copy(small_ref, packed_ref.at[r, y, c], local_sem.at[4]))
+    cross.append(remote(small_ref, packed_ref.at[r, y, c], cc_send.at[4], cc_recv.at[4], {"cc": 1 - c}))
+    own_out = out_w_ref.at[:, columns]
+    local.append(pltpu.make_async_copy(own_out, wo_ref.at[r, y, c, :, columns], local_sem.at[5]))
+    local.append(pltpu.make_async_copy(x_ref, xs_ref.at[t], local_sem.at[6]))
+    local.append(pltpu.make_async_copy(g_ref, gs_ref.at[t], local_sem.at[7]))
+
+    def wo_y_copy(from_y, step):
+        return remote(own_out, wo_ref.at[r, from_y, c, :, columns], wo_y_send.at[step], wo_y_recv.at[from_y],
+                      {"cy": lax.rem(y + step, y_count)})
+
+    for copy in cross:
+        copy.start()
+    for step in range(1, y_count):
+        wo_y_copy(y, step).start()
+    for copy in local:
+        copy.start()
+
+    def token_copy(which, source, target, slot, kind, where):
+        return remote(source, target.at[slot], tok_send.at[which, kind], tok_recv.at[which, kind], where)
+
+    tokens = []
+    for which, (source, target) in enumerate(((x_ref, xs_ref), (g_ref, gs_ref))):
+        tokens.append([
+            token_copy(which, source, target, t, 0, {"seq": 1 - q}),
+            token_copy(which, source, target, t, 1, {"cc": 1 - c}),
+        ])
+    tokens[0][0].start()
+    tokens[0][1].start()
+
+    def piece(kind, row, at_y):
+        if kind == 0:
+            return packed_ref.at[row, at_y]
+        if kind == 1:
+            return wo_ref.at[row, :, c, :, columns]
+        return wide_ref.at[row, at_y, :, :, pl.ds((kind - 2) * middle, middle)]
+
+    def z_copy(kind, origin, step):
+        sems = up_send if step > 0 else down_send
+        block = piece(kind, origin, y)
+        return remote(block, block, sems.at[kind, origin], z_recv.at[kind, origin], {"row": r + step})
+
+    def y_copy(kind, origin, from_y, step):
+        block = piece(kind, origin, from_y)
+        return remote(block, block, y_send.at[kind, origin, step], y_recv.at[kind, origin, from_y],
+                      {"cy": lax.rem(y + step, y_count)})
+
+    def wo_x_copy(origin):
+        block = piece(1, origin, y)
+        return remote(block, block, wo_x_send.at[origin], wo_x_recv.at[origin], {"seq": 1 - q})
+
+    def wo_c_copy(origin):
+        block = wo_ref.at[origin, :, c]
+        return remote(block, block, wo_c_send.at[origin], wo_c_recv.at[origin], {"cc": 1 - c})
+
+    def pass_on(kind, origin, up, down):
+        if up:
+            @pl.when(r < row_count - 1)
+            def _():
+                z_copy(kind, origin, 1).start()
+        if down:
+            @pl.when(r > 0)
+            def _():
+                z_copy(kind, origin, -1).start()
+        if kind == 1:
+            wo_x_copy(origin).start()
+        else:
+            for step in range(1, y_count):
+                y_copy(kind, origin, y, step).start()
+
+    local[4].wait()
+    cross[4].wait_recv()
+    pass_on(0, r, True, True)
+    for kind in (2, 3):
+        for block in (2 * (kind - 2), 2 * (kind - 2) + 1):
+            local[block].wait()
+            cross[block].wait_recv()
+        pass_on(kind, r, True, True)
+    local[5].wait()
+    for step in range(1, y_count):
+        wo_y_copy(lax.rem(y + step, y_count), step).wait_recv()
+    pass_on(1, r, True, True)
+    tokens[1][0].start()
+    tokens[1][1].start()
+    for k in range(1, row_count):
+        for kind in (0, 2, 3, 1):
+            @pl.when(r - k >= 0)
+            def _():
+                z_copy(kind, r - k, 1).wait_recv()
+                pass_on(kind, r - k, True, False)
+
+            @pl.when(r + k < row_count)
+            def _():
+                z_copy(kind, r + k, -1).wait_recv()
+                pass_on(kind, r + k, False, True)
+
+    relays = []
+    for which, target in enumerate((xs_ref, gs_ref)):
+        tokens[which][0].wait_recv()
+        slot = c * 2 + 1 - q
+        relay = token_copy(which, target.at[slot], target, slot, 2, {"cc": 1 - c})
+        relay.start()
+        relays.append(relay)
+    for origin in range(row_count):
+        wo_x_copy(origin).wait_recv()
+        wo_c_copy(origin).start()
+    for origin in range(row_count):
+        for kind in (0, 2, 3):
+            for step in range(1, y_count):
+                y_copy(kind, origin, lax.rem(y + step, y_count), step).wait_recv()
+        wo_c_copy(origin).wait_recv()
+    for which in range(2):
+        tokens[which][1].wait_recv()
+        relays[which].wait_recv()
+        tokens[which][0].wait_send()
+        tokens[which][1].wait_send()
+        relays[which].wait_send()
+    local[6].wait()
+    local[7].wait()
+    for copy in cross:
+        copy.wait_send()
+    for step in range(1, y_count):
+        wo_y_copy(y, step).wait_send()
+    for origin in range(row_count):
+        for kind in range(4):
+            @pl.when((r >= origin) & (r < row_count - 1))
+            def _():
+                z_copy(kind, origin, 1).wait_send()
+
+            @pl.when((r <= origin) & (r > 0))
+            def _():
+                z_copy(kind, origin, -1).wait_send()
+
+            if kind != 1:
+                for step in range(1, y_count):
+                    y_copy(kind, origin, y, step).wait_send()
+        wo_x_copy(origin).wait_send()
+        wo_c_copy(origin).wait_send()
+
+
+def gather_first(qkvu, small, out_w, x, g, features):
+    row_count, y_count = lax.axis_size("row"), lax.axis_size("cy")
+    rows = qkvu.shape[0]
+    width = out_w.shape[1]
+    vm = pl.BlockSpec(memory_space=pltpu.VMEM)
+    anywhere = pl.BlockSpec(memory_space=pl.ANY)
+    dma = pltpu.SemaphoreType.DMA
+    lead = (row_count, y_count, 2)
+    wide, packed, wo, xs, gs = pl.pallas_call(
+        functools.partial(gather_kernel, row_count, y_count, features),
+        in_specs=[vm] * 5,
+        out_specs=[anywhere] * 5,
+        out_shape=[
+            jax.ShapeDtypeStruct(lead + (rows, 4 * features), bf16),
+            jax.ShapeDtypeStruct(lead + small.shape, bf16),
+            jax.ShapeDtypeStruct(lead + (rows, width), bf16),
+            jax.ShapeDtypeStruct((4,) + x.shape, bf16),
+            jax.ShapeDtypeStruct((4,) + g.shape, bf16),
+        ],
+        scratch_shapes=[dma((8,)), dma((5,)), dma((5,)), dma((2, 3)), dma((2, 3)),
+                        dma((4, row_count)), dma((4, row_count)), dma((4, row_count)),
+                        dma((4, row_count, y_count)), dma((4, row_count, y_count)),
+                        dma((y_count,)), dma((y_count,))] + [dma((row_count,))] * 4,
+        compiler_params=pltpu.CompilerParams(collective_id=1, has_side_effects=True, vmem_limit_bytes=48 * 1024 * 1024),
+        name="gather_first",
+    )(qkvu, small, out_w, x, g)
+    total = row_count * y_count * 2 * rows
+    return (wide.reshape(total, 4 * features), packed, wo.reshape(total, width),
+            xs.reshape(4 * x.shape[0], -1), gs.reshape(4 * g.shape[0], -1))
+
+
+def scatter_kernel(row_count, y_count, p_ref, dh_ref, gu_ref, dn_ref, res_ref, gu_res_ref, dn_res_ref, dh_res_ref,
+                   yin_ref, up_ref, down_ref, out_ref, dcc_ref, dst_ref, dseq_ref,
+                   y_send, y_recv, up_send, up_recv, down_send, down_recv, t_send, t_recv, n_send, n_recv,
+                   dh_send, dh_recv, local_sem):
+    r, y = lax.axis_index("row"), lax.axis_index("cy")
+    c, q = lax.axis_index("cc"), lax.axis_index("seq")
+    t = c * 2 + q
+    depth = p_ref.shape[1]
+    piece = 16 if depth % 16 == 0 else depth
+    greet(r, row_count, y, y_count)
+
+    def y_copy(dest, step):
+        to = lax.rem(y + step, y_count)
+        return remote(p_ref.at[dest * y_count + to], yin_ref.at[dest, step - 1], y_send.at[dest, step - 1],
+                      y_recv.at[dest, step - 1], {"cy": to})
+
+    def z_copy(dest, step):
+        landing, sends, recvs = (up_ref, up_send, up_recv) if step > 0 else (down_ref, down_send, down_recv)
+        return remote(out_ref.at[dest], landing.at[dest], sends.at[dest], recvs.at[dest], {"row": r + step})
+
+    def add_up(dest, extra):
+        def body(i, carry):
+            rows = pl.ds(pl.multiple_of(i * piece, piece), piece)
+            total = p_ref[dest * y_count + y, rows].astype(f32)
+            for step in range(1, y_count):
+                total = total + yin_ref[dest, step - 1, rows].astype(f32)
+            for more in extra:
+                total = total + more[dest, rows].astype(f32)
+            out_ref[dest, rows] = total.astype(bf16)
+            return carry
+
+        lax.fori_loop(0, depth // piece, body, 0)
+
+    order = []
+    for k in range(row_count - 1, 0, -1):
+        order += [(k, 1), (k, -1)]
+
+    def ordered(act):
+        for k, step in order:
+            dest = r + step * k
+            valid = (dest < row_count) if step > 0 else (dest >= 0)
+
+            @pl.when(valid)
+            def _():
+                act(dest, step)
+
+    def start_y(dest, step):
+        for hop in range(1, y_count):
+            y_copy(dest, hop).start()
+
+    def forward(dest, step):
+        for hop in range(1, y_count):
+            y_copy(dest, hop).wait_recv()
+        landing = up_ref if step > 0 else down_ref
+        inner = (r > 0) if step > 0 else (r < row_count - 1)
+
+        @pl.when(inner)
+        def _():
+            z_copy(dest, step).wait_recv()
+            add_up(dest, [landing])
+
+        @pl.when(jnp.logical_not(inner))
+        def _():
+            add_up(dest, [])
+
+        z_copy(dest, step).start()
+
+    half = depth // 2
+
+    def t_copies(which, source, target):
+        own = source.at[pl.ds(pl.multiple_of(c * half, half), half)]
+        other = source.at[pl.ds(pl.multiple_of((1 - c) * half, half), half)]
+        away = {"cc": 1 - c, "seq": 1 - q}
+        pieces = ((own, {"seq": 1 - q}), (other, away), (other, {"cc": 1 - c}))
+        return [
+            remote(part, target.at[t], t_send.at[which, kind], t_recv.at[which, kind], where)
+            for kind, (part, where) in enumerate(pieces)
+        ], pltpu.make_async_copy(own, target.at[t], local_sem.at[which])
+
+    dh_cc = remote(dh_ref.at[pl.ds((1 - c) * 2, 2)], dcc_ref, dh_send.at[0], dh_recv.at[0], {"cc": 1 - c})
+    dh_seq = remote(dst_ref, dseq_ref, dh_send.at[1], dh_recv.at[1], {"seq": 1 - q})
+    dh_cc.start()
+    ordered(start_y)
+    start_y(r, 0)
+    tokens = dh_ref.shape[1]
+    step_rows = 16 if tokens % 16 == 0 else tokens
+
+    def token_loop(act):
+        def body(i, carry):
+            act(pl.ds(pl.multiple_of(i * step_rows, step_rows), step_rows))
+            return carry
+
+        lax.fori_loop(0, tokens // step_rows, body, 0)
+
+    dh_cc.wait_recv()
+
+    def stage(rows):
+        dst_ref[rows] = (dh_ref[c * 2 + 1 - q, rows].astype(f32) + dcc_ref[1 - q, rows].astype(f32)).astype(bf16)
+
+    token_loop(stage)
+    gu_last, gu_local = t_copies(1, gu_ref, gu_res_ref)
+    dn_last = remote(dn_ref, dn_res_ref.at[q], n_send.at[0], n_recv.at[0], {"seq": 1 - q})
+    dn_local = pltpu.make_async_copy(dn_ref, dn_res_ref.at[q], local_sem.at[2])
+    gu_local.start()
+    dn_local.start()
+    dh_seq.start()
+    for copy in gu_last:
+        copy.start()
+    dn_last.start()
+    ordered(forward)
+    dh_seq.wait_recv()
+
+    def settle(rows):
+        total = dh_ref[t, rows].astype(f32) + dcc_ref[q, rows].astype(f32)
+        dh_res_ref[rows] = total + dseq_ref[rows].astype(f32)
+
+    token_loop(settle)
+    for hop in range(1, y_count):
+        y_copy(r, hop).wait_recv()
+
+    @pl.when(r == 0)
+    def _():
+        z_copy(r, -1).wait_recv()
+        add_up(r, [down_ref])
+
+    @pl.when(r == row_count - 1)
+    def _():
+        z_copy(r, 1).wait_recv()
+        add_up(r, [up_ref])
+
+    @pl.when((r > 0) & (r < row_count - 1))
+    def _():
+        z_copy(r, 1).wait_recv()
+        z_copy(r, -1).wait_recv()
+        add_up(r, [up_ref, down_ref])
+
+    last, local = t_copies(0, out_ref.at[r], res_ref)
+    for copy in last:
+        copy.start()
+    local.start()
+
+    def sent(dest, step):
+        for hop in range(1, y_count):
+            y_copy(dest, hop).wait_send()
+        z_copy(dest, step).wait_send()
+
+    ordered(sent)
+    for hop in range(1, y_count):
+        y_copy(r, hop).wait_send()
+    for copy in gu_last + [dn_last]:
+        copy.wait()
+    dh_cc.wait_send()
+    dh_seq.wait_send()
+    gu_local.wait()
+    dn_local.wait()
+    for copy in last:
+        copy.wait()
+    local.wait()
+
+
+def scatter_last(partial, d_h, gate_up_sum, down_sum):
+    row_count, y_count = lax.axis_size("row"), lax.axis_size("cy")
+    total, cols = partial.shape
+    depth = total // (row_count * y_count)
+    tokens, width = d_h.shape[0] // 4, d_h.shape[1]
+    vm = pl.BlockSpec(memory_space=pltpu.VMEM)
+    dma = pltpu.SemaphoreType.DMA
+    block = lambda *lead: pltpu.VMEM(lead + (depth, cols), bf16)
+    shape = jax.ShapeDtypeStruct
+    return pl.pallas_call(
+        functools.partial(scatter_kernel, row_count, y_count),
+        in_specs=[vm] * 4,
+        out_specs=[vm] * 4,
+        out_shape=[shape((4, depth // 2, cols), bf16), shape((4, depth // 2, gate_up_sum.shape[1]), bf16),
+                   shape((2,) + down_sum.shape, bf16), shape((tokens, width), f32)],
+        scratch_shapes=[block(row_count, y_count - 1), block(row_count), block(row_count), block(row_count),
+                        pltpu.VMEM((2, tokens, width), bf16), pltpu.VMEM((tokens, width), bf16),
+                        pltpu.VMEM((tokens, width), bf16),
+                        dma((row_count, y_count - 1)), dma((row_count, y_count - 1)), dma((row_count,)), dma((row_count,)),
+                        dma((row_count,)), dma((row_count,)), dma((2, 3)), dma((2, 3)), dma((1,)), dma((1,)),
+                        dma((2,)), dma((2,)), dma((3,))],
+        compiler_params=pltpu.CompilerParams(collective_id=2, has_side_effects=True, vmem_limit_bytes=56 * 1024 * 1024),
+        name="scatter_last",
+    )(partial.reshape(row_count * y_count, depth, cols), d_h.reshape(4, tokens, width), gate_up_sum, down_sum)
+
+
 def swapped(value, axis):
     return lax.ppermute(value, axis, [(0, 1), (1, 0)])
 
@@ -438,6 +847,18 @@
     return own + swapped(other, "seq").astype(f32)
 
 
+def reduce_columns(partial):
+    half = partial.shape[1] // 2
+    cc, seq = lax.axis_index("cc"), lax.axis_index("seq")
+    mine = lax.dynamic_slice_in_dim(partial, cc * half, half, 1)
+    theirs = lax.dynamic_slice_in_dim(partial, (1 - cc) * half, half, 1).astype(bf16)
+    mine = mine + swapped(theirs, "cc").astype(f32)
+    quarter = half // 2
+    own = lax.dynamic_slice_in_dim(mine, seq * quarter, quarter, 1)
+    other = lax.dynamic_slice_in_dim(mine, (1 - seq) * quarter, quarter, 1).astype(bf16)
+    return own + swapped(other, "seq").astype(f32)
+
+
 def rms_norm(values, gain):
     return values * lax.rsqrt(jnp.mean(values * values, -1, keepdims=True) + epsilon) * gain
 
@@ -459,22 +880,6 @@
 
 def share_rows(mine, theirs):
     return in_order(mine, swapped(theirs, "cc"), lax.axis_index("cc"))
-
-
-def finish(reduced):
-    cc, seq = lax.axis_index("cc"), lax.axis_index("seq")
-    rows = reduced.shape[0] // 2
-    mine = lax.dynamic_slice_in_dim(reduced, cc * rows, rows, 0)
-    theirs = swapped(lax.dynamic_slice_in_dim(reduced, (1 - cc) * rows, rows, 0), "cc")
-    first = cc == 0
-    pair = jnp.stack([jnp.where(first, mine, theirs), jnp.where(first, theirs, mine)])
-    other = swapped(pair, "seq")
-    first = seq == 0
-    return [
-        (jnp.where(first, pair[i], other[i]) if j == 0 else jnp.where(first, other[i], pair[i])).astype(f32)
-        for i in range(2)
-        for j in range(2)
-    ]
 
 
 def per_device(
@@ -493,7 +898,7 @@
     taps = conv_kernel.shape[0]
     rows = qkvu_weight.shape[0]
     ff_rows = down_weight.shape[0]
-    ff_part = ff_rows // group
+    ff_part = 2 * ff_rows // group
     span = group * tok_count
     length = seq_len[0]
     first_slot = cy * span
@@ -501,37 +906,30 @@
     valid = (first_slot + member * tok_count + jnp.arange(tok_count) < length)[:, None]
     all_axes = ("row", "cy")
 
-    small = jnp.concatenate(
-        [norm_gain1[:, None], norm_gain2[:, None], conv_kernel.T, beta_weight], axis=1
+    small = jnp.concatenate([norm_gain1[None], norm_gain2[None], conv_kernel, beta_weight.T], axis=0)
+    small = jnp.pad(small, ((0, 32 - small.shape[0]), (0, CH - rows)))
+    wide_qkvu, packed, wide_out, span_input, span_grad = gather_first(
+        qkvu_weight, small, out_weight, own16, out_grad[0], features
     )
-    small = jnp.pad(small, ((0, 0), (0, CH - small.shape[1])))
-    mine, theirs = column_share(qkvu_weight.reshape(rows, 4, group, features), 4, group, 2)
-    mine = jnp.concatenate([mine.reshape(rows, 4 * features), small], axis=1)
-    theirs = jnp.concatenate([theirs.reshape(rows, 4 * features), small], axis=1)
-    wide = lax.all_gather(share_rows(mine, theirs), all_axes, axis=0, tiled=True)
-    wide_qkvu = wide[:, : 4 * features]
-    packed = wide[:, 4 * features :]
-    wide_out = lax.all_gather(out_weight, ("row", "cy", "cc"), axis=0, tiled=True)
-    shards = width // rows
-    mine, theirs = column_share(gate_up_weight.reshape(rows, 2, shards, group, ff_part), 2, group, 3)
+    pairs = width // (2 * rows)
+    mine, theirs = column_share(gate_up_weight.reshape(rows, 2, pairs, group, ff_part), 2, group, 3)
     gate_up_pair = share_rows(mine.reshape(rows, -1), theirs.reshape(rows, -1))
-    mine, theirs = column_share(down_weight.reshape(group, ff_part, width), 1, group, 0)
-    down_pair = share_rows(mine, theirs)
+    down_own = lax.dynamic_slice_in_dim(down_weight, seq * ff_part, ff_part, 0)
     wide_gate_up = lax.all_gather(gate_up_pair, all_axes, axis=0, tiled=True)
-    wide_down = lax.all_gather(down_pair, all_axes, axis=0, tiled=True)
-
-    gain_one = packed[:, 0].astype(f32)
-    gain_two = packed[:, 1].astype(f32)
-    kernel = lax.dynamic_slice_in_dim(packed[:, 2 : 2 + taps], member * features, features, 0)
-    kernel = jnp.pad(kernel.T.astype(f32), ((0, 8 - taps), (0, 0)))
-    beta_local = lax.dynamic_slice_in_dim(packed[:, 2 + taps : 2 + taps + heads], member * local, local, 1)
-    beta_pad = jnp.pad(beta_local, ((0, 0), (0, CH - local)))
-
-    span_input = gather_group(own16)
-    span_grad = jnp.where(valid_span, gather_group(out_grad[0]), 0)
+    wide_down = lax.all_gather(down_own, all_axes, axis=0, tiled=True)
+
+    packed = packed[..., :rows].transpose(3, 0, 1, 2, 4).reshape(packed.shape[3], width)
+    gain_one = packed[0].astype(f32)
+    gain_two = packed[1].astype(f32)
+    kernel = lax.dynamic_slice_in_dim(packed[2 : 2 + taps], member * features, features, 1)
+    kernel = jnp.pad(kernel.astype(f32), ((0, 8 - taps), (0, 0)))
+    beta_local = lax.dynamic_slice_in_dim(packed[2 + taps : 2 + taps + heads], member * local, local, 0)
+    beta_pad = jnp.pad(beta_local, ((0, CH - local), (0, 0)))
+
+    span_grad = jnp.where(valid_span, span_grad, 0)
     h_first = rms_norm(span_input.astype(f32), gain_one).astype(bf16)
     projected = jnp.dot(h_first, wide_qkvu, preferred_element_type=f32).astype(bf16)
-    logits = jnp.dot(h_first, beta_pad, preferred_element_type=f32).astype(bf16)
+    logits = jnp.einsum("td,hd->th", h_first, beta_pad, preferred_element_type=f32).astype(bf16)
     rim = passed_along(projected[span - 8 :, 3 * features :], "cy", 1)
     far = jnp.reshape(cy * span, (1,)).astype(jnp.int32)
 
@@ -589,9 +987,7 @@
     d_mid = grad_rows + mid_norm_grad
     d_branch = d_mid.astype(bf16)
     out_term = jnp.einsum("td,te->de", back, d_branch, preferred_element_type=f32)
-    out_sum = lax.psum_scatter(
-        out_term.astype(bf16), ("row", "cy", "cc"), scatter_dimension=0, tiled=True
-    )
+    out_part = reduce_columns(out_term)
     d_back = jnp.einsum("te,de->td", d_branch, wide_out, preferred_element_type=f32).astype(bf16)
     d_attn = lax.all_to_all(d_back, ("cc", "seq"), split_axis=1, concat_axis=0, tiled=True)
 
@@ -639,11 +1035,9 @@
     qkvu_term = jnp.einsum("td,tn->dn", h_first, d_projected, preferred_element_type=f32)
     beta_term = jnp.einsum("td,ht->dh", h_first, d_logits, preferred_element_type=f32)
     d_h_first = jnp.einsum("tn,dn->td", d_projected, wide_qkvu, preferred_element_type=f32)
-    d_h_first = d_h_first + jnp.einsum("ht,dh->td", d_logits, beta_local, preferred_element_type=f32)
-    d_h_first = reduce_group(d_h_first)
-    _, pull_first = jax.vjp(rms_norm, tokens, gain_one)
-    input_norm_grad, gain_one_term = pull_first(d_h_first)
-    input_grad = (d_mid + input_norm_grad).astype(bf16)[None]
+    d_h_first = d_h_first + jnp.einsum("ht,hd->td", d_logits, beta_local, preferred_element_type=f32)
+    normed = rms_norm(span_input.astype(f32), 1.0)
+    gain_one_term = jnp.sum(d_h_first * normed, 0)
 
     kernel_term = lax.dynamic_update_slice_in_dim(
         jnp.zeros((width, taps), f32), jnp.concatenate(kernel_rows, axis=1).T, member * features, 0
@@ -656,19 +1050,19 @@
     )
     used = small_term.shape[1]
     small_term = jnp.pad(small_term, ((0, 0), (0, CH - used)))
-    qkvu_sum = lax.psum_scatter(
-        jnp.concatenate([qkvu_term, small_term], axis=1).astype(bf16),
-        all_axes, scatter_dimension=0, tiled=True,
+    last, last_gate_up, last_down, d_h_first = scatter_last(
+        jnp.concatenate([qkvu_term, small_term, out_part], axis=1).astype(bf16),
+        d_h_first.astype(bf16), gate_up_sum, down_sum,
     )
-    parts = finish(qkvu_sum)
-    qkvu_grad = jnp.stack([part[:, : 4 * features].reshape(rows, 4, features) for part in parts], axis=2)
-    qkvu_grad = qkvu_grad.reshape(rows, 4 * width)
-    small_grad = sum(part[:, 4 * features :] for part in parts)
-    gate_up_grad = jnp.stack(
-        [part.reshape(rows, 2, shards, ff_part) for part in finish(gate_up_sum)], axis=3
-    ).reshape(rows, -1)
-    down_grad = jnp.concatenate(finish(down_sum), axis=0)
-    out_grad_own = out_sum.astype(f32) + swapped(out_sum, "seq").astype(f32)
+    _, pull_first = jax.vjp(rms_norm, tokens, gain_one)
+    input_grad = (d_mid + pull_first(d_h_first)[0]).astype(bf16)[None]
+    qkvu_grad = last[:, :, : 4 * features].reshape(group, rows, 4, features).transpose(1, 2, 0, 3)
+    qkvu_grad = qkvu_grad.reshape(rows, 4 * width).astype(f32)
+    small_grad = jnp.sum(last[:, :, 4 * features : 4 * features + CH].astype(f32), 0)
+    out_grad_own = last[:, :, 4 * features + CH :].transpose(1, 0, 2).reshape(rows, width).astype(f32)
+    gate_up_grad = last_gate_up.reshape(group, rows, 2, pairs, ff_part).transpose(1, 2, 3, 0, 4)
+    gate_up_grad = gate_up_grad.reshape(rows, -1).astype(f32)
+    down_grad = last_down.reshape(ff_rows, width).astype(f32)
     return (
         layer_output,
         input_grad,

time: 784 us -> 701 us (0.89)
  waiting for transfers between devices: 346 us -> 79.5 us
  Pallas kernels: 146 us -> 321 us
  matrix products: 80.5 us -> 90.9 us
    pallas_call x0 -> x2, Pallas kernels: none -> 176 us  [the longest x1 98.2 us: scatter_last(): pl.pallas_call(functools.partial(scatter_kernel, row_count, y_count), in_...]
    reduce_scatter x2 -> x0, waiting for transfers between devices: 118 us -> none  [the longest x1 104 us: per_device(): lax.psum_scatter(jnp.concatenate([qkvu_term, small_term], axis=1).astype(...]
    all_gather x3 -> x1, waiting for transfers between devices: 97.5 us -> 18.6 us  [per_device(): wide_down = lax.all_gather(down_own, all_axes, axis=0, tiled=True)]
    ppermute x22 -> x9, waiting for transfers between devices: 99.2 us -> 46.9 us  [swapped(): return lax.ppermute(value, axis, [(0, 1), (1, 0)])]
    convert_element_type x0 -> x10, local copies, waits for them, and re-layouts: none -> 24.2 us  [the longest x3 11.5 us: per_device(): qkvu_grad = qkvu_grad.reshape(rows, 4 * width).astype(f32)]
    all_gather x1, waiting for transfers between devices: 16.4 us -> 0.01 us  [per_device(): wide_gate_up = lax.all_gather(gate_up_pair, all_axes, axis=0, tiled=True)]
    ppermute x22 -> x9, starting transfers between devices: 22.5 us -> 9.54 us  [swapped(): return lax.ppermute(value, axis, [(0, 1), (1, 0)])]
    unnamed x166 -> x176, local copies, waits for them, and re-layouts: 34.9 us -> 25.9 us
  transfers between devices with their start and end apart: 46 -> 29, of which waited for: 20 -> 6; matrix products, arithmetic and copies ran while one was open for 21% -> 20% of each run, Pallas kernels for 19% -> 32%
where the time goes in v2:
time: 701 us; the launch traced here: 691 us
  Pallas kernels  321 us (46%)
  matrix products  90.9 us (13%)
  local copies, waits for them, and re-layouts  80.5 us (11%)
  waiting for transfers between devices  79.5 us (11%)
  other arithmetic  53.1 us (8%)
  starting transfers between devices  49.4 us (7%)
  between operations  16.2 us (2%)
    pallas_call x1, Pallas kernels, scatter_last(): pl.pallas_call(functools.partial(scatter_kernel, row_count, y_count), in_...  98.2 us
    pallas_call x1, Pallas kernels, gather_first(): pl.pallas_call(functools.partial(gather_kernel, row_count, y_count, featu...  77.5 us
    ppermute x9, waiting for transfers between devices, swapped(): return lax.ppermute(value, axis, [(0, 1), (1, 0)])  46.9 us
    pallas_call x3, Pallas kernels, prep_back(): pl.pallas_call(functools.partial(prep_back_kernel, unroll, head), grid=(1...  44.4 us
    pallas_call x3, Pallas kernels, attend_back(): pl.pallas_call(attend_back_kernel, grid=(1,), in_specs=[pl.BlockSpec(memo...  43.1 us
    pallas_call x3, Pallas kernels, prep(): pl.pallas_call(functools.partial(prep_kernel, unroll, head), grid=(1,), i...  32.4 us
    unnamed x176, local copies, waits for them, and re-layouts  25.9 us
    pallas_call x3, Pallas kernels, attend(): pl.pallas_call(attend_kernel, grid=(1,), in_specs=[pl.BlockSpec(memory_sp...  25.7 us
  transfers between devices with their start and end apart: 29, of which 6 were waited for; matrix products, arithmetic and copies ran while one was open for 20% of the time, Pallas kernels for 32%

profile of v2, /device:TPU:1, one launch (start us, length us, event | category | flops | bytes accessed | tf_op | source)
XLA Modules:
  0.0 690.8 jit_solution(17828611021820689494)
XLA Ops:
  20.6 77.5 %gather_first.1 = (bf16[4,2,2,96,1536]{4,3,2,1,0:T(8,128)(2,1)}, bf16[4,2,2,32,128]{4,3,2,1,0:T(8,128)(2,1)S(1)}, bf16[4,2,2,96,1536]{4,3,2,1,0:T(8,128)(2,1)}, ...) custom-call(bf16[96,6144]{1,0:T(8,128)(2,1)S(1)} %copy-done.5, bf16[32,128]{1,0:T(8,128)(2,1)S(1)} %fusion.24.small_ref, ...), custom_call_target="tpu_custom_call" | custom-call | tf_op jit(solution)/shard_map/gather_first/pallas_call | solution.py:607
  128.6 10.8 %prep.3 = (bf16[1024,128]{1,0:T(8,128)(2,1)}, bf16[1024,128]{1,0:T(8,128)(2,1)}, bf16[1024,128]{1,0:T(8,128)(2,1)}, bf16[1024,128]{1,0:T(8,128)(2,1)}, bf16[1024...) custom-call(bf16[1024,1536]{1,0:T(8,128)(2,1)} %copy-done.43, bf16[1024,1536]{1,0:T(8,128)(2,1)} %copy-done.43, ...), custom_call_target="tpu_custom_call" | custom-call | flops 10240000000 | bytes 4194304 | tf_op jit(solution)/shard_map/prep/pallas_call | solution.py:330
  140.7 10.8 %prep.4 = (bf16[1024,128]{1,0:T(8,128)(2,1)}, bf16[1024,128]{1,0:T(8,128)(2,1)}, bf16[1024,128]{1,0:T(8,128)(2,1)}, bf16[1024,128]{1,0:T(8,128)(2,1)}, bf16[1024...) custom-call(bf16[1024,1536]{1,0:T(8,128)(2,1)} %copy-done.43, bf16[1024,1536]{1,0:T(8,128)(2,1)} %copy-done.43, ...), custom_call_target="tpu_custom_call" | custom-call | flops 10240000000 | bytes 4194304 | tf_op jit(solution)/shard_map/prep/pallas_call | solution.py:330
  152.8 10.8 %prep.5 = (bf16[1024,128]{1,0:T(8,128)(2,1)}, bf16[1024,128]{1,0:T(8,128)(2,1)}, bf16[1024,128]{1,0:T(8,128)(2,1)}, bf16[1024,128]{1,0:T(8,128)(2,1)}, bf16[1024...) custom-call(bf16[1024,1536]{1,0:T(8,128)(2,1)} %copy-done.43, bf16[1024,1536]{1,0:T(8,128)(2,1)} %copy-done.43, ...), custom_call_target="tpu_custom_call" | custom-call | flops 10240000000 | bytes 4194304 | tf_op jit(solution)/shard_map/prep/pallas_call | solution.py:330
  165.7 8.5 %attend.3 = bf16[1024,128]{1,0:T(8,128)(2,1)} custom-call(s32[1]{0:T(128)} %bitcast.2.far_ref, bf16[1024,128]{1,0:T(8,128)(2,1)} %get-tuple-element.82.qh_ref, bf16[1024,128]{1,0:T(8,128)(2,1)} %get-tuple-element.83.kh_ref, bf16[1024,128]{1,0:T(8,128)(2,1)} %get-tuple-element.84.p_ref, f32[1024,128]{1,0:T(8,128)} %get-tuple-element.85.s_in_ref, ...), custom_call_target="tpu_custom_call" | custom-call | flops 10240000000 | bytes 4194304 | tf_op jit(solution)/shard_map/attend/pallas_call | solution.py:347
  174.9 8.5 %attend.4 = bf16[1024,128]{1,0:T(8,128)(2,1)} custom-call(s32[1]{0:T(128)} %bitcast.2.far_ref, bf16[1024,128]{1,0:T(8,128)(2,1)} %get-tuple-element.87.qh_ref, bf16[1024,128]{1,0:T(8,128)(2,1)} %get-tuple-element.88.kh_ref, bf16[1024,128]{1,0:T(8,128)(2,1)} %get-tuple-element.89.p_ref, f32[1024,128]{1,0:T(8,128)} %get-tuple-element.90.s_in_ref, ...), custom_call_target="tpu_custom_call" | custom-call | flops 10240000000 | bytes 4194304 | tf_op jit(solution)/shard_map/attend/pallas_call | solution.py:347
  184.2 8.6 %attend.5 = bf16[1024,128]{1,0:T(8,128)(2,1)} custom-call(s32[1]{0:T(128)} %bitcast.2.far_ref, bf16[1024,128]{1,0:T(8,128)(2,1)} %get-tuple-element.92.qh_ref, bf16[1024,128]{1,0:T(8,128)(2,1)} %get-tuple-element.93.kh_ref, bf16[1024,128]{1,0:T(8,128)(2,1)} %get-tuple-element.94.p_ref, f32[1024,128]{1,0:T(8,128)} %get-tuple-element.95.s_in_ref, ...), custom_call_target="tpu_custom_call" | custom-call | flops 10240000000 | bytes 4194304 | tf_op jit(solution)/shard_map/attend/pallas_call | solution.py:347
  198.9 10.6 %all-to-all-done = bf16[4,256,384]{1,2,0:T(8,128)(2,1)S(1)} async-done(((bf16[4,256,384]{1,2,0:T(8,128)(2,1)}), bf16[4,256,384]{1,2,0:T(8,128)(2,1)S(1)}, u32[]{:S(2)}, u32[]{:S(2)}) %all-to-all-start) | async-done | bytes 786464 | tf_op jit(solution)/shard_map/all_to_all | solution.py:960
  224.8 8.5 %collective-permute-done.7 = bf16[256,1536]{1,0:T(8,128)(2,1)S(1)} collective-permute-done((bf16[256,1536]{1,0:T(8,128)(2,1)S(1)}, bf16[256,1536]{1,0:T(8,128)(2,1)S(1)}, u32[]{:S(2)}, u32[]{:S(2)}) %collective-permute-start.7) | collective-permute-done | bytes 786464 | tf_op jit(solution)/shard_map/ppermute | solution.py:817
  246.1 12.0 %fusion.3 = f32[1024,2048]{1,0:T(8,128)} fusion(bf16[1536,2048]{1,0:T(8,128)(2,1)} %all-gather.3.cloned.1.call-done, bf16[512,1536]{1,0:T(8,128)(2,1)} %get-tuple-element.184, bf16[512,1536]{1,0:T(8,128)(2,1)} %get-tuple-element.183), kind=kOutput, calls=%fused_computation.36 | convolution fusion | flops 6448742400 | bytes 17825792 | tf_op jit(solution)/shard_map/dot_general | solution.py:964
  258.2 18.6 %all-gather.5.cloned.1.call-done = bf16[1024,1536]{1,0:T(8,128)(2,1)} async-done(((bf16[128,1536]{1,0:T(8,128)(2,1)}), bf16[1024,1536]{1,0:T(8,128)(2,1)}) %all-gather.5.cloned.1.call-update) | async-done | bytes 3145744 | tf_op jit(solution)/shard_map/all_gather | solution.py:919
  276.8 12.3 %multiply_convert_fusion.3 = (bf16[1024,1024]{1,0:T(8,128)(2,1)}, bf16[1024,1024]{1,0:T(8,128)(2,1)}, bf16[1024,1024]{1,0:T(8,128)(2,1)S(1)}) fusion(f32[1024,2048]{1,0:T(8,128)} %fusion.3, bf16[1024,1536]{1,0:T(8,128)(2,1)} %bitcast_select_fusion, bf16[1024,1536]{1,0:T(8,128)(2,1)} %all-gather.5.cloned.1.call-done), kind=kOutput, calls=%fused_computation.13 | convolution fusion | flops 3236954112 | bytes 20971520 | tf_op jit(solution)/shard_map/td,fd->tf/dot_general | solution.py:973
  305.4 9.0 %fusion.2 = f32[1024,1536]{1,0:T(8,128)S(1)} fusion(bf16[1536,2048]{1,0:T(8,128)(2,1)} %all-gather.3.cloned.1.call-done, bf16[1024,1024]{1,0:T(8,128)(2,1)S(1)} %copy-done.71, bf16[1024,1024]{1,0:T(8,128)(2,1)S(1)} %copy-done.69), kind=kOutput, calls=%fused_computation.30 | convolution fusion | flops 6450839552 | bytes 16777216 | tf_op jit(solution)/shard_map/tf,df->td/dot_general | solution.py:978
  335.6 8.8 %convolution_convert_fusion = bf16[1536,2048]{1,0:T(8,128)(2,1)} fusion(bf16[1024,1024]{1,0:T(8,128)(2,1)S(1)} %copy-done.72, bf16[1024,1024]{1,0:T(8,128)(2,1)S(1)} %copy-done.70, bf16[512,1536]{1,0:T(8,128)(2,1)S(1)} %copy-done.26, bf16[512,1536]{1,0:T(8,128)(2,1)S(1)} %copy-done.25), kind=kOutput, calls=%fused_computation | convolution fusion | flops 6460276736 | bytes 13631488 | tf_op jit(solution)/shard_map/td,tf->df/dot_general | solution.py:981
  344.5 19.9 %collective-permute-done.13 = bf16[256,1536]{1,0:T(8,128)(2,1)S(1)} collective-permute-done((bf16[256,1536]{1,0:T(8,128)(2,1)}, bf16[256,1536]{1,0:T(8,128)(2,1)S(1)}, u32[]{:S(2)}, u32[]{:S(2)}) %collective-permute-start.13) | collective-permute-done | bytes 786464 | tf_op jit(solution)/shard_map/ppermute | solution.py:817
  388.7 14.3 %attend_back.3 = (f32[1024,128]{1,0:T(8,128)}, f32[1024,128]{1,0:T(8,128)}, f32[1024,128]{1,0:T(8,128)}, bf16[1024,128]{1,0:T(8,128)(2,1)}, f32[1024,128]{1,0:T(...) custom-call(s32[1]{0:T(128)} %bitcast.2.far_ref, bf16[1024,128]{1,0:T(8,128)(2,1)} %get-tuple-element.82.qh_ref, ...), custom_call_target="tpu_custom_call" | custom-call | flops 30720000000 | bytes 8388608 | tf_op jit(solution)/shard_map/attend_back/pallas_call | solution.py:367
  405.6 14.5 %attend_back.4 = (f32[1024,128]{1,0:T(8,128)}, f32[1024,128]{1,0:T(8,128)}, f32[1024,128]{1,0:T(8,128)}, bf16[1024,128]{1,0:T(8,128)(2,1)}, f32[1024,128]{1,0:T(...) custom-call(s32[1]{0:T(128)} %bitcast.2.far_ref, bf16[1024,128]{1,0:T(8,128)(2,1)} %get-tuple-element.87.qh_ref, ...), custom_call_target="tpu_custom_call" | custom-call | flops 30720000000 | bytes 8388608 | tf_op jit(solution)/shard_map/attend_back/pallas_call | solution.py:367
  422.8 14.3 %attend_back.5 = (f32[1024,128]{1,0:T(8,128)}, f32[1024,128]{1,0:T(8,128)}, f32[1024,128]{1,0:T(8,128)}, bf16[1024,128]{1,0:T(8,128)(2,1)}, f32[1024,128]{1,0:T(...) custom-call(s32[1]{0:T(128)} %bitcast.2.far_ref, bf16[1024,128]{1,0:T(8,128)(2,1)} %get-tuple-element.92.qh_ref, ...), custom_call_target="tpu_custom_call" | custom-call | flops 30720000000 | bytes 8388608 | tf_op jit(solution)/shard_map/attend_back/pallas_call | solution.py:367
  439.8 14.6 %prep_back.3 = (bf16[1024,128]{1,0:T(8,128)(2,1)}, bf16[1024,128]{1,0:T(8,128)(2,1)}, bf16[1024,128]{1,0:T(8,128)(2,1)}, f32[1032,128]{1,0:T(8,128)}, f32[8,128]{1,0:T(8,128)}, /*index=5*/f32[8,128]{1,0:T(8,128)}) custom-call(bf16[1024,1536]{1,0:T(8,128)(2,1)} %copy-done.43, bf16[1024,1536]{1,0:T(8,128)(2,1)} %copy-done.43, bf16[1024,1536]{1,0:T(8,128)(2,1)} %copy-done.43, ...), custom_call_target="tpu_custom_call" | custom-call | flops 30720000000 | bytes 8388608 | tf_op jit(solution)/shard_map/prep_back/pallas_call | solution.py:390
  455.2 14.6 %prep_back.4 = (bf16[1024,128]{1,0:T(8,128)(2,1)}, bf16[1024,128]{1,0:T(8,128)(2,1)}, bf16[1024,128]{1,0:T(8,128)(2,1)}, f32[1032,128]{1,0:T(8,128)}, f32[8,128]{1,0:T(8,128)}, /*index=5*/f32[8,128]{1,0:T(8,128)}) custom-call(bf16[1024,1536]{1,0:T(8,128)(2,1)} %copy-done.43, bf16[1024,1536]{1,0:T(8,128)(2,1)} %copy-done.43, bf16[1024,1536]{1,0:T(8,128)(2,1)} %copy-done.43, ...), custom_call_target="tpu_custom_call" | custom-call | flops 30720000000 | bytes 8388608 | tf_op jit(solution)/shard_map/prep_back/pallas_call | solution.py:390
  472.5 15.2 %prep_back.5 = (bf16[1024,128]{1,0:T(8,128)(2,1)}, bf16[1024,128]{1,0:T(8,128)(2,1)}, bf16[1024,128]{1,0:T(8,128)(2,1)}, f32[1032,128]{1,0:T(8,128)}, f32[8,128]{1,0:T(8,128)}, /*index=5*/f32[8,128]{1,0:T(8,128)}) custom-call(bf16[1024,1536]{1,0:T(8,128)(2,1)} %copy-done.43, bf16[1024,1536]{1,0:T(8,128)(2,1)} %copy-done.43, bf16[1024,1536]{1,0:T(8,128)(2,1)} %copy-done.43, ...), custom_call_target="tpu_custom_call" | custom-call | flops 30720000000 | bytes 8388608 | tf_op jit(solution)/shard_map/prep_back/pallas_call | solution.py:390
  501.2 11.8 %fusion.40 = (bf16[1024,1536]{1,0:T(8,128)(2,1)}, bf16[1536]{0:T(1024)(128)(2,1)S(1)}) fusion(f32[1024]{0:T(1024)S(1)} %bitcast.152, bf16[4,256,1536]{2,1,0:T(8,128)(2,1)} %get-tuple-element.79, f32[1024,1536]{1,0:T(8,128)} %fusion.39, bf16[1024,1536]{1,0:T(8,128)(2,1)} %maximum_dynamic-update-slice_fusion, bf16[1536,1536]{1,0:T(8,128)(2,1)} %bitcast.156), kind=kOutput, calls=%fused_computation.141 | convolution fusion | flops 4841273856 | bytes 20454400 | tf_op jit(solution)/shard_map/tn,dn->td/dot_general | solution.py:1037
  527.6 18.5 %collective-permute-done.22 = bf16[1536,384]{1,0:T(8,128)(2,1)S(1)} collective-permute-done((bf16[1536,384]{1,0:T(8,128)(2,1)}, bf16[1536,384]{1,0:T(8,128)(2,1)S(1)}, u32[]{:S(2)}, u32[]{:S(2)}) %collective-permute-start.22) | collective-permute-done | bytes 1179680 | tf_op jit(solution)/shard_map/ppermute | solution.py:817
  549.8 98.2 %scatter_last.1 = (bf16[4,96,2048]{2,1,0:T(8,128)(2,1)}, bf16[4,96,2048]{2,1,0:T(8,128)(2,1)}, bf16[2,128,1536]{2,1,0:T(8,128)(2,1)}, f32[256,1536]{1,0:T(8,128)}) custom-call(bf16[8,192,2048]{2,1,0:T(8,128)(2,1)} %pad_maximum_fusion.p_ref, bf16[4,256,1536]{2,1,0:T(8,128)(2,1)} %bitcast.139, bf16[192,2048]{1,0:T(8,128)(2,1)} %reduce-scatter.3.cloned.1.call-done.gu_ref, ...), custom_call_target="tpu_custom_call" | custom-call | tf_op jit(solution)/shard_map/scatter_last/pallas_call | solution.py:799
  (339 shorter events, 223.4 us)
Async XLA Ops:
  7.2 238.9 %all-gather.3.cloned.1.call-start = ((), (), s32[]{:S(2)}) async-start(), calls=%async_computation.4 | async-start | bytes 7077888 | tf_op jit(solution)/shard_map/all_gather | solution.py:918
  19.5 81.3 %collective-permute-start.9 = (bf16[96,2048]{1,0:T(8,128)(2,1)}, bf16[96,2048]{1,0:T(8,128)(2,1)}, u32[]{:S(2)}, u32[]{:S(2)}) collective-permute-start(bf16[96,2048]{1,0:T(8,128)(2,1)} %bitcast.116), channel_id=1, source_target_pairs={{0,2},{2,0},{1,3},{3,1},{4,6},{6,4},{5,7},{7,5},{8,10},{10,8},{9,1... | collective-permute-start | bytes 1179656 | tf_op jit(solution)/shard_map/ppermute | solution.py:817
  111.4 16.6 %collective-permute-start = (bf16[8,384]{1,0:T(8,128)(2,1)S(1)}, bf16[8,384]{1,0:T(8,128)(2,1)S(1)}, u32[]{:S(2)}, u32[]{:S(2)}) collective-permute-start(bf16[8,384]{1,0:T(8,128)(2,1)S(1)} %slice.128), channel_id=1, source_target_pairs={{0,4},{1,5},{2,6},{3,7},{8,12},{9,13},{10,14},{11,15},{16,20},{17,... | collective-permute-start | bytes 18440 | tf_op jit(solution)/shard_map/ppermute | solution.py:823
  114.7 48.9 %collective-permute-start.2 = (bf16[1024,128]{1,0:T(8,128)(2,1)S(1)}, bf16[1024,128]{1,0:T(8,128)(2,1)}, u32[]{:S(2)}, u32[]{:S(2)}) collective-permute-start(bf16[1024,128]{1,0:T(8,128)(2,1)S(1)} %get-tuple-element.185), channel_id=1, source_target_pairs={{0,4},{1,5},{2,6},{3,7},{8,12},{9,13},{10,14},{11,15},{16,20},{17,... | collective-permute-start | bytes 786440 | tf_op jit(solution)/shard_map/ppermute | solution.py:823
  116.7 57.5 %collective-permute-start.4 = (bf16[1024,128]{1,0:T(8,128)(2,1)S(1)}, bf16[1024,128]{1,0:T(8,128)(2,1)}, u32[]{:S(2)}, u32[]{:S(2)}) collective-permute-start(bf16[1024,128]{1,0:T(8,128)(2,1)S(1)} %get-tuple-element.187), channel_id=1, source_target_pairs={{0,4},{1,5},{2,6},{3,7},{8,12},{9,13},{10,14},{11,15},{16,20},{17,... | collective-permute-start | bytes 786440 | tf_op jit(solution)/shard_map/ppermute | solution.py:823
  118.7 64.7 %collective-permute-start.6 = (bf16[1024,128]{1,0:T(8,128)(2,1)S(1)}, bf16[1024,128]{1,0:T(8,128)(2,1)}, u32[]{:S(2)}, u32[]{:S(2)}) collective-permute-start(bf16[1024,128]{1,0:T(8,128)(2,1)S(1)} %get-tuple-element.186), channel_id=1, source_target_pairs={{0,4},{1,5},{2,6},{3,7},{8,12},{9,13},{10,14},{11,15},{16,20},{17,... | collective-permute-start | bytes 786440 | tf_op jit(solution)/shard_map/ppermute | solution.py:823
  139.4 25.5 %collective-permute-start.1 = (bf16[1024,128]{1,0:T(8,128)(2,1)}, bf16[1024,128]{1,0:T(8,128)(2,1)S(1)}, u32[]{:S(2)}, u32[]{:S(2)}) collective-permute-start(bf16[1024,128]{1,0:T(8,128)(2,1)} %get-tuple-element.86), channel_id=1, source_target_pairs={{0,4},{1,5},{2,6},{3,7},{8,12},{9,13},{10,14},{11,15},{16,20},{17,... | collective-permute-start | bytes 786440 | tf_op jit(solution)/shard_map/ppermute | solution.py:823
  151.5 22.7 %collective-permute-start.3 = (bf16[1024,128]{1,0:T(8,128)(2,1)}, bf16[1024,128]{1,0:T(8,128)(2,1)S(1)}, u32[]{:S(2)}, u32[]{:S(2)}) collective-permute-start(bf16[1024,128]{1,0:T(8,128)(2,1)} %get-tuple-element.91), channel_id=1, source_target_pairs={{0,4},{1,5},{2,6},{3,7},{8,12},{9,13},{10,14},{11,15},{16,20},{17,... | collective-permute-start | bytes 786440 | tf_op jit(solution)/shard_map/ppermute | solution.py:823
  163.6 19.8 %collective-permute-start.5 = (bf16[1024,128]{1,0:T(8,128)(2,1)}, bf16[1024,128]{1,0:T(8,128)(2,1)S(1)}, u32[]{:S(2)}, u32[]{:S(2)}) collective-permute-start(bf16[1024,128]{1,0:T(8,128)(2,1)} %get-tuple-element.96), channel_id=1, source_target_pairs={{0,4},{1,5},{2,6},{3,7},{8,12},{9,13},{10,14},{11,15},{16,20},{17,... | collective-permute-start | bytes 786440 | tf_op jit(solution)/shard_map/ppermute | solution.py:823
  198.8 78.0 %all-gather.5.cloned.1.call-start = ((), (), s32[]{:S(2)}) async-start(), calls=%async_computation.5 | async-start | bytes 3538944 | tf_op jit(solution)/shard_map/all_gather | solution.py:919
  214.9 18.3 %collective-permute-start.7 = (bf16[256,1536]{1,0:T(8,128)(2,1)S(1)}, bf16[256,1536]{1,0:T(8,128)(2,1)S(1)}, u32[]{:S(2)}, u32[]{:S(2)}) collective-permute-start(bf16[256,1536]{1,0:T(8,128)(2,1)S(1)} %multiply_convert_fusion.5), channel_id=1, source_target_pairs={{0,1},{1,0},{2,3},{3,2},{4,5},{5,4},{6,7},{7,6},{8,9},{9,8},{10,11... | collective-permute-start | bytes 2359304 | tf_op jit(solution)/shard_map/ppermute | solution.py:817
  216.3 333.5 %reduce-scatter.5.cloned.1.call-start = ((), (), s32[]{:S(2)}) async-start(), calls=%async_computation.7 | async-start | bytes 3538944 | tf_op jit(solution)/shard_map/reduce_scatter | solution.py:982
  295.5 254.3 %reduce-scatter.3.cloned.1.call-start = ((), (), s32[]{:S(2)}) async-start(), calls=%async_computation.6 | async-start | bytes 7077888 | tf_op jit(solution)/shard_map/reduce_scatter | solution.py:983
  303.0 21.0 %collective-permute-start.10 = (bf16[512,1536]{1,0:T(8,128)(2,1)}, bf16[512,1536]{1,0:T(8,128)(2,1)}, u32[]{:S(2)}, u32[]{:S(2)}) collective-permute-start(bf16[512,1536]{1,0:T(8,128)(2,1)} %dynamic-slice_convert_fusion.2), channel_id=1, source_target_pairs={{0,2},{2,0},{1,3},{3,1},{4,6},{6,4},{5,7},{7,5},{8,10},{10,8},{9,1... | collective-permute-start | bytes 4718600 | tf_op jit(solution)/shard_map/ppermute | solution.py:817
  328.0 38.2 %collective-permute-start.11 = (bf16[256,1536]{1,0:T(8,128)(2,1)}, bf16[256,1536]{1,0:T(8,128)(2,1)}, u32[]{:S(2)}, u32[]{:S(2)}) collective-permute-start(bf16[256,1536]{1,0:T(8,128)(2,1)} %dynamic-slice_convert_fusion.5), channel_id=1, source_target_pairs={{0,1},{1,0},{2,3},{3,2},{4,5},{5,4},{6,7},{7,6},{8,9},{9,8},{10,11... | collective-permute-start | bytes 2359304 | tf_op jit(solution)/shard_map/ppermute | solution.py:817
  334.7 29.7 %collective-permute-start.13 = (bf16[256,1536]{1,0:T(8,128)(2,1)}, bf16[256,1536]{1,0:T(8,128)(2,1)S(1)}, u32[]{:S(2)}, u32[]{:S(2)}) collective-permute-start(bf16[256,1536]{1,0:T(8,128)(2,1)} %dynamic-slice_convert_fusion.4), channel_id=1, source_target_pairs={{0,1},{1,0},{2,3},{3,2},{4,5},{5,4},{6,7},{7,6},{8,9},{9,8},{10,11... | collective-permute-start | bytes 2359304 | tf_op jit(solution)/shard_map/ppermute | solution.py:817
  384.5 128.6 %collective-permute-start.21 = (bf16[1536,768]{1,0:T(8,128)(2,1)}, bf16[1536,768]{1,0:T(8,128)(2,1)}, u32[]{:S(2)}, u32[]{:S(2)}) collective-permute-start(bf16[1536,768]{1,0:T(8,128)(2,1)} %dynamic-slice_convert_fusion), channel_id=1, source_target_pairs={{0,2},{2,0},{1,3},{3,1},{4,6},{6,4},{5,7},{7,5},{8,10},{10,8},{9,1... | collective-permute-start | bytes 7077896 | tf_op jit(solution)/shard_map/ppermute | solution.py:817
  403.0 34.1 %collective-permute-start.14 = (bf16[1024,128]{1,0:T(8,128)(2,1)}, bf16[1024,128]{1,0:T(8,128)(2,1)S(1)}, u32[]{:S(2)}, u32[]{:S(2)}) collective-permute-start(bf16[1024,128]{1,0:T(8,128)(2,1)} %get-tuple-element.106), channel_id=1, source_target_pairs={{4,0},{5,1},{6,2},{7,3},{12,8},{13,9},{14,10},{15,11},{20,16},{21,... | collective-permute-start | bytes 786440 | tf_op jit(solution)/shard_map/ppermute | solution.py:823
  404.3 34.2 %collective-permute-start.15 = (bf16[1024,128]{1,0:T(8,128)(2,1)}, bf16[1024,128]{1,0:T(8,128)(2,1)S(1)}, u32[]{:S(2)}, u32[]{:S(2)}) collective-permute-start(bf16[1024,128]{1,0:T(8,128)(2,1)} %get-tuple-element.107), channel_id=1, source_target_pairs={{4,0},{5,1},{6,2},{7,3},{12,8},{13,9},{14,10},{15,11},{20,16},{21,... | collective-permute-start | bytes 786440 | tf_op jit(solution)/shard_map/ppermute | solution.py:823
  420.1 34.3 %collective-permute-start.16 = (bf16[1024,128]{1,0:T(8,128)(2,1)}, bf16[1024,128]{1,0:T(8,128)(2,1)S(1)}, u32[]{:S(2)}, u32[]{:S(2)}) collective-permute-start(bf16[1024,128]{1,0:T(8,128)(2,1)} %get-tuple-element.116), channel_id=1, source_target_pairs={{4,0},{5,1},{6,2},{7,3},{12,8},{13,9},{14,10},{15,11},{20,16},{21,... | collective-permute-start | bytes 786440 | tf_op jit(solution)/shard_map/ppermute | solution.py:823
  421.4 33.1 %collective-permute-start.17 = (bf16[1024,128]{1,0:T(8,128)(2,1)}, bf16[1024,128]{1,0:T(8,128)(2,1)S(1)}, u32[]{:S(2)}, u32[]{:S(2)}) collective-permute-start(bf16[1024,128]{1,0:T(8,128)(2,1)} %get-tuple-element.117), channel_id=1, source_target_pairs={{4,0},{5,1},{6,2},{7,3},{12,8},{13,9},{14,10},{15,11},{20,16},{21,... | collective-permute-start | bytes 786440 | tf_op jit(solution)/shard_map/ppermute | solution.py:823
  437.2 34.5 %collective-permute-start.18 = (bf16[1024,128]{1,0:T(8,128)(2,1)}, bf16[1024,128]{1,0:T(8,128)(2,1)S(1)}, u32[]{:S(2)}, u32[]{:S(2)}) collective-permute-start(bf16[1024,128]{1,0:T(8,128)(2,1)} %get-tuple-element.126), channel_id=1, source_target_pairs={{4,0},{5,1},{6,2},{7,3},{12,8},{13,9},{14,10},{15,11},{20,16},{21,... | collective-permute-start | bytes 786440 | tf_op jit(solution)/shard_map/ppermute | solution.py:823
  438.5 33.2 %collective-permute-start.19 = (bf16[1024,128]{1,0:T(8,128)(2,1)}, bf16[1024,128]{1,0:T(8,128)(2,1)S(1)}, u32[]{:S(2)}, u32[]{:S(2)}) collective-permute-start(bf16[1024,128]{1,0:T(8,128)(2,1)} %get-tuple-element.127), channel_id=1, source_target_pairs={{4,0},{5,1},{6,2},{7,3},{12,8},{13,9},{14,10},{15,11},{20,16},{21,... | collective-permute-start | bytes 786440 | tf_op jit(solution)/shard_map/ppermute | solution.py:823
  518.9 27.3 %collective-permute-start.22 = (bf16[1536,384]{1,0:T(8,128)(2,1)}, bf16[1536,384]{1,0:T(8,128)(2,1)S(1)}, u32[]{:S(2)}, u32[]{:S(2)}) collective-permute-start(bf16[1536,384]{1,0:T(8,128)(2,1)} %dynamic-slice_convert_fusion.3), channel_id=1, source_target_pairs={{0,1},{1,0},{2,3},{3,2},{4,5},{5,4},{6,7},{7,6},{8,9},{9,8},{10,11... | collective-permute-start | bytes 3538952 | tf_op jit(solution)/shard_map/ppermute | solution.py:817
  (85 other events, 822.9 us)
Sparse Core Ops, SparseCore 0:
  103.0 101.9 all-gather.2
  216.4 60.3 all-gather.4
  295.6 73.8 reduce-scatter.4
  373.0 128.4 reduce-scatter.2

commit v3 on v2

--- a/solution.py
+++ b/solution.py
@@ -170,7 +170,7 @@
 
 
 def attend_back_kernel(far_ref, qh_ref, kh_ref, p_ref, s_in_ref, v_ref, kr_ref, vr_ref, do_ref,
-                       dqh_ref, dkh_ref, dp_ref, ds_ref, dv_ref, dkr_ref, dvr_ref,
+                       dqh_ref, dkh_ref, dp_ref, ds_ref, dv_ref, dfar_ref,
                        q_ref, s_ref, save_ref, pl_ref, pr_ref, dsl_ref, dsr_ref, dq_ref):
     scale = CH ** -0.5
     far = far_ref[0]
@@ -203,8 +203,8 @@
     far_count = kr_ref.shape[0]
     for b in range(0, far_count, count):
         part = slice(b, b + count)
-        dvr_ref[part, :] = mm(pr_ref[:, part], do, 0, 0).astype(bf16)
-        dkr_ref[part, :] = mm(dsr_ref[:, part], q_ref[...], 0, 0).astype(bf16)
+        dfar_ref[1, part, :] = mm(pr_ref[:, part], do, 0, 0).astype(bf16)
+        dfar_ref[0, part, :] = mm(dsr_ref[:, part], q_ref[...], 0, 0).astype(bf16)
     dv_ref[...] = mm(pl_ref[...], do, 0, 0)
     for m in range(chunks):
         span = slice(m * CH, (m + 1) * CH)
@@ -225,7 +225,7 @@
 
 def prep_back_kernel(unroll, head, q_ref, k_ref, u_ref, rim_ref, kernel_ref, logits_ref,
                      w_ref, t_ref, kh_ref, p_ref, ds_ref, dqh_ref, dkh_ref, dp_ref, dv_ref,
-                     dkt_ref, dvt_ref,
+                     dfar_ref,
                      gq_ref, gk_ref, gv_ref, gu_ref, glog_ref, gker_ref,
                      ext_ref, mv_ref, save_ref, dk_ref, dps_ref, dw_ref, dc_ref):
     count = q_ref.shape[0]
@@ -238,7 +238,7 @@
         save_ref[m, rows, :] = cur
         if m < chunks - 1:
             mv_ref[rows, :] = mm(cur, p_ref[m * CH : (m + 1) * CH, :], 1, 1).astype(bf16)
-    dk_ref[...] = dkt_ref[...].astype(f32)
+    dk_ref[...] = dfar_ref[0].astype(f32)
     dps_ref[...] = dp_ref[...]
     for m in range(chunks - 1, 0, -1):
         rows = slice(0, m * CH)
@@ -247,7 +247,7 @@
         dps_ref[span, :] = dps_ref[span, :] + mm(d_new, save_ref[m, rows, :], 0, 0)
         dk_ref[rows, :] = mm(d_new, p_ref[span, :])
     dk_ref[...] = dk_ref[...] + dkh_ref[...]
-    gv_ref[...] = (dv_ref[...] + dvt_ref[...].astype(f32)).astype(bf16)
+    gv_ref[...] = (dv_ref[...] + dfar_ref[1].astype(f32)).astype(bf16)
     ones = jnp.ones((8, CH), f32)
 
     def chunk(start):
@@ -326,7 +326,7 @@
 def prep(projected, rim, kernel, logits, head, heads):
     count = projected.shape[0]
     sq = jax.ShapeDtypeStruct((count, CH), bf16)
-    unroll = 4
+    unroll = 8 if count % (8 * CH) == 0 else 4
     return pl.pallas_call(
         functools.partial(prep_kernel, unroll, head),
         grid=(1,),
@@ -348,7 +348,7 @@
         attend_kernel,
         grid=(1,),
         in_specs=[pl.BlockSpec(memory_space=pltpu.SMEM), c, c, c, c, column(count, 2 * heads + head),
-                  whole((fc, CH)), whole((fc, CH))],
+                  whole((fc, CH)), column(fc, head)],
         out_specs=c,
         out_shape=jax.ShapeDtypeStruct((count, CH), bf16),
         scratch_shapes=[pltpu.VMEM((count, CH), bf16), pltpu.VMEM((count, count), f32)],
@@ -363,14 +363,14 @@
     c = whole((count, CH))
     r = whole((fc, CH))
     w32 = jax.ShapeDtypeStruct((count, CH), f32)
-    far16 = jax.ShapeDtypeStruct((fc, CH), bf16)
+    far16 = jax.ShapeDtypeStruct((2, fc, CH), bf16)
     return pl.pallas_call(
         attend_back_kernel,
         grid=(1,),
         in_specs=[pl.BlockSpec(memory_space=pltpu.SMEM), c, c, c, c, column(count, 2 * heads + head),
-                  r, r, column(count, head)],
-        out_specs=[c, c, c, c, c, r, r],
-        out_shape=[w32, w32, w32, jax.ShapeDtypeStruct((count, CH), bf16), w32, far16, far16],
+                  r, column(fc, head), column(count, head)],
+        out_specs=[c, c, c, c, c, whole((2, fc, CH))],
+        out_shape=[w32, w32, w32, jax.ShapeDtypeStruct((count, CH), bf16), w32, far16],
         scratch_shapes=[pltpu.VMEM((count, CH), bf16), pltpu.VMEM((count, count), f32),
                         pltpu.VMEM((count // CH - 1, count, CH), bf16),
                         pltpu.VMEM((count, count), bf16), pltpu.VMEM((count, fc), bf16),
@@ -381,17 +381,17 @@
     )(far, qh, kh, p, s_in, projected, kr, vr, d_attn)
 
 
-def prep_back(projected, rim, kernel, logits, w, t, kh, p, ds, dqh, dkh, dp, dv, dkt, dvt, head, heads):
+def prep_back(projected, rim, kernel, logits, w, t, kh, p, ds, dqh, dkh, dp, dv, dfar, head, heads):
     count = projected.shape[0]
     c = whole((count, CH))
     sq = jax.ShapeDtypeStruct((count, CH), bf16)
     chunks = count // CH
-    unroll = 2
+    unroll = 8 if count % (8 * CH) == 0 else 2
     return pl.pallas_call(
         functools.partial(prep_back_kernel, unroll, head),
         grid=(1,),
         in_specs=[column(count, head), column(count, heads + head), column(count, 3 * heads + head),
-                  column(8, head), column(8, head), c] + [c] * 11,
+                  column(8, head), column(8, head), c] + [c] * 9 + [whole((2, count, CH))],
         out_specs=[c, c, c, whole((count + 8, CH)), whole((chunks, CH)), whole((8, CH))],
         out_shape=[sq, sq, sq, jax.ShapeDtypeStruct((count + 8, CH), f32),
                    jax.ShapeDtypeStruct((chunks, CH), f32), jax.ShapeDtypeStruct((8, CH), f32)],
@@ -401,7 +401,7 @@
                         pltpu.VMEM((count + 16, CH), f32)],
         compiler_params=params(), name="prep_back",
         cost_estimate=estimate(count * 3 * 10**7, count * 8192),
-    )(projected, projected, projected, rim, kernel, logits, w, t, kh, p, ds, dqh, dkh, dp, dv, dkt, dvt)
+    )(projected, projected, projected, rim, kernel, logits, w, t, kh, p, ds, dqh, dkh, dp, dv, dfar)
 
 
 MESH = pl.DeviceIdType.MESH
@@ -435,9 +435,9 @@
     return pltpu.make_async_remote_copy(source, target, send, recv, device_id=where, device_id_type=MESH)
 
 
-def gather_kernel(row_count, y_count, features, qkvu_ref, small_ref, out_w_ref, x_ref, g_ref,
-                  wide_ref, packed_ref, wo_ref, xs_ref, gs_ref,
-                  local_sem, cc_send, cc_recv, tok_send, tok_recv, up_send, down_send, z_recv, y_send, y_recv,
+def gather_kernel(row_count, y_count, features, part, qkvu_ref, small_ref, out_w_ref, x_ref, g_ref, gu_ref, dn_ref,
+                  wide_ref, packed_ref, wo_ref, xs_ref, gs_ref, pair_ref,
+                  dn_local, gu_local, gu_send, gu_recv, local_sem, cc_send, cc_recv, tok_send, tok_recv, up_send, down_send, z_recv, y_send, y_recv,
                   wo_y_send, wo_y_recv, wo_x_send, wo_x_recv, wo_c_send, wo_c_recv):
     r, y = lax.axis_index("row"), lax.axis_index("cy")
     c, q = lax.axis_index("cc"), lax.axis_index("seq")
@@ -463,6 +463,27 @@
     local.append(pltpu.make_async_copy(x_ref, xs_ref.at[t], local_sem.at[6]))
     local.append(pltpu.make_async_copy(g_ref, gs_ref.at[t], local_sem.at[7]))
 
+    blocks = gu_local.shape[0]
+    rows = gu_ref.shape[-2]
+
+    def gu_copies(block):
+        if blocks == 1:
+            mine, theirs, place = gu_ref.at[t], gu_ref.at[other_t], pair_ref.at[c]
+        else:
+            mine = gu_ref.at[:, pl.ds(pl.multiple_of((block * 4 + t) * part, part), part)]
+            theirs = gu_ref.at[:, pl.ds(pl.multiple_of((block * 4 + other_t) * part, part), part)]
+            place = pair_ref.at[pl.ds(pl.multiple_of((block * 2 + c) * rows, rows), rows)]
+        return (pltpu.make_async_copy(mine, place, gu_local.at[block]),
+                remote(theirs, place, gu_send.at[block], gu_recv.at[block], {"cc": 1 - c}))
+
+    down = []
+    if blocks > 1:
+        kept_rows = pl.ds(pl.multiple_of(q * part, part), part)
+        for block in range(width // part):
+            place = pair_ref.at[pl.ds(blocks * 2 * rows + block * part, part)]
+            down.append(pltpu.make_async_copy(
+                dn_ref.at[kept_rows, pl.ds(block * part, part)], place, dn_local.at[block]))
+
     def wo_y_copy(from_y, step):
         return remote(own_out, wo_ref.at[r, from_y, c, :, columns], wo_y_send.at[step], wo_y_recv.at[from_y],
                       {"cy": lax.rem(y + step, y_count)})
@@ -485,6 +506,11 @@
         ])
     tokens[0][0].start()
     tokens[0][1].start()
+    for block in range(blocks):
+        for copy in gu_copies(block):
+            copy.start()
+    for copy in down:
+        copy.start()
 
     def piece(kind, row, at_y):
         if kind == 0:
@@ -575,6 +601,11 @@
         relays[which].wait_send()
     local[6].wait()
     local[7].wait()
+    for block in range(blocks):
+        for copy in gu_copies(block):
+            copy.wait()
+    for copy in down:
+        copy.wait()
     for copy in cross:
         copy.wait_send()
     for step in range(1, y_count):
@@ -596,7 +627,7 @@
         wo_c_copy(origin).wait_send()
 
 
-def gather_first(qkvu, small, out_w, x, g, features):
+def gather_first(qkvu, small, out_w, x, g, gate_up, down, features, part):
     row_count, y_count = lax.axis_size("row"), lax.axis_size("cy")
     rows = qkvu.shape[0]
     width = out_w.shape[1]
@@ -604,32 +635,40 @@
     anywhere = pl.BlockSpec(memory_space=pl.ANY)
     dma = pltpu.SemaphoreType.DMA
     lead = (row_count, y_count, 2)
-    wide, packed, wo, xs, gs = pl.pallas_call(
-        functools.partial(gather_kernel, row_count, y_count, features),
-        in_specs=[vm] * 5,
-        out_specs=[anywhere] * 5,
+    blocks, cols = gate_up.shape[1] // (4 * part), gate_up.shape[1] // 4
+    if part % 128:
+        gate_up = gate_up.reshape(rows, blocks, 4, part).transpose(2, 0, 1, 3).reshape(4, rows, cols)
+        blocks = 1
+    lines = blocks * 2 * rows + down.shape[0] // 2 * (width // part)
+    pair_shape = (2, rows, cols) if blocks == 1 else (lines, part)
+    wide, packed, wo, xs, gs, pair = pl.pallas_call(
+        functools.partial(gather_kernel, row_count, y_count, features, part),
+        in_specs=[vm] * 7,
+        out_specs=[anywhere] * 6,
         out_shape=[
             jax.ShapeDtypeStruct(lead + (rows, 4 * features), bf16),
             jax.ShapeDtypeStruct(lead + small.shape, bf16),
             jax.ShapeDtypeStruct(lead + (rows, width), bf16),
             jax.ShapeDtypeStruct((4,) + x.shape, bf16),
             jax.ShapeDtypeStruct((4,) + g.shape, bf16),
+            jax.ShapeDtypeStruct(pair_shape, bf16),
         ],
-        scratch_shapes=[dma((8,)), dma((5,)), dma((5,)), dma((2, 3)), dma((2, 3)),
+        scratch_shapes=[dma((max(1, width // part),)), dma((blocks,)), dma((blocks,)), dma((blocks,)), dma((8,)), dma((5,)), dma((5,)), dma((2, 3)), dma((2, 3)),
                         dma((4, row_count)), dma((4, row_count)), dma((4, row_count)),
                         dma((4, row_count, y_count)), dma((4, row_count, y_count)),
                         dma((y_count,)), dma((y_count,))] + [dma((row_count,))] * 4,
         compiler_params=pltpu.CompilerParams(collective_id=1, has_side_effects=True, vmem_limit_bytes=48 * 1024 * 1024),
         name="gather_first",
-    )(qkvu, small, out_w, x, g)
+    )(qkvu, small, out_w, x, g, gate_up, down)
     total = row_count * y_count * 2 * rows
     return (wide.reshape(total, 4 * features), packed, wo.reshape(total, width),
-            xs.reshape(4 * x.shape[0], -1), gs.reshape(4 * g.shape[0], -1))
-
-
-def scatter_kernel(row_count, y_count, p_ref, dh_ref, gu_ref, dn_ref, res_ref, gu_res_ref, dn_res_ref, dh_res_ref,
-                   yin_ref, up_ref, down_ref, out_ref, dcc_ref, dst_ref, dseq_ref,
-                   y_send, y_recv, up_send, up_recv, down_send, down_recv, t_send, t_recv, n_send, n_recv,
+            xs.reshape(4 * x.shape[0], -1), gs.reshape(4 * g.shape[0], -1), pair)
+
+
+def scatter_kernel(row_count, y_count, features, part, p_ref, dh_ref, br_ref, gu_ref,
+                   qkvu_res_ref, rest_ref, gu_out_ref, dh_res_ref, br_res_ref,
+                   yin_ref, up_ref, down_ref, out_ref, res_ref, gu_res_ref, dcc_ref, dst_ref, dseq_ref,
+                   y_send, y_recv, up_send, up_recv, down_send, down_recv, t_send, t_recv,
                    dh_send, dh_recv, local_sem):
     r, y = lax.axis_index("row"), lax.axis_index("cy")
     c, q = lax.axis_index("cc"), lax.axis_index("seq")
@@ -638,24 +677,33 @@
     piece = 16 if depth % 16 == 0 else depth
     greet(r, row_count, y, y_count)
 
-    def y_copy(dest, step):
+    pieces = t_send.shape[0] - 1
+    cut = p_ref.shape[2] // pieces
+
+    def lanes(i):
+        return pl.ds(i * cut, cut)
+
+    def y_copy(i, dest, step):
         to = lax.rem(y + step, y_count)
-        return remote(p_ref.at[dest * y_count + to], yin_ref.at[dest, step - 1], y_send.at[dest, step - 1],
-                      y_recv.at[dest, step - 1], {"cy": to})
-
-    def z_copy(dest, step):
+        return remote(p_ref.at[dest * y_count + to, :, lanes(i)], yin_ref.at[dest, step - 1, :, lanes(i)],
+                      y_send.at[i, dest, step - 1], y_recv.at[i, dest, step - 1], {"cy": to})
+
+    def z_copy(i, dest, step):
         landing, sends, recvs = (up_ref, up_send, up_recv) if step > 0 else (down_ref, down_send, down_recv)
-        return remote(out_ref.at[dest], landing.at[dest], sends.at[dest], recvs.at[dest], {"row": r + step})
-
-    def add_up(dest, extra):
-        def body(i, carry):
-            rows = pl.ds(pl.multiple_of(i * piece, piece), piece)
-            total = p_ref[dest * y_count + y, rows].astype(f32)
+        return remote(out_ref.at[dest, :, lanes(i)], landing.at[dest, :, lanes(i)], sends.at[i, dest],
+                      recvs.at[i, dest], {"row": r + step})
+
+    def add_up(i, dest, extra):
+        span = slice(i * cut, (i + 1) * cut)
+
+        def body(at, carry):
+            rows = pl.ds(pl.multiple_of(at * piece, piece), piece)
+            total = p_ref[dest * y_count + y, rows, span].astype(f32)
             for step in range(1, y_count):
-                total = total + yin_ref[dest, step - 1, rows].astype(f32)
+                total = total + yin_ref[dest, step - 1, rows, span].astype(f32)
             for more in extra:
-                total = total + more[dest, rows].astype(f32)
-            out_ref[dest, rows] = total.astype(bf16)
+                total = total + more[dest, rows, span].astype(f32)
+            out_ref[dest, rows, span] = total.astype(bf16)
             return carry
 
         lax.fori_loop(0, depth // piece, body, 0)
@@ -664,41 +712,42 @@
     for k in range(row_count - 1, 0, -1):
         order += [(k, 1), (k, -1)]
 
-    def ordered(act):
+    def ordered(i, act):
         for k, step in order:
             dest = r + step * k
             valid = (dest < row_count) if step > 0 else (dest >= 0)
 
             @pl.when(valid)
             def _():
-                act(dest, step)
-
-    def start_y(dest, step):
+                act(i, dest, step)
+
+    def start_y(i, dest, step):
         for hop in range(1, y_count):
-            y_copy(dest, hop).start()
-
-    def forward(dest, step):
+            y_copy(i, dest, hop).start()
+
+    def forward(i, dest, step):
         for hop in range(1, y_count):
-            y_copy(dest, hop).wait_recv()
+            y_copy(i, dest, hop).wait_recv()
         landing = up_ref if step > 0 else down_ref
         inner = (r > 0) if step > 0 else (r < row_count - 1)
 
         @pl.when(inner)
         def _():
-            z_copy(dest, step).wait_recv()
-            add_up(dest, [landing])
+            z_copy(i, dest, step).wait_recv()
+            add_up(i, dest, [landing])
 
         @pl.when(jnp.logical_not(inner))
         def _():
-            add_up(dest, [])
-
-        z_copy(dest, step).start()
+            add_up(i, dest, [])
+
+        z_copy(i, dest, step).start()
 
     half = depth // 2
 
-    def t_copies(which, source, target):
-        own = source.at[pl.ds(pl.multiple_of(c * half, half), half)]
-        other = source.at[pl.ds(pl.multiple_of((1 - c) * half, half), half)]
+    def t_copies(which, source, target, span):
+        target = target.at[:, :, span]
+        own = source.at[pl.ds(pl.multiple_of(c * half, half), half), span]
+        other = source.at[pl.ds(pl.multiple_of((1 - c) * half, half), half), span]
         away = {"cc": 1 - c, "seq": 1 - q}
         pieces = ((own, {"seq": 1 - q}), (other, away), (other, {"cc": 1 - c}))
         return [
@@ -706,11 +755,19 @@
             for kind, (part, where) in enumerate(pieces)
         ], pltpu.make_async_copy(own, target.at[t], local_sem.at[which])
 
-    dh_cc = remote(dh_ref.at[pl.ds((1 - c) * 2, 2)], dcc_ref, dh_send.at[0], dh_recv.at[0], {"cc": 1 - c})
-    dh_seq = remote(dst_ref, dseq_ref, dh_send.at[1], dh_recv.at[1], {"seq": 1 - q})
-    dh_cc.start()
-    ordered(start_y)
-    start_y(r, 0)
+    sums = (dh_ref, br_ref)
+    cc_copies = [
+        remote(source.at[pl.ds((1 - c) * 2, 2)], dcc_ref.at[i], dh_send.at[i], dh_recv.at[i], {"cc": 1 - c})
+        for i, source in enumerate(sums)
+    ]
+    seq_copies = [
+        remote(dst_ref.at[i], dseq_ref.at[i], dh_send.at[2 + i], dh_recv.at[2 + i], {"seq": 1 - q}) for i in range(2)
+    ]
+    for copy in cc_copies:
+        copy.start()
+    for i in range(pieces):
+        ordered(i, start_y)
+        start_y(i, r, 0)
     tokens = dh_ref.shape[1]
     step_rows = 16 if tokens % 16 == 0 else tokens
 
@@ -721,96 +778,255 @@
 
         lax.fori_loop(0, tokens // step_rows, body, 0)
 
-    dh_cc.wait_recv()
-
-    def stage(rows):
-        dst_ref[rows] = (dh_ref[c * 2 + 1 - q, rows].astype(f32) + dcc_ref[1 - q, rows].astype(f32)).astype(bf16)
-
-    token_loop(stage)
-    gu_last, gu_local = t_copies(1, gu_ref, gu_res_ref)
-    dn_last = remote(dn_ref, dn_res_ref.at[q], n_send.at[0], n_recv.at[0], {"seq": 1 - q})
-    dn_local = pltpu.make_async_copy(dn_ref, dn_res_ref.at[q], local_sem.at[2])
+    for i, source in enumerate(sums):
+        cc_copies[i].wait_recv()
+
+        def stage(rows):
+            total = source[c * 2 + 1 - q, rows].astype(f32) + dcc_ref[i, 1 - q, rows].astype(f32)
+            dst_ref[i, rows] = total.astype(bf16)
+
+        token_loop(stage)
+    gu_last, gu_local = t_copies(pieces, gu_ref, gu_res_ref, pl.ds(0, gu_ref.shape[1]))
     gu_local.start()
-    dn_local.start()
-    dh_seq.start()
+    for copy in seq_copies:
+        copy.start()
     for copy in gu_last:
         copy.start()
-    dn_last.start()
-    ordered(forward)
-    dh_seq.wait_recv()
-
-    def settle(rows):
-        total = dh_ref[t, rows].astype(f32) + dcc_ref[q, rows].astype(f32)
-        dh_res_ref[rows] = total + dseq_ref[rows].astype(f32)
-
-    token_loop(settle)
-    for hop in range(1, y_count):
-        y_copy(r, hop).wait_recv()
-
-    @pl.when(r == 0)
-    def _():
-        z_copy(r, -1).wait_recv()
-        add_up(r, [down_ref])
-
-    @pl.when(r == row_count - 1)
-    def _():
-        z_copy(r, 1).wait_recv()
-        add_up(r, [up_ref])
-
-    @pl.when((r > 0) & (r < row_count - 1))
-    def _():
-        z_copy(r, 1).wait_recv()
-        z_copy(r, -1).wait_recv()
-        add_up(r, [up_ref, down_ref])
-
-    last, local = t_copies(0, out_ref.at[r], res_ref)
-    for copy in last:
-        copy.start()
-    local.start()
-
-    def sent(dest, step):
+
+    def finish_piece(i):
         for hop in range(1, y_count):
-            y_copy(dest, hop).wait_send()
-        z_copy(dest, step).wait_send()
-
-    ordered(sent)
-    for hop in range(1, y_count):
-        y_copy(r, hop).wait_send()
-    for copy in gu_last + [dn_last]:
+            y_copy(i, r, hop).wait_recv()
+
+        @pl.when(r == 0)
+        def _():
+            z_copy(i, r, -1).wait_recv()
+            add_up(i, r, [down_ref])
+
+        @pl.when(r == row_count - 1)
+        def _():
+            z_copy(i, r, 1).wait_recv()
+            add_up(i, r, [up_ref])
+
+        @pl.when((r > 0) & (r < row_count - 1))
+        def _():
+            z_copy(i, r, 1).wait_recv()
+            z_copy(i, r, -1).wait_recv()
+            add_up(i, r, [up_ref, down_ref])
+
+        last, local = t_copies(i, out_ref.at[r], res_ref, lanes(i))
+        for copy in last:
+            copy.start()
+        local.start()
+        return last + [local]
+
+    finals = []
+    for i in range(pieces - 1):
+        ordered(i, forward)
+        finals += finish_piece(i)
+    ordered(pieces - 1, forward)
+    for i, (source, result) in enumerate(((dh_ref, dh_res_ref), (br_ref, br_res_ref))):
+        seq_copies[i].wait_recv()
+
+        def settle(rows):
+            total = source[t, rows].astype(f32) + dcc_ref[i, q, rows].astype(f32)
+            result[rows] = total + dseq_ref[i, rows].astype(f32)
+
+        token_loop(settle)
+    for copy in gu_last:
+        copy.wait_recv()
+    gu_local.wait()
+    for quarter in range(4):
+        if part % 128:
+            gu_out_ref[quarter] = gu_res_ref[quarter]
+            continue
+        for block in range(gu_ref.shape[1] // part):
+            place = (block * 4 + quarter) * part
+            gu_out_ref[:, place : place + part] = gu_res_ref[quarter, :, block * part : (block + 1) * part]
+    finals += finish_piece(pieces - 1)
+
+    def sent(i, dest, step):
+        for hop in range(1, y_count):
+            y_copy(i, dest, hop).wait_send()
+        z_copy(i, dest, step).wait_send()
+
+    for i in range(pieces):
+        ordered(i, sent)
+        for hop in range(1, y_count):
+            y_copy(i, r, hop).wait_send()
+    for copy in gu_last + cc_copies + seq_copies:
+        copy.wait_send()
+    for copy in finals:
         copy.wait()
-    dh_cc.wait_send()
-    dh_seq.wait_send()
-    gu_local.wait()
-    dn_local.wait()
-    for copy in last:
-        copy.wait()
-    local.wait()
-
-
-def scatter_last(partial, d_h, gate_up_sum, down_sum):
+    for quarter in range(4):
+        for block in range(4):
+            place = block * 4 * features + quarter * features
+            qkvu_res_ref[:, place : place + features] = res_ref[quarter, :, block * features : (block + 1) * features]
+        rest_ref[quarter] = res_ref[quarter, :, 4 * features :]
+
+
+def scatter_last(partial, d_h, branch, gate_up_sum, features, part):
     row_count, y_count = lax.axis_size("row"), lax.axis_size("cy")
     total, cols = partial.shape
     depth = total // (row_count * y_count)
+    half = depth // 2
     tokens, width = d_h.shape[0] // 4, d_h.shape[1]
     vm = pl.BlockSpec(memory_space=pltpu.VMEM)
     dma = pltpu.SemaphoreType.DMA
     block = lambda *lead: pltpu.VMEM(lead + (depth, cols), bf16)
     shape = jax.ShapeDtypeStruct
+    gu_cols = gate_up_sum.shape[1]
+    pieces = 2
     return pl.pallas_call(
-        functools.partial(scatter_kernel, row_count, y_count),
+        functools.partial(scatter_kernel, row_count, y_count, features, part),
         in_specs=[vm] * 4,
-        out_specs=[vm] * 4,
-        out_shape=[shape((4, depth // 2, cols), bf16), shape((4, depth // 2, gate_up_sum.shape[1]), bf16),
-                   shape((2,) + down_sum.shape, bf16), shape((tokens, width), f32)],
+        out_specs=[vm] * 5,
+        out_shape=[shape((half, 16 * features), bf16), shape((4, half, cols - 4 * features), bf16),
+                   shape((4, half, gu_cols) if part % 128 else (half, 4 * gu_cols), bf16),
+                   shape((tokens, width), f32), shape((tokens, width), f32)],
         scratch_shapes=[block(row_count, y_count - 1), block(row_count), block(row_count), block(row_count),
-                        pltpu.VMEM((2, tokens, width), bf16), pltpu.VMEM((tokens, width), bf16),
-                        pltpu.VMEM((tokens, width), bf16),
-                        dma((row_count, y_count - 1)), dma((row_count, y_count - 1)), dma((row_count,)), dma((row_count,)),
-                        dma((row_count,)), dma((row_count,)), dma((2, 3)), dma((2, 3)), dma((1,)), dma((1,)),
-                        dma((2,)), dma((2,)), dma((3,))],
-        compiler_params=pltpu.CompilerParams(collective_id=2, has_side_effects=True, vmem_limit_bytes=56 * 1024 * 1024),
+                        pltpu.VMEM((4, half, cols), bf16), pltpu.VMEM((4, half, gu_cols), bf16),
+                        pltpu.VMEM((2, 2, tokens, width), bf16), pltpu.VMEM((2, tokens, width), bf16),
+                        pltpu.VMEM((2, tokens, width), bf16),
+                        dma((pieces, row_count, y_count - 1)), dma((pieces, row_count, y_count - 1))]
+                       + [dma((pieces, row_count))] * 4
+                       + [dma((pieces + 1, 3)), dma((pieces + 1, 3)), dma((4,)), dma((4,)), dma((pieces + 1,))],
+        compiler_params=pltpu.CompilerParams(collective_id=2, has_side_effects=True, vmem_limit_bytes=60 * 1024 * 1024),
         name="scatter_last",
-    )(partial.reshape(row_count * y_count, depth, cols), d_h.reshape(4, tokens, width), gate_up_sum, down_sum)
+    )(partial.reshape(row_count * y_count, depth, cols), d_h.reshape(4, tokens, width),
+      branch.reshape(4, tokens, width), gate_up_sum)
+
+
+def greet_group(c, q):
+    barrier = pltpu.get_barrier_semaphore()
+    for where in ({"cc": 1 - c}, {"seq": 1 - q}):
+        pl.semaphore_signal(barrier, inc=1, device_id=where, device_id_type=MESH)
+    pl.semaphore_wait(barrier, 2)
+
+
+def group_gather_kernel(x_ref, all_ref, send, recv, local_sem):
+    c, q = lax.axis_index("cc"), lax.axis_index("seq")
+    t = c * 2 + q
+    greet_group(c, q)
+    local = pltpu.make_async_copy(x_ref, all_ref.at[t], local_sem.at[0])
+    across = remote(x_ref, all_ref.at[t], send.at[0], recv.at[0], {"seq": 1 - q})
+    beside = remote(x_ref, all_ref.at[t], send.at[1], recv.at[1], {"cc": 1 - c})
+    across.start()
+    beside.start()
+    local.start()
+    across.wait_recv()
+    block = all_ref.at[c * 2 + 1 - q]
+    relay = remote(block, block, send.at[2], recv.at[2], {"cc": 1 - c})
+    relay.start()
+    local.wait()
+    across.wait_send()
+    beside.wait()
+    relay.wait()
+
+
+def group_gather(x):
+    dma = pltpu.SemaphoreType.DMA
+    gathered = pl.pallas_call(
+        group_gather_kernel,
+        in_specs=[pl.BlockSpec(memory_space=pltpu.VMEM)],
+        out_specs=pl.BlockSpec(memory_space=pltpu.VMEM),
+        out_shape=jax.ShapeDtypeStruct((4,) + x.shape, x.dtype),
+        scratch_shapes=[dma((3,)), dma((3,)), dma((1,))],
+        compiler_params=pltpu.CompilerParams(collective_id=3, has_side_effects=True, vmem_limit_bytes=16 * 1024 * 1024),
+        name="group_gather",
+    )(x)
+    return gathered.reshape(4 * x.shape[0], x.shape[1])
+
+
+def group_sum_kernel(p_ref, sum_ref, stage_ref, land_ref, out_ref, in_ref, send, recv):
+    c, q = lax.axis_index("cc"), lax.axis_index("seq")
+    tokens = p_ref.shape[1]
+    step_rows = 16 if tokens % 64 == 0 else tokens // 4
+    quarter = tokens // 4
+    greet_group(c, q)
+
+    def loop(begin, count, act):
+        def body(i, carry):
+            act(pl.ds(pl.multiple_of(begin + i * step_rows, step_rows), step_rows))
+            return carry
+
+        lax.fori_loop(0, count // step_rows, body, 0)
+
+    parts = [pl.ds(k * quarter, quarter) for k in range(4)]
+    beside = []
+    for side, which in ((1 - q, 0), (q, 1)):
+        for k in range(4):
+            def stage(rows):
+                stage_ref[side, rows] = p_ref[(1 - c) * 2 + side, rows].astype(bf16)
+
+            loop(k * quarter, quarter, stage)
+            copy = remote(stage_ref.at[side, parts[k]], land_ref.at[side, parts[k]],
+                          send.at[which, k], recv.at[which, k], {"cc": 1 - c})
+            copy.start()
+            beside.append(copy)
+    across = []
+    for k in range(4):
+        beside[k].wait_recv()
+
+        def pair(rows):
+            total = p_ref[c * 2 + 1 - q, rows] + land_ref[1 - q, rows].astype(f32)
+            out_ref[rows] = total.astype(bf16)
+
+        loop(k * quarter, quarter, pair)
+        copy = remote(out_ref.at[parts[k]], in_ref.at[parts[k]], send.at[2, k], recv.at[2, k], {"seq": 1 - q})
+        copy.start()
+        across.append(copy)
+    for k in range(4):
+        beside[4 + k].wait_recv()
+        across[k].wait_recv()
+
+        def settle(rows):
+            total = p_ref[c * 2 + q, rows] + land_ref[q, rows].astype(f32)
+            sum_ref[rows] = total + in_ref[rows].astype(f32)
+
+        loop(k * quarter, quarter, settle)
+    for copy in beside + across:
+        copy.wait_send()
+
+
+def group_sum(partial):
+    tokens, width = partial.shape[0] // 4, partial.shape[1]
+    dma = pltpu.SemaphoreType.DMA
+    return pl.pallas_call(
+        group_sum_kernel,
+        in_specs=[pl.BlockSpec(memory_space=pltpu.VMEM)],
+        out_specs=pl.BlockSpec(memory_space=pltpu.VMEM),
+        out_shape=jax.ShapeDtypeStruct((tokens, width), f32),
+        scratch_shapes=[pltpu.VMEM((2, tokens, width), bf16), pltpu.VMEM((2, tokens, width), bf16),
+                        pltpu.VMEM((tokens, width), bf16), pltpu.VMEM((tokens, width), bf16),
+                        dma((3, 4)), dma((3, 4))],
+        compiler_params=pltpu.CompilerParams(collective_id=4, has_side_effects=True, vmem_limit_bytes=32 * 1024 * 1024),
+        name="group_sum",
+    )(partial.reshape(4, tokens, width))
+
+
+def unpack_kernel(lines, both_ref, gate_up_ref, down_ref):
+    rows, part = gate_up_ref.shape[0], down_ref.shape[0]
+    lanes = both_ref.shape[2]
+    for block in range(lines // rows):
+        gate_up_ref[:, block * lanes : (block + 1) * lanes] = both_ref[0, block * rows : (block + 1) * rows]
+    for block in range(down_ref.shape[1] // lanes):
+        start = lines + block * part
+        down_ref[:, block * lanes : (block + 1) * lanes] = both_ref[0, start : start + part]
+
+
+def unpack(both, lines, rows, width):
+    count, total, lanes = both.shape
+    part = (total - lines) * lanes // width
+    cols = lines // rows * lanes
+    size = both.size * 4
+    return pl.pallas_call(
+        functools.partial(unpack_kernel, lines),
+        grid=(count,),
+        in_specs=[pl.BlockSpec((1, total, lanes), lambda i: (i, 0, 0))],
+        out_specs=[pl.BlockSpec((rows, cols), lambda i: (i, 0)), pl.BlockSpec((part, width), lambda i: (i, 0))],
+        out_shape=[jax.ShapeDtypeStruct((count * rows, cols), bf16), jax.ShapeDtypeStruct((count * part, width), bf16)],
+        compiler_params=params(), name="unpack", cost_estimate=estimate(0, size),
+    )(both)
 
 
 def swapped(value, axis):
@@ -830,24 +1046,7 @@
     )
 
 
-def gather_group(value):
-    pair = in_order(value, swapped(value, "seq"), lax.axis_index("seq"))
-    return in_order(pair, swapped(pair, "cc"), lax.axis_index("cc"))
-
-
-def reduce_group(partial):
-    half = partial.shape[0] // 2
-    cc, seq = lax.axis_index("cc"), lax.axis_index("seq")
-    mine = lax.dynamic_slice_in_dim(partial, cc * half, half, 0)
-    theirs = lax.dynamic_slice_in_dim(partial, (1 - cc) * half, half, 0).astype(bf16)
-    mine = mine + swapped(theirs, "cc").astype(f32)
-    quarter = half // 2
-    own = lax.dynamic_slice_in_dim(mine, seq * quarter, quarter, 0)
-    other = lax.dynamic_slice_in_dim(mine, (1 - seq) * quarter, quarter, 0).astype(bf16)
-    return own + swapped(other, "seq").astype(f32)
-
-
-def reduce_columns(partial):
+def halve_columns(partial):
     half = partial.shape[1] // 2
     cc, seq = lax.axis_index("cc"), lax.axis_index("seq")
     mine = lax.dynamic_slice_in_dim(partial, cc * half, half, 1)
@@ -856,7 +1055,7 @@
     quarter = half // 2
     own = lax.dynamic_slice_in_dim(mine, seq * quarter, quarter, 1)
     other = lax.dynamic_slice_in_dim(mine, (1 - seq) * quarter, quarter, 1).astype(bf16)
-    return own + swapped(other, "seq").astype(f32)
+    return own, other
 
 
 def rms_norm(values, gain):
@@ -868,18 +1067,6 @@
     for m in range(blocks.shape[0]):
         keys = lax.dot_general(keys, blocks[m], (((1,), (1,)), ((), ())), preferred_element_type=f32)
     return keys
-
-
-def column_share(shard, parts, group, axis):
-    cc, seq = lax.axis_index("cc"), lax.axis_index("seq")
-    pair = lax.axis_size("seq")
-    mine = lax.dynamic_index_in_dim(shard, cc * pair + seq, axis, keepdims=False)
-    theirs = lax.dynamic_index_in_dim(shard, (1 - cc) * pair + seq, axis, keepdims=False)
-    return mine, theirs
-
-
-def share_rows(mine, theirs):
-    return in_order(mine, swapped(theirs, "cc"), lax.axis_index("cc"))
 
 
 def per_device(
@@ -908,15 +1095,18 @@
 
     small = jnp.concatenate([norm_gain1[None], norm_gain2[None], conv_kernel, beta_weight.T], axis=0)
     small = jnp.pad(small, ((0, 32 - small.shape[0]), (0, CH - rows)))
-    wide_qkvu, packed, wide_out, span_input, span_grad = gather_first(
-        qkvu_weight, small, out_weight, own16, out_grad[0], features
+    wide_qkvu, packed, wide_out, span_input, span_grad, gate_up_pair = gather_first(
+        qkvu_weight, small, out_weight, own16, out_grad[0], gate_up_weight, down_weight, features, ff_part
     )
-    pairs = width // (2 * rows)
-    mine, theirs = column_share(gate_up_weight.reshape(rows, 2, pairs, group, ff_part), 2, group, 3)
-    gate_up_pair = share_rows(mine.reshape(rows, -1), theirs.reshape(rows, -1))
-    down_own = lax.dynamic_slice_in_dim(down_weight, seq * ff_part, ff_part, 0)
-    wide_gate_up = lax.all_gather(gate_up_pair, all_axes, axis=0, tiled=True)
-    wide_down = lax.all_gather(down_own, all_axes, axis=0, tiled=True)
+    if ff_part % CH:
+        down_own = lax.dynamic_slice_in_dim(down_weight, seq * ff_part, ff_part, 0)
+        wide_gate_up = lax.all_gather(gate_up_pair.reshape(2 * rows, -1), all_axes, axis=0, tiled=True)
+        wide_down = lax.all_gather(down_own, all_axes, axis=0, tiled=True)
+    else:
+        lines = 2 * rows * gate_up_weight.shape[1] // (group * ff_part)
+        both = lax.all_gather(gate_up_pair, all_axes, axis=0, tiled=False)
+        both = both.reshape(-1, *gate_up_pair.shape)
+        wide_gate_up, wide_down = unpack(both, lines, 2 * rows, width)
 
     packed = packed[..., :rows].transpose(3, 0, 1, 2, 4).reshape(packed.shape[3], width)
     gain_one = packed[0].astype(f32)
@@ -933,48 +1123,50 @@
     rim = passed_along(projected[span - 8 :, 3 * features :], "cy", 1)
     far = jnp.reshape(cy * span, (1,)).astype(jnp.int32)
 
+    values = projected[:, 2 * features : 3 * features]
+    value_hops = []
+    for hop in range(1, cy_size):
+        values = passed_along(values, "cy", 1)
+        value_hops.append(values)
+    far_values = jnp.concatenate(value_hops, 0)
     prepared, kept = [], []
     for head in range(local):
         prepared.append(prep(projected, rim, kernel, logits, head, local))
     for head in range(local):
         transforms = prepared[head][4]
         keys = prepared[head][6]
-        values = projected[:, (2 * local + head) * CH : (2 * local + head + 1) * CH]
         hops = []
         for hop in range(1, cy_size):
             keys = passed_along(keys, "cy", 1)
-            values = passed_along(values, "cy", 1)
-            hops.append((keys, values))
+            hops.append(keys)
             if hop < cy_size - 1:
                 keys = move_keys(keys.astype(f32), transforms.astype(f32)).astype(bf16)
         kept.append(hops)
-    far_keys = [jnp.concatenate([k for k, _ in hops], 0) for hops in kept]
-    far_values = [jnp.concatenate([v for _, v in hops], 0) for hops in kept]
+    far_keys = [jnp.concatenate(hops, 0) for hops in kept]
     attn = []
     for head in range(local):
         _, _, qh, kh, p, s_in, _ = prepared[head]
         attn.append(
-            attend(far, qh, kh, p, s_in, projected, far_keys[head], far_values[head], head, local)
+            attend(far, qh, kh, p, s_in, projected, far_keys[head], far_values, head, local)
         )
     attn = jnp.concatenate(attn, axis=1)
     back = lax.all_to_all(attn, ("cc", "seq"), split_axis=0, concat_axis=1, tiled=True)
     tokens = own16.astype(f32)
     x_mid = tokens + jnp.dot(back, wide_out, preferred_element_type=f32)
-    h_second = gather_group(rms_norm(x_mid, gain_two).astype(bf16))
+    h_second = group_gather(rms_norm(x_mid, gain_two).astype(bf16))
     gate_up = jnp.dot(h_second, wide_gate_up, preferred_element_type=f32)
     hidden_count = wide_down.shape[0]
     gate_part, up_part = gate_up[:, :hidden_count], gate_up[:, hidden_count:]
     sigmoid_gate = jax.nn.sigmoid(gate_part)
     silu_gate = gate_part * sigmoid_gate
     hidden = (silu_gate * up_part).astype(bf16)
-    branch = reduce_group(jnp.dot(hidden, wide_down, preferred_element_type=f32))
-    layer_output = jnp.where(valid, x_mid + branch, 0.0).astype(bf16)[None]
+    branch = jnp.dot(hidden, wide_down, preferred_element_type=f32)
 
     d_hidden = jnp.einsum("td,fd->tf", span_grad, wide_down, preferred_element_type=f32)
     d_gate = d_hidden * up_part * sigmoid_gate * (1.0 + gate_part * (1.0 - sigmoid_gate))
     d_up = d_hidden * silu_gate
     d_gate_up = jnp.concatenate([d_gate, d_up], axis=1).astype(bf16)
-    d_h_second = reduce_group(
+    d_h_second = group_sum(
         jnp.einsum("tf,df->td", d_gate_up, wide_gate_up, preferred_element_type=f32)
     )
     down_term = jnp.einsum("tf,td->fd", hidden, span_grad, preferred_element_type=f32)
@@ -987,38 +1179,41 @@
     d_mid = grad_rows + mid_norm_grad
     d_branch = d_mid.astype(bf16)
     out_term = jnp.einsum("td,te->de", back, d_branch, preferred_element_type=f32)
-    out_part = reduce_columns(out_term)
+    own_part, other_part = halve_columns(out_term)
     d_back = jnp.einsum("te,de->td", d_branch, wide_out, preferred_element_type=f32).astype(bf16)
     d_attn = lax.all_to_all(d_back, ("cc", "seq"), split_axis=1, concat_axis=0, tiled=True)
+    d_attn, other_part = lax.optimization_barrier((d_attn, other_part))
+    out_part = own_part + swapped(other_part, "seq").astype(f32)
 
     backs = []
     for head in range(local):
         _, _, qh, kh, p, s_in, _ = prepared[head]
         backs.append(
             attend_back(
-                far, qh, kh, p, s_in, projected, far_keys[head], far_values[head], d_attn, head, local
+                far, qh, kh, p, s_in, projected, far_keys[head], far_values, d_attn, head, local
             )
         )
-    pieces, logit_rows, kernel_rows, rims = [], [], [], []
+    first, out_part = lax.optimization_barrier((backs[-1][0], out_part))
+    backs[-1] = [first] + list(backs[-1][1:])
+    pieces, logit_rows, kernel_rows = [], [], []
+    down_both = in_order(down_sum, swapped(down_sum, "seq"), seq)
     for head in range(local):
         w, t, _, kh, p, _, _ = prepared[head]
-        dqh, dkh, dp, ds, dv, dkr, dvr = backs[head]
+        dqh, dkh, dp, ds, dv, dfars = backs[head]
         outgoing = None
         for hop in reversed(range(1, cy_size)):
-            part = slice((hop - 1) * span, hop * span)
-            d_keys, d_values = dkr[part], dvr[part]
+            d_both = dfars[:, (hop - 1) * span : hop * span]
             if outgoing is not None:
-                incoming = [passed_along(value, "cy", -1) for value in outgoing]
-                received = kept[head][hop - 1][0].astype(f32)
+                incoming = passed_along(outgoing, "cy", -1).astype(f32)
+                received = kept[head][hop - 1].astype(f32)
                 _, pull = jax.vjp(move_keys, received, p.astype(f32))
-                extra, d_transform = pull(incoming[0].astype(f32))
-                d_keys = (d_keys.astype(f32) + extra).astype(bf16)
-                d_values = (d_values.astype(f32) + incoming[1].astype(f32)).astype(bf16)
+                extra, d_transform = pull(incoming[0])
+                d_both = (d_both.astype(f32) + jnp.stack([extra, incoming[1]])).astype(bf16)
                 dp = dp + d_transform
-            outgoing = (d_keys, d_values)
-        dkt, dvt = [passed_along(value, "cy", -1) for value in outgoing]
+            outgoing = d_both
+        dfar = passed_along(outgoing, "cy", -1)
         gq, gk, gv, gu, glog, gker = prep_back(
-            projected, rim, kernel, logits, w, t, kh, p, ds, dqh, dkh, dp, dv, dkt, dvt, head, local
+            projected, rim, kernel, logits, w, t, kh, p, ds, dqh, dkh, dp, dv, dfar, head, local
         )
         pieces.append((gq, gk, gv, gu))
         logit_rows.append(glog.reshape(1, span))
@@ -1050,19 +1245,20 @@
     )
     used = small_term.shape[1]
     small_term = jnp.pad(small_term, ((0, 0), (0, CH - used)))
-    last, last_gate_up, last_down, d_h_first = scatter_last(
+    qkvu_grad, rest, gate_up_grad, d_h_first, branch = scatter_last(
         jnp.concatenate([qkvu_term, small_term, out_part], axis=1).astype(bf16),
-        d_h_first.astype(bf16), gate_up_sum, down_sum,
+        d_h_first.astype(bf16), branch.astype(bf16), gate_up_sum, features, ff_part,
     )
+    layer_output = jnp.where(valid, x_mid + branch, 0.0).astype(bf16)[None]
     _, pull_first = jax.vjp(rms_norm, tokens, gain_one)
     input_grad = (d_mid + pull_first(d_h_first)[0]).astype(bf16)[None]
-    qkvu_grad = last[:, :, : 4 * features].reshape(group, rows, 4, features).transpose(1, 2, 0, 3)
-    qkvu_grad = qkvu_grad.reshape(rows, 4 * width).astype(f32)
-    small_grad = jnp.sum(last[:, :, 4 * features : 4 * features + CH].astype(f32), 0)
-    out_grad_own = last[:, :, 4 * features + CH :].transpose(1, 0, 2).reshape(rows, width).astype(f32)
-    gate_up_grad = last_gate_up.reshape(group, rows, 2, pairs, ff_part).transpose(1, 2, 3, 0, 4)
-    gate_up_grad = gate_up_grad.reshape(rows, -1).astype(f32)
-    down_grad = last_down.reshape(ff_rows, width).astype(f32)
+    qkvu_grad = qkvu_grad.astype(f32)
+    if ff_part % CH:
+        gate_up_grad = gate_up_grad.reshape(group, rows, -1, ff_part).transpose(1, 2, 0, 3).reshape(rows, -1)
+    gate_up_grad = gate_up_grad.astype(f32)
+    small_grad = jnp.sum(rest[:, :, :CH].astype(f32), 0)
+    out_grad_own = jnp.concatenate([rest[i, :, CH:] for i in range(group)], axis=1).astype(f32)
+    down_grad = down_both.astype(f32)
     return (
         layer_output,
         input_grad,

time: 701 us -> 617 us (0.88)
  waiting for transfers between devices: 79.5 us -> 27.7 us
  Pallas kernels: 321 us -> 362 us
  local copies, waits for them, and re-layouts: 80.5 us -> 55.5 us
  starting transfers between devices: 49.4 us -> 26.7 us
  other arithmetic: 53.1 us -> 37 us
    pallas_call x1 -> x4, Pallas kernels: 98.2 us -> 147 us  [the longest x1 92.3 us: scatter_last(): pl.pallas_call(functools.partial(scatter_kernel, row_count, y_count, feat...]
    ppermute x9 -> x3, waiting for transfers between devices: 46.9 us -> 4.19 us  [swapped(): return lax.ppermute(value, axis, [(0, 1), (1, 0)])]
    convert_element_type x12 -> x2, local copies, waits for them, and re-layouts: 27.5 us -> 1.85 us  [the longest x1 1.72 us: halve_columns(): lax.dynamic_slice_in_dim(partial, (1 - cc) * half, half, 1).astype(bf16)]
    reduce_scatter x1, starting transfers between devices: 8.47 us -> 0.01 us  [per_device(): lax.psum_scatter(down_term.astype(bf16), all_axes, scatter_dimension=0, t...]
    dynamic_slice x2 -> x0, local copies, waits for them, and re-layouts: 8.16 us -> none  [the longest x1 7.39 us: column_share(): lax.dynamic_index_in_dim(shard, cc * pair + seq, axis, keepdims=False)]
    unnamed x176 -> x148, local copies, waits for them, and re-layouts: 25.9 us -> 33.9 us
    ppermute x9 -> x3, starting transfers between devices: 9.54 us -> 2.16 us  [swapped(): return lax.ppermute(value, axis, [(0, 1), (1, 0)])]
    ppermute x14 -> x9, starting transfers between devices: 22.7 us -> 16.1 us  [passed_along(): lax.ppermute(value, axis, [(source, source + steps) for source in range(l...]
  transfers between devices with their start and end apart: 29 -> 17, of which waited for: 6 -> 3; matrix products, arithmetic and copies ran while one was open for 20% -> 20% of each run, Pallas kernels for 32% -> 29%
where the time goes in v3:
time: 617 us; the launch traced here: 610 us
  Pallas kernels  362 us (59%)
  matrix products  86 us (14%)
  local copies, waits for them, and re-layouts  55.5 us (9%)
  other arithmetic  37 us (6%)
  waiting for transfers between devices  27.7 us (4%)
  starting transfers between devices  26.7 us (4%)
  between operations  15.5 us (3%)
    pallas_call x1, Pallas kernels, scatter_last(): pl.pallas_call(functools.partial(scatter_kernel, row_count, y_count, feat...  92.3 us
    pallas_call x1, Pallas kernels, gather_first(): pl.pallas_call(functools.partial(gather_kernel, row_count, y_count, featu...  79.6 us
    pallas_call x3, Pallas kernels, attend_back(): pl.pallas_call(attend_back_kernel, grid=(1,), in_specs=[pl.BlockSpec(memo...  43.2 us
    pallas_call x3, Pallas kernels, prep_back(): pl.pallas_call(functools.partial(prep_back_kernel, unroll, head), grid=(1...  40.7 us
    unnamed x148, local copies, waits for them, and re-layouts  33.9 us
    pallas_call x3, Pallas kernels, prep(): pl.pallas_call(functools.partial(prep_kernel, unroll, head), grid=(1,), i...  25.8 us
    pallas_call x3, Pallas kernels, attend(): pl.pallas_call(attend_kernel, grid=(1,), in_specs=[pl.BlockSpec(memory_sp...  25.7 us
    pallas_call x1, Pallas kernels, group_sum(): pl.pallas_call(group_sum_kernel, in_specs=[pl.BlockSpec(memory_space=pltp...  22.4 us
  transfers between devices with their start and end apart: 17, of which 3 were waited for; matrix products, arithmetic and copies ran while one was open for 20% of the time, Pallas kernels for 29%

profile of v3, /device:TPU:1, one launch (start us, length us, event | category | flops | bytes accessed | tf_op | source)
XLA Modules:
  0.0 610.2 jit_solution(2430114581573597619)
XLA Ops:
  13.6 79.6 %gather_first.1 = (bf16[4,2,2,96,1536]{4,3,2,1,0:T(8,128)(2,1)}, bf16[4,2,2,32,128]{4,3,2,1,0:T(8,128)(2,1)S(1)}, bf16[4,2,2,96,1536]{4,3,2,1,0:T(8,128)(2,1)}, ...) custom-call(bf16[96,6144]{1,0:T(8,128)(2,1)S(1)} %copy-done.5, ...), custom_call_target="tpu_custom_call" | custom-call | tf_op jit(solution)/shard_map/gather_first/pallas_call | solution.py:644
  117.4 8.6 %prep.3 = (bf16[1024,128]{1,0:T(8,128)(2,1)}, bf16[1024,128]{1,0:T(8,128)(2,1)}, bf16[1024,128]{1,0:T(8,128)(2,1)}, bf16[1024,128]{1,0:T(8,128)(2,1)}, bf16[1024...) custom-call(bf16[1024,1536]{1,0:T(8,128)(2,1)} %copy-done.39, bf16[1024,1536]{1,0:T(8,128)(2,1)} %copy-done.39, ...), custom_call_target="tpu_custom_call" | custom-call | flops 10240000000 | bytes 4194304 | tf_op jit(solution)/shard_map/prep/pallas_call | solution.py:330
  127.2 8.6 %prep.4 = (bf16[1024,128]{1,0:T(8,128)(2,1)}, bf16[1024,128]{1,0:T(8,128)(2,1)}, bf16[1024,128]{1,0:T(8,128)(2,1)}, bf16[1024,128]{1,0:T(8,128)(2,1)}, bf16[1024...) custom-call(bf16[1024,1536]{1,0:T(8,128)(2,1)} %copy-done.39, bf16[1024,1536]{1,0:T(8,128)(2,1)} %copy-done.39, ...), custom_call_target="tpu_custom_call" | custom-call | flops 10240000000 | bytes 4194304 | tf_op jit(solution)/shard_map/prep/pallas_call | solution.py:330
  137.3 8.6 %prep.5 = (bf16[1024,128]{1,0:T(8,128)(2,1)}, bf16[1024,128]{1,0:T(8,128)(2,1)}, bf16[1024,128]{1,0:T(8,128)(2,1)}, bf16[1024,128]{1,0:T(8,128)(2,1)}, bf16[1024...) custom-call(bf16[1024,1536]{1,0:T(8,128)(2,1)} %copy-done.39, bf16[1024,1536]{1,0:T(8,128)(2,1)} %copy-done.39, ...), custom_call_target="tpu_custom_call" | custom-call | flops 10240000000 | bytes 4194304 | tf_op jit(solution)/shard_map/prep/pallas_call | solution.py:330
  147.9 8.5 %attend.3 = bf16[1024,128]{1,0:T(8,128)(2,1)} custom-call(s32[1]{0:T(128)} %bitcast.2.far_ref, bf16[1024,128]{1,0:T(8,128)(2,1)} %get-tuple-element.87.qh_ref, bf16[1024,128]{1,0:T(8,128)(2,1)} %get-tuple-element.88.kh_ref, bf16[1024,128]{1,0:T(8,128)(2,1)} %get-tuple-element.89.p_ref, f32[1024,128]{1,0:T(8,128)} %get-tuple-element.90.s_in_ref, ...), custom_call_target="tpu_custom_call" | custom-call | flops 10240000000 | bytes 4194304 | tf_op jit(solution)/shard_map/attend/pallas_call | solution.py:347
  157.1 8.6 %attend.4 = bf16[1024,128]{1,0:T(8,128)(2,1)} custom-call(s32[1]{0:T(128)} %bitcast.2.far_ref, bf16[1024,128]{1,0:T(8,128)(2,1)} %get-tuple-element.92.qh_ref, bf16[1024,128]{1,0:T(8,128)(2,1)} %get-tuple-element.93.kh_ref, bf16[1024,128]{1,0:T(8,128)(2,1)} %get-tuple-element.94.p_ref, f32[1024,128]{1,0:T(8,128)} %get-tuple-element.95.s_in_ref, ...), custom_call_target="tpu_custom_call" | custom-call | flops 10240000000 | bytes 4194304 | tf_op jit(solution)/shard_map/attend/pallas_call | solution.py:347
  166.4 8.6 %attend.5 = bf16[1024,128]{1,0:T(8,128)(2,1)} custom-call(s32[1]{0:T(128)} %bitcast.2.far_ref, bf16[1024,128]{1,0:T(8,128)(2,1)} %get-tuple-element.97.qh_ref, bf16[1024,128]{1,0:T(8,128)(2,1)} %get-tuple-element.98.kh_ref, bf16[1024,128]{1,0:T(8,128)(2,1)} %get-tuple-element.99.p_ref, f32[1024,128]{1,0:T(8,128)} %get-tuple-element.100.s_in_ref, ...), custom_call_target="tpu_custom_call" | custom-call | flops 10240000000 | bytes 4194304 | tf_op jit(solution)/shard_map/attend/pallas_call | solution.py:347
  197.1 21.8 %group_gather.1 = bf16[4,256,1536]{2,1,0:T(8,128)(2,1)S(1)} custom-call(bf16[256,1536]{1,0:T(8,128)(2,1)S(1)} %multiply_convert_fusion.5.x_ref), custom_call_target="tpu_custom_call" | custom-call | tf_op jit(solution)/shard_map/group_gather/pallas_call | solution.py:928
  219.0 16.5 %all-gather.3.cloned.1.call-done = bf16[36864,128]{1,0:T(8,128)(2,1)} async-done(((bf16[4608,128]{1,0:T(8,128)(2,1)}), bf16[36864,128]{1,0:T(8,128)(2,1)}) %all-gather.3.cloned.1.call-update) | async-done | bytes 9437200 | tf_op jit(solution)/shard_map/all_gather | solution.py:1107
  235.5 10.3 %unpack.1 = (bf16[1536,2048]{1,0:T(8,128)(2,1)}, bf16[1024,1536]{1,0:T(8,128)(2,1)}) custom-call(bf16[8,4608,128]{2,1,0:T(8,128)(2,1)} %bitcast.125), custom_call_target="tpu_custom_call" | custom-call | bytes 18874368 | tf_op jit(solution)/shard_map/unpack/pallas_call | solution.py:1022
  245.8 9.0 %fusion.39 = f32[1024,2048]{0,1:T(8,128)S(1)} fusion(bf16[1024,1536]{1,0:T(8,128)(2,1)S(1)} %bitcast.111, bf16[1536,2048]{1,0:T(8,128)(2,1)} %get-tuple-element.108), kind=kOutput, calls=%fused_computation.126 | convolution fusion | flops 6442450944 | bytes 17825792 | tf_op jit(solution)/shard_map/dot_general | solution.py:1157
  272.1 10.5 %fusion.2 = f32[1024,1536]{1,0:T(8,128)S(1)} fusion(bf16[1536,2048]{1,0:T(8,128)(2,1)} %get-tuple-element.108, bf16[1024,1024]{0,1:T(8,128)(2,1)} %get-tuple-element.187, bf16[1024,1024]{0,1:T(8,128)(2,1)} %get-tuple-element.186), kind=kOutput, calls=%fused_computation.26 | convolution fusion | flops 6450839552 | bytes 16777216 | tf_op jit(solution)/shard_map/tf,df->td/dot_general | solution.py:1170
  282.6 22.4 %group_sum.1 = f32[256,1536]{1,0:T(8,128)S(1)} custom-call(f32[4,256,1536]{2,1,0:T(8,128)S(1)} %bitcast.110), custom_call_target="tpu_custom_call" | custom-call | tf_op jit(solution)/shard_map/group_sum/pallas_call | solution.py:994
  318.9 10.9 %convolution_convert_fusion = bf16[1536,2048]{1,0:T(8,128)(2,1)} fusion(bf16[1024,1536]{1,0:T(8,128)(2,1)S(1)} %bitcast.112, bf16[1024,1024]{0,1:T(8,128)(2,1)} %get-tuple-element.187, bf16[1024,1024]{0,1:T(8,128)(2,1)} %get-tuple-element.186), kind=kOutput, calls=%fused_computation | convolution fusion | flops 6453985280 | bytes 13631488 | tf_op jit(solution)/shard_map/td,tf->df/dot_general | solution.py:1173
  331.3 6.9 %convolution_convert_fusion.4 = bf16[1024,1536]{1,0:T(8,128)(2,1)} fusion(bf16[1024,1024]{0,1:T(8,128)(2,1)S(1)} %copy-done.59, bf16[1024,1536]{1,0:T(8,128)(2,1)} %get-tuple-element.107), kind=kOutput, calls=%fused_computation.19 | convolution fusion | flops 3222798336 | bytes 8388608 | tf_op jit(solution)/shard_map/dot_general | solution.py:1163
  343.1 14.3 %attend_back.3 = (f32[1024,128]{1,0:T(8,128)}, f32[1024,128]{1,0:T(8,128)}, f32[1024,128]{1,0:T(8,128)}, bf16[1024,128]{1,0:T(8,128)(2,1)}, f32[1024,128]{1,0:T(8,128)}, /*index=5*/bf16[2,1024,128]{2,1,0:T(8,128)(2,1)}) custom-call(s32[1]{0:T(128)} %bitcast.2.far_ref, bf16[1024,128]{1,0:T(8,128)(2,1)} %get-tuple-element.87.qh_ref, ...), custom_call_target="tpu_custom_call" | custom-call | flops 30720000000 | bytes 8388608 | tf_op jit(solution)/shard_map/attend_back/pallas_call | solution.py:367
  358.8 14.5 %attend_back.4 = (f32[1024,128]{1,0:T(8,128)}, f32[1024,128]{1,0:T(8,128)}, f32[1024,128]{1,0:T(8,128)}, bf16[1024,128]{1,0:T(8,128)(2,1)}, f32[1024,128]{1,0:T(8,128)}, /*index=5*/bf16[2,1024,128]{2,1,0:T(8,128)(2,1)}) custom-call(s32[1]{0:T(128)} %bitcast.2.far_ref, bf16[1024,128]{1,0:T(8,128)(2,1)} %get-tuple-element.92.qh_ref, ...), custom_call_target="tpu_custom_call" | custom-call | flops 30720000000 | bytes 8388608 | tf_op jit(solution)/shard_map/attend_back/pallas_call | solution.py:367
  375.9 14.4 %attend_back.5 = (f32[1024,128]{1,0:T(8,128)}, f32[1024,128]{1,0:T(8,128)}, f32[1024,128]{1,0:T(8,128)}, bf16[1024,128]{1,0:T(8,128)(2,1)}, f32[1024,128]{1,0:T(8,128)}, /*index=5*/bf16[2,1024,128]{2,1,0:T(8,128)(2,1)}) custom-call(s32[1]{0:T(128)} %bitcast.2.far_ref, bf16[1024,128]{1,0:T(8,128)(2,1)} %get-tuple-element.97.qh_ref, ...), custom_call_target="tpu_custom_call" | custom-call | flops 30720000000 | bytes 8388608 | tf_op jit(solution)/shard_map/attend_back/pallas_call | solution.py:367
  392.8 13.3 %prep_back.3 = (bf16[1024,128]{1,0:T(8,128)(2,1)}, bf16[1024,128]{1,0:T(8,128)(2,1)}, bf16[1024,128]{1,0:T(8,128)(2,1)}, f32[1032,128]{1,0:T(8,128)}, f32[8,128]{1,0:T(8,128)}, /*index=5*/f32[8,128]{1,0:T(8,128)}) custom-call(bf16[1024,1536]{1,0:T(8,128)(2,1)} %copy-done.39, bf16[1024,1536]{1,0:T(8,128)(2,1)} %copy-done.39, bf16[1024,1536]{1,0:T(8,128)(2,1)} %copy-done.39, ...), custom_call_target="tpu_custom_call" | custom-call | flops 30720000000 | bytes 8388608 | tf_op jit(solution)/shard_map/prep_back/pallas_call | solution.py:390
  407.0 14.0 %prep_back.4 = (bf16[1024,128]{1,0:T(8,128)(2,1)}, bf16[1024,128]{1,0:T(8,128)(2,1)}, bf16[1024,128]{1,0:T(8,128)(2,1)}, f32[1032,128]{1,0:T(8,128)}, f32[8,128]{1,0:T(8,128)}, /*index=5*/f32[8,128]{1,0:T(8,128)}) custom-call(bf16[1024,1536]{1,0:T(8,128)(2,1)} %copy-done.39, bf16[1024,1536]{1,0:T(8,128)(2,1)} %copy-done.39, bf16[1024,1536]{1,0:T(8,128)(2,1)} %copy-done.39, ...), custom_call_target="tpu_custom_call" | custom-call | flops 30720000000 | bytes 8388608 | tf_op jit(solution)/shard_map/prep_back/pallas_call | solution.py:390
  430.9 13.3 %prep_back.5 = (bf16[1024,128]{1,0:T(8,128)(2,1)}, bf16[1024,128]{1,0:T(8,128)(2,1)}, bf16[1024,128]{1,0:T(8,128)(2,1)}, f32[1032,128]{1,0:T(8,128)}, f32[8,128]{1,0:T(8,128)}, /*index=5*/f32[8,128]{1,0:T(8,128)}) custom-call(bf16[1024,1536]{1,0:T(8,128)(2,1)} %copy-done.39, bf16[1024,1536]{1,0:T(8,128)(2,1)} %copy-done.39, bf16[1024,1536]{1,0:T(8,128)(2,1)} %copy-done.39, ...), custom_call_target="tpu_custom_call" | custom-call | flops 30720000000 | bytes 8388608 | tf_op jit(solution)/shard_map/prep_back/pallas_call | solution.py:390
  464.4 10.3 %fusion.38 = (bf16[1024,1536]{1,0:T(8,128)(2,1)}, bf16[1536]{0:T(1024)(128)(2,1)S(1)}) fusion(f32[1024]{0:T(1024)S(1)} %bitcast.138, bf16[4,256,1536]{2,1,0:T(8,128)(2,1)S(1)} %copy-done.15, f32[1024,1536]{1,0:T(8,128)} %fusion.37, bf16[1024,1536]{1,0:T(8,128)(2,1)} %maximum_dynamic-update-slice_fusion, bf16[1536,1536]{1,0:T(8,128)(2,1)} %bitcast.142), kind=kOutput, calls=%fused_computation.125 | convolution fusion | flops 4841273856 | bytes 20454400 | tf_op jit(solution)/shard_map/tn,dn->td/dot_general | solution.py:1232
  475.1 9.2 %convolution_convert_fusion.1 = bf16[8,192,1536]{2,1,0:T(8,128)(2,1)} fusion(bf16[8,192,1024]{2,1,0:T(8,128)(2,1)} %bitcast.127, bf16[1024,1536]{1,0:T(8,128)(2,1)} %maximum_dynamic-update-slice_fusion), kind=kOutput, calls=%fused_computation.9 | convolution fusion | flops 4834197504 | bytes 11010048 | tf_op jit(solution)/shard_map/td,tn->dn/dot_general | solution.py:1230
  496.0 92.3 %scatter_last.1 = (bf16[96,6144]{1,0:T(8,128)(2,1)}, bf16[4,96,512]{2,1,0:T(8,128)(2,1)}, bf16[96,8192]{1,0:T(8,128)(2,1)}, f32[256,1536]{1,0:T(8,128)}, f32[256,1536]{1,0:T(8,128)}) custom-call(bf16[8,192,2048]{2,1,0:T(8,128)(2,1)} %pad_maximum_fusion.p_ref, bf16[4,256,1536]{2,1,0:T(8,128)(2,1)} %bitcast.131, bf16[4,256,1536]{2,1,0:T(8,128)(2,1)} %bitcast.130, ...), custom_call_target="tpu_custom_call" | custom-call | tf_op jit(solution)/shard_map/scatter_last/pallas_call | solution.py:879
  (273 shorter events, 159.6 us)
Async XLA Ops:
  7.2 228.3 %all-gather.3.cloned.1.call-start = ((), (), s32[]{:S(2)}) async-start(), calls=%async_computation.6 | async-start | bytes 10616832 | tf_op jit(solution)/shard_map/all_gather | solution.py:1107
  103.7 13.1 %collective-permute-start = (bf16[8,384]{1,0:T(8,128)(2,1)S(1)}, bf16[8,384]{1,0:T(8,128)(2,1)S(1)}, u32[]{:S(2)}, u32[]{:S(2)}) collective-permute-start(bf16[8,384]{1,0:T(8,128)(2,1)S(1)} %slice.128), channel_id=1, source_target_pairs={{0,4},{1,5},{2,6},{3,7},{8,12},{9,13},{10,14},{11,15},{16,20},{17,... | collective-permute-start | bytes 18440 | tf_op jit(solution)/shard_map/ppermute | solution.py:1039
  107.8 39.4 %collective-permute-start.2 = (bf16[1024,384]{1,0:T(8,128)(2,1)}, bf16[1024,384]{1,0:T(8,128)(2,1)}, u32[]{:S(2)}, u32[]{:S(2)}) collective-permute-start(bf16[1024,384]{1,0:T(8,128)(2,1)} %slice.131), channel_id=1, source_target_pairs={{0,4},{1,5},{2,6},{3,7},{8,12},{9,13},{10,14},{11,15},{16,20},{17,... | collective-permute-start | bytes 2359304 | tf_op jit(solution)/shard_map/ppermute | solution.py:1039
  125.9 21.3 %collective-permute-start.1 = (bf16[1024,128]{1,0:T(8,128)(2,1)}, bf16[1024,128]{1,0:T(8,128)(2,1)S(1)}, u32[]{:S(2)}, u32[]{:S(2)}) collective-permute-start(bf16[1024,128]{1,0:T(8,128)(2,1)} %get-tuple-element.91), channel_id=1, source_target_pairs={{0,4},{1,5},{2,6},{3,7},{8,12},{9,13},{10,14},{11,15},{16,20},{17,... | collective-permute-start | bytes 786440 | tf_op jit(solution)/shard_map/ppermute | solution.py:1039
  135.8 20.6 %collective-permute-start.3 = (bf16[1024,128]{1,0:T(8,128)(2,1)}, bf16[1024,128]{1,0:T(8,128)(2,1)S(1)}, u32[]{:S(2)}, u32[]{:S(2)}) collective-permute-start(bf16[1024,128]{1,0:T(8,128)(2,1)} %get-tuple-element.96), channel_id=1, source_target_pairs={{0,4},{1,5},{2,6},{3,7},{8,12},{9,13},{10,14},{11,15},{16,20},{17,... | collective-permute-start | bytes 786440 | tf_op jit(solution)/shard_map/ppermute | solution.py:1039
  145.9 19.8 %collective-permute-start.4 = (bf16[1024,128]{1,0:T(8,128)(2,1)}, bf16[1024,128]{1,0:T(8,128)(2,1)S(1)}, u32[]{:S(2)}, u32[]{:S(2)}) collective-permute-start(bf16[1024,128]{1,0:T(8,128)(2,1)} %get-tuple-element.101), channel_id=1, source_target_pairs={{0,4},{1,5},{2,6},{3,7},{8,12},{9,13},{10,14},{11,15},{16,20},{17,... | collective-permute-start | bytes 786440 | tf_op jit(solution)/shard_map/ppermute | solution.py:1039
  177.2 14.4 %all-to-all-start = ((bf16[4,256,384]{1,2,0:T(8,128)(2,1)}), bf16[4,256,384]{1,2,0:T(8,128)(2,1)S(1)}, u32[]{:S(2)}, u32[]{:S(2)}) async-start(bf16[4,256,384]{1,2,0:T(8,128)(2,1)} %copy.51), calls=%async_computation | async-start | bytes 1572864 | tf_op jit(solution)/shard_map/all_to_all | solution.py:1153
  180.9 303.5 %reduce-scatter.5.cloned.1.call-start = ((), (), s32[]{:S(2)}) async-start(), calls=%async_computation.5 | async-start | bytes 3538944 | tf_op jit(solution)/shard_map/reduce_scatter | solution.py:1174
  272.1 33.4 %copy-start.48 = (pred[256]{0:T(512)(128)(4,1)}, pred[256]{0:T(512)(128)(4,1)S(1)}, u32[]{:S(2)}) copy-start(pred[256]{0:T(512)(128)(4,1)S(1)} %add_compare_fusion.1) | copy-start | bytes 772
  282.6 22.5 %copy-start.10 = (f32[256,1536]{1,0:T(8,128)S(1)}, f32[256,1536]{1,0:T(8,128)}, u32[]{:S(2)}) copy-start(f32[256,1536]{1,0:T(8,128)} %copy-done.9) | copy-start | bytes 4718596
  309.8 28.4 %collective-permute-start.5 = (bf16[1536,768]{1,0:T(8,128)(2,1)}, bf16[1536,768]{1,0:T(8,128)(2,1)}, u32[]{:S(2)}, u32[]{:S(2)}) collective-permute-start(bf16[1536,768]{1,0:T(8,128)(2,1)} %dynamic-slice_convert_fusion), channel_id=1, source_target_pairs={{0,2},{2,0},{1,3},{3,1},{4,6},{6,4},{5,7},{7,5},{8,10},{10,8},{9,1... | collective-permute-start | bytes 7077896 | tf_op jit(solution)/shard_map/ppermute | solution.py:1033
  313.5 29.7 %all-to-all-start.1 = ((bf16[256,4,384]{2,0,1:T(8,128)(2,1)}), bf16[256,4,384]{2,0,1:T(8,128)(2,1)}, u32[]{:S(2)}, u32[]{:S(2)}) async-start(bf16[256,4,384]{2,0,1:T(8,128)(2,1)} %bitcast.128), calls=%async_computation.1 | async-start | bytes 1572864 | tf_op jit(solution)/shard_map/all_to_all | solution.py:1184
  318.3 177.8 %reduce-scatter.3.cloned.1.call-start = ((), (), s32[]{:S(2)}) async-start(), calls=%async_computation.4 | async-start | bytes 7077888 | tf_op jit(solution)/shard_map/reduce_scatter | solution.py:1175
  357.5 34.6 %collective-permute-start.6 = (bf16[2,1024,128]{2,1,0:T(8,128)(2,1)}, bf16[2,1024,128]{2,1,0:T(8,128)(2,1)S(1)}, u32[]{:S(2)}, u32[]{:S(2)}) collective-permute-start(bf16[2,1024,128]{2,1,0:T(8,128)(2,1)} %get-tuple-element.115), channel_id=1, source_target_pairs={{4,0},{5,1},{6,2},{7,3},{12,8},{13,9},{14,10},{15,11},{20,16},{21,... | collective-permute-start | bytes 1572872 | tf_op jit(solution)/shard_map/ppermute | solution.py:1039
  373.2 32.9 %collective-permute-start.7 = (bf16[2,1024,128]{2,1,0:T(8,128)(2,1)}, bf16[2,1024,128]{2,1,0:T(8,128)(2,1)S(1)}, u32[]{:S(2)}, u32[]{:S(2)}) collective-permute-start(bf16[2,1024,128]{2,1,0:T(8,128)(2,1)} %get-tuple-element.124), channel_id=1, source_target_pairs={{4,0},{5,1},{6,2},{7,3},{12,8},{13,9},{14,10},{15,11},{20,16},{21,... | collective-permute-start | bytes 1572872 | tf_op jit(solution)/shard_map/ppermute | solution.py:1039
  374.5 55.1 %collective-permute-start.8 = (bf16[1536,384]{1,0:T(8,128)(2,1)S(1)}, bf16[1536,384]{1,0:T(8,128)(2,1)S(1)}, u32[]{:S(2)}, u32[]{:S(2)}) collective-permute-start(bf16[1536,384]{1,0:T(8,128)(2,1)S(1)} %dynamic-slice_convert_fusion.1), channel_id=1, source_target_pairs={{0,1},{1,0},{2,3},{3,2},{4,5},{5,4},{6,7},{7,6},{8,9},{9,8},{10,11... | collective-permute-start | bytes 3538952 | tf_op jit(solution)/shard_map/ppermute | solution.py:1033
  390.3 40.6 %collective-permute-start.9 = (bf16[2,1024,128]{2,1,0:T(8,128)(2,1)}, bf16[2,1024,128]{2,1,0:T(8,128)(2,1)}, u32[]{:S(2)}, u32[]{:S(2)}) collective-permute-start(bf16[2,1024,128]{2,1,0:T(8,128)(2,1)} %get-tuple-element.135), channel_id=1, source_target_pairs={{4,0},{5,1},{6,2},{7,3},{12,8},{13,9},{14,10},{15,11},{20,16},{21,... | collective-permute-start | bytes 1572872 | tf_op jit(solution)/shard_map/ppermute | solution.py:1039
  406.2 23.4 %slice-start.5 = ((s8[4718592]{0:T(1024)(128)(4,1)}), s8[4194304]{0:T(1024)(128)(4,1)S(1)}, s32[]{:S(2)}) async-start(s8[4718592]{0:T(1024)(128)(4,1)} %bitcast.121), calls=%async_computation.12 | async-start | bytes 8388608
  407.0 22.6 %slice-start.6 = ((s8[4718592]{0:T(1024)(128)(4,1)}), s8[524288]{0:T(1024)(128)(4,1)S(1)}, s32[]{:S(2)}) async-start(s8[4718592]{0:T(1024)(128)(4,1)} %bitcast.121), calls=%async_computation.13 | async-start | bytes 1048576
  422.2 33.7 %copy-start.23 = (f32[1024,128]{1,0:T(8,128)}, f32[1024,128]{1,0:T(8,128)S(1)}, u32[]{:S(2)}) copy-start(f32[1024,128]{1,0:T(8,128)S(1)} %slice.107) | copy-start | bytes 1572868
  424.0 31.9 %copy-start.24 = (f32[1024,128]{1,0:T(8,128)}, f32[1024,128]{1,0:T(8,128)S(1)}, u32[]{:S(2)}) copy-start(f32[1024,128]{1,0:T(8,128)S(1)} %slice.108) | copy-start | bytes 1572868
  430.9 20.2 %copy-start.33 = (bf16[1024,128]{1,0:T(8,128)(2,1)S(1)}, bf16[1024,128]{1,0:T(8,128)(2,1)}, u32[]{:S(2)}) copy-start(bf16[1024,128]{1,0:T(8,128)(2,1)} %get-tuple-element.138) | copy-start | bytes 786436
  446.3 15.2 %collective-permute-start.10 = (f32[8,384]{1,0:T(8,128)S(1)}, f32[8,384]{1,0:T(8,128)S(1)}, u32[]{:S(2)}, u32[]{:S(2)}) collective-permute-start(f32[8,384]{1,0:T(8,128)S(1)} %pad_maximum_fusion.7), channel_id=1, source_target_pairs={{4,0},{5,1},{6,2},{7,3},{12,8},{13,9},{14,10},{15,11},{20,16},{21,... | collective-permute-start | bytes 36872 | tf_op jit(solution)/shard_map/ppermute | solution.py:1039
  484.4 10.3 %collective-permute-start.11 = (bf16[128,1536]{1,0:T(8,128)(2,1)}, bf16[128,1536]{1,0:T(8,128)(2,1)S(1)}, u32[]{:S(2)}, u32[]{:S(2)}) collective-permute-start(bf16[128,1536]{1,0:T(8,128)(2,1)} %reduce-scatter.5.cloned.1.call-done), channel_id=1, source_target_pairs={{0,1},{1,0},{2,3},{3,2},{4,5},{5,4},{6,7},{7,6},{8,9},{9,8},{10,11... | collective-permute-start | bytes 1179656 | tf_op jit(solution)/shard_map/ppermute | solution.py:1033
  (60 other events, 319.7 us)
Sparse Core Ops, SparseCore 0:
  93.3 142.1 all-gather.2
  267.5 72.5 reduce-scatter.4
  343.6 122.6 reduce-scatter.2

commit v4 on v3

--- a/solution.py
+++ b/solution.py
@@ -129,8 +129,9 @@
     for c in range(chunks):
         span = slice(c * CH, (c + 1) * CH)
         s_ref[span, span] = jnp.where(upto, s_in_ref[span, :], negative)
-        if c + 1 < chunks:
-            s_ref[span, (c + 1) * CH :] = jnp.full((CH, count - (c + 1) * CH), negative, f32)
+        end = chunks // 2 * CH if c < chunks // 2 else count
+        if (c + 1) * CH < end:
+            s_ref[span, (c + 1) * CH : end] = jnp.full((CH, end - (c + 1) * CH), negative, f32)
     for m in range(chunks - 2, -1, -1):
         rows = slice((m + 1) * CH, count)
         span = slice(m * CH, (m + 1) * CH)
@@ -141,8 +142,8 @@
         q_ref[rows, :] = mm(cur, p_ref[span, :]).astype(bf16)
 
 
-def strip_weights(scale, far, begin, q_ref, s_ref, kr_ref):
-    local = s_ref[pl.ds(begin, CH), :] * scale
+def strip_weights(scale, far, begin, near, q_ref, s_ref, kr_ref):
+    local = s_ref[pl.ds(begin, CH), :near] * scale
     q = q_ref[pl.ds(begin, CH), :]
     remote = mm(q, kr_ref[...], 1, 1) * scale
     cols = lax.broadcasted_iota(jnp.int32, remote.shape, 1)
@@ -159,14 +160,18 @@
     far = far_ref[0]
     walk_queries(qh_ref, kh_ref, p_ref, s_in_ref, q_ref, s_ref, None)
 
-    def strip(c, carry):
+    count = qh_ref.shape[0]
+
+    def strip(near, c, carry):
         begin = pl.multiple_of(c * CH, CH)
-        e_local, e_remote, total = strip_weights(scale, far, begin, q_ref, s_ref, kr_ref)
-        summed = mm(e_local, v_ref[...]) + mm(e_remote, vr_ref[...])
+        e_local, e_remote, total = strip_weights(scale, far, begin, near, q_ref, s_ref, kr_ref)
+        summed = mm(e_local, v_ref[:near]) + mm(e_remote, vr_ref[...])
         o_ref[pl.ds(begin, CH), :] = (summed / total).astype(bf16)
         return carry
 
-    lax.fori_loop(0, qh_ref.shape[0] // CH, strip, 0)
+    middle = count // CH // 2
+    lax.fori_loop(0, middle, functools.partial(strip, middle * CH), 0)
+    lax.fori_loop(middle, count // CH, functools.partial(strip, count), 0)
 
 
 def attend_back_kernel(far_ref, qh_ref, kh_ref, p_ref, s_in_ref, v_ref, kr_ref, vr_ref, do_ref,
@@ -178,34 +183,38 @@
     chunks = count // CH
     walk_queries(qh_ref, kh_ref, p_ref, s_in_ref, q_ref, s_ref, save_ref)
 
-    def strip(c, carry):
+    def strip(near, c, carry):
         begin = pl.multiple_of(c * CH, CH)
-        e_local, e_remote, total = strip_weights(scale, far, begin, q_ref, s_ref, kr_ref)
+        e_local, e_remote, total = strip_weights(scale, far, begin, near, q_ref, s_ref, kr_ref)
         inverse = 1.0 / total
         p_local, p_remote = e_local * inverse, e_remote * inverse
         do = do_ref[pl.ds(begin, CH), :]
-        dp_local = mm(do, v_ref[...], 1, 1)
+        dp_local = mm(do, v_ref[:near], 1, 1)
         dp_remote = mm(do, vr_ref[...], 1, 1)
         delta = jnp.sum(p_local * dp_local, -1, keepdims=True) + jnp.sum(
             p_remote * dp_remote, -1, keepdims=True
         )
         d_local = p_local * (dp_local - delta) * scale
         d_remote = (p_remote * (dp_remote - delta) * scale).astype(bf16)
-        pl_ref[pl.ds(begin, CH), :] = p_local.astype(bf16)
+        pl_ref[pl.ds(begin, CH), :near] = p_local.astype(bf16)
         pr_ref[pl.ds(begin, CH), :] = p_remote.astype(bf16)
-        dsl_ref[pl.ds(begin, CH), :] = d_local.astype(bf16)
+        dsl_ref[pl.ds(begin, CH), :near] = d_local.astype(bf16)
         dsr_ref[pl.ds(begin, CH), :] = d_remote
         dq_ref[pl.ds(begin, CH), :] = mm(d_remote, kr_ref[...])
         return carry
 
-    lax.fori_loop(0, chunks, strip, 0)
+    middle = chunks // 2
+    split = middle * CH
+    lax.fori_loop(0, middle, functools.partial(strip, split), 0)
+    lax.fori_loop(middle, chunks, functools.partial(strip, count), 0)
     do = do_ref[...]
     far_count = kr_ref.shape[0]
     for b in range(0, far_count, count):
         part = slice(b, b + count)
         dfar_ref[1, part, :] = mm(pr_ref[:, part], do, 0, 0).astype(bf16)
         dfar_ref[0, part, :] = mm(dsr_ref[:, part], q_ref[...], 0, 0).astype(bf16)
-    dv_ref[...] = mm(pl_ref[...], do, 0, 0)
+    dv_ref[:split] = mm(pl_ref[:, :split], do, 0, 0)
+    dv_ref[split:] = mm(pl_ref[split:, split:], do_ref[split:], 0, 0)
     for m in range(chunks):
         span = slice(m * CH, (m + 1) * CH)
         ds_ref[span, :] = dsl_ref[span, span]
@@ -444,7 +453,8 @@
     t, other_t = c * 2 + q, (1 - c) * 2 + q
     width = wo_ref.shape[-1]
     half = width // 2
-    middle = wide_ref.shape[-1] // 2
+    middle = features
+    kinds = (0, 1, 2, 3, 4, 5)
     columns = pl.ds(pl.multiple_of(q * half, half), half)
     greet(r, row_count, y, y_count)
 
@@ -488,10 +498,10 @@
         return remote(own_out, wo_ref.at[r, from_y, c, :, columns], wo_y_send.at[step], wo_y_recv.at[from_y],
                       {"cy": lax.rem(y + step, y_count)})
 
+    for step in range(1, y_count):
+        wo_y_copy(y, step).start()
     for copy in cross:
         copy.start()
-    for step in range(1, y_count):
-        wo_y_copy(y, step).start()
     for copy in local:
         copy.start()
 
@@ -555,19 +565,18 @@
     local[4].wait()
     cross[4].wait_recv()
     pass_on(0, r, True, True)
-    for kind in (2, 3):
-        for block in (2 * (kind - 2), 2 * (kind - 2) + 1):
-            local[block].wait()
-            cross[block].wait_recv()
-        pass_on(kind, r, True, True)
     local[5].wait()
     for step in range(1, y_count):
         wo_y_copy(lax.rem(y + step, y_count), step).wait_recv()
     pass_on(1, r, True, True)
+    for kind in kinds[2:]:
+        local[kind - 2].wait()
+        cross[kind - 2].wait_recv()
+        pass_on(kind, r, True, True)
     tokens[1][0].start()
     tokens[1][1].start()
     for k in range(1, row_count):
-        for kind in (0, 2, 3, 1):
+        for kind in kinds:
             @pl.when(r - k >= 0)
             def _():
                 z_copy(kind, r - k, 1).wait_recv()
@@ -589,7 +598,7 @@
         wo_x_copy(origin).wait_recv()
         wo_c_copy(origin).start()
     for origin in range(row_count):
-        for kind in (0, 2, 3):
+        for kind in kinds[:1] + kinds[2:]:
             for step in range(1, y_count):
                 y_copy(kind, origin, lax.rem(y + step, y_count), step).wait_recv()
         wo_c_copy(origin).wait_recv()
@@ -611,7 +620,7 @@
     for step in range(1, y_count):
         wo_y_copy(y, step).wait_send()
     for origin in range(row_count):
-        for kind in range(4):
+        for kind in kinds:
             @pl.when((r >= origin) & (r < row_count - 1))
             def _():
                 z_copy(kind, origin, 1).wait_send()
@@ -654,8 +663,8 @@
             jax.ShapeDtypeStruct(pair_shape, bf16),
         ],
         scratch_shapes=[dma((max(1, width // part),)), dma((blocks,)), dma((blocks,)), dma((blocks,)), dma((8,)), dma((5,)), dma((5,)), dma((2, 3)), dma((2, 3)),
-                        dma((4, row_count)), dma((4, row_count)), dma((4, row_count)),
-                        dma((4, row_count, y_count)), dma((4, row_count, y_count)),
+                        dma((6, row_count)), dma((6, row_count)), dma((6, row_count)),
+                        dma((6, row_count, y_count)), dma((6, row_count, y_count)),
                         dma((y_count,)), dma((y_count,))] + [dma((row_count,))] * 4,
         compiler_params=pltpu.CompilerParams(collective_id=1, has_side_effects=True, vmem_limit_bytes=48 * 1024 * 1024),
         name="gather_first",
@@ -665,11 +674,12 @@
             xs.reshape(4 * x.shape[0], -1), gs.reshape(4 * g.shape[0], -1), pair)
 
 
-def scatter_kernel(row_count, y_count, features, part, p_ref, dh_ref, br_ref, gu_ref,
-                   qkvu_res_ref, rest_ref, gu_out_ref, dh_res_ref, br_res_ref,
-                   yin_ref, up_ref, down_ref, out_ref, res_ref, gu_res_ref, dcc_ref, dst_ref, dseq_ref,
+def scatter_kernel(row_count, y_count, features, part, p_ref, small_ref, o_ref, dh_ref, br_ref, gu_ref,
+                   qkvu_res_ref, small_out_ref, out_res_ref, gu_out_ref, dh_res_ref, br_res_ref,
+                   yin_ref, up_ref, down_ref, out_ref, ups_ref, downs_ref, outs_ref, ylast_ref, olast_ref, res_ref, gu_res_ref, dcc_ref, dst_ref, dseq_ref,
                    y_send, y_recv, up_send, up_recv, down_send, down_recv, t_send, t_recv,
-                   dh_send, dh_recv, local_sem):
+                   dh_send, dh_recv, local_sem,
+                   o_up_send, o_up_recv, o_down_send, o_down_recv, o_y_send, o_y_recv):
     r, y = lax.axis_index("row"), lax.axis_index("cy")
     c, q = lax.axis_index("cc"), lax.axis_index("seq")
     t = c * 2 + q
@@ -677,15 +687,24 @@
     piece = 16 if depth % 16 == 0 else depth
     greet(r, row_count, y, y_count)
 
-    pieces = t_send.shape[0] - 1
-    cut = p_ref.shape[2] // pieces
+    wide = p_ref.shape[2]
+    small = small_ref.shape[2]
+    third = wide // 3
+    spans = ((0, small), (small, third), (small + third, third), (small + 2 * third, third))
+    pieces = len(spans)
 
     def lanes(i):
-        return pl.ds(i * cut, cut)
+        return pl.ds(*spans[i])
+
+    def source(i):
+        if i == 0:
+            return small_ref, slice(0, small)
+        return p_ref, slice(spans[i][0] - small, spans[i][0] - small + spans[i][1])
 
     def y_copy(i, dest, step):
         to = lax.rem(y + step, y_count)
-        return remote(p_ref.at[dest * y_count + to, :, lanes(i)], yin_ref.at[dest, step - 1, :, lanes(i)],
+        ref, span = source(i)
+        return remote(ref.at[dest * y_count + to, :, pl.ds(span.start, span.stop - span.start)], yin_ref.at[dest, step - 1, :, lanes(i)],
                       y_send.at[i, dest, step - 1], y_recv.at[i, dest, step - 1], {"cy": to})
 
     def z_copy(i, dest, step):
@@ -694,11 +713,12 @@
                       recvs.at[i, dest], {"row": r + step})
 
     def add_up(i, dest, extra):
-        span = slice(i * cut, (i + 1) * cut)
+        ref, own_span = source(i)
+        span = slice(spans[i][0], spans[i][0] + spans[i][1])
 
         def body(at, carry):
             rows = pl.ds(pl.multiple_of(at * piece, piece), piece)
-            total = p_ref[dest * y_count + y, rows, span].astype(f32)
+            total = ref[dest * y_count + y, rows, own_span].astype(f32)
             for step in range(1, y_count):
                 total = total + yin_ref[dest, step - 1, rows, span].astype(f32)
             for more in extra:
@@ -741,6 +761,58 @@
             add_up(i, dest, [])
 
         z_copy(i, dest, step).start()
+
+    def o_copy(dest, step):
+        landing, sends, recvs = (ups_ref, o_up_send, o_up_recv) if step > 0 else (downs_ref, o_down_send, o_down_recv)
+        return remote(outs_ref.at[dest], landing.at[dest], sends.at[dest], recvs.at[dest], {"row": r + step})
+
+    def o_add(dest, extra):
+        def body(at, carry):
+            rows = pl.ds(pl.multiple_of(at * piece, piece), piece)
+            for at_y in range(y_count):
+                total = o_ref[dest, at_y, rows].astype(f32)
+                for more in extra:
+                    total = total + more[dest, at_y, rows].astype(f32)
+                outs_ref[dest, at_y, rows] = total.astype(bf16)
+            return carry
+
+        lax.fori_loop(0, depth // piece, body, 0)
+
+    def o_forward(i, dest, step):
+        landing = ups_ref if step > 0 else downs_ref
+        inner = (r > 0) if step > 0 else (r < row_count - 1)
+
+        @pl.when(inner)
+        def _():
+            o_copy(dest, step).wait_recv()
+            o_add(dest, [landing])
+
+        @pl.when(jnp.logical_not(inner))
+        def _():
+            o_add(dest, [])
+
+        o_copy(dest, step).start()
+
+    def o_settle():
+        @pl.when(r == 0)
+        def _():
+            o_copy(r, -1).wait_recv()
+            o_add(r, [downs_ref])
+
+        @pl.when(r == row_count - 1)
+        def _():
+            o_copy(r, 1).wait_recv()
+            o_add(r, [ups_ref])
+
+        @pl.when((r > 0) & (r < row_count - 1))
+        def _():
+            o_copy(r, 1).wait_recv()
+            o_copy(r, -1).wait_recv()
+            o_add(r, [ups_ref, downs_ref])
+
+    def o_y_copy(step):
+        to = lax.rem(y + step, y_count)
+        return remote(outs_ref.at[r, to], ylast_ref.at[step - 1], o_y_send.at[step - 1], o_y_recv.at[step - 1], {"cy": to})
 
     half = depth // 2
 
@@ -757,17 +829,27 @@
 
     sums = (dh_ref, br_ref)
     cc_copies = [
-        remote(source.at[pl.ds((1 - c) * 2, 2)], dcc_ref.at[i], dh_send.at[i], dh_recv.at[i], {"cc": 1 - c})
-        for i, source in enumerate(sums)
+        remote(partial.at[pl.ds((1 - c) * 2, 2)], dcc_ref.at[i], dh_send.at[i], dh_recv.at[i], {"cc": 1 - c})
+        for i, partial in enumerate(sums)
     ]
     seq_copies = [
         remote(dst_ref.at[i], dseq_ref.at[i], dh_send.at[2 + i], dh_recv.at[2 + i], {"seq": 1 - q}) for i in range(2)
     ]
+    gu_last, gu_local = t_copies(pieces, gu_ref, gu_res_ref, pl.ds(0, gu_ref.shape[1]))
+    gu_local.start()
+    for copy in gu_last:
+        copy.start()
     for copy in cc_copies:
         copy.start()
-    for i in range(pieces):
-        ordered(i, start_y)
-        start_y(i, r, 0)
+    ordered(0, start_y)
+    start_y(0, r, 0)
+    ordered(1, start_y)
+    start_y(1, r, 0)
+    ordered(2, start_y)
+    start_y(2, r, 0)
+    ordered(3, start_y)
+    start_y(3, r, 0)
+    stages = [(n, step) for n in range(row_count - 1, 0, -1) for step in (1, -1)]
     tokens = dh_ref.shape[1]
     step_rows = 16 if tokens % 16 == 0 else tokens
 
@@ -778,20 +860,24 @@
 
         lax.fori_loop(0, tokens // step_rows, body, 0)
 
-    for i, source in enumerate(sums):
-        cc_copies[i].wait_recv()
-
-        def stage(rows):
-            total = source[c * 2 + 1 - q, rows].astype(f32) + dcc_ref[i, 1 - q, rows].astype(f32)
-            dst_ref[i, rows] = total.astype(bf16)
-
-        token_loop(stage)
-    gu_last, gu_local = t_copies(pieces, gu_ref, gu_res_ref, pl.ds(0, gu_ref.shape[1]))
-    gu_local.start()
-    for copy in seq_copies:
-        copy.start()
-    for copy in gu_last:
-        copy.start()
+    def stage_tokens():
+        for i, partial in enumerate(sums):
+            cc_copies[i].wait_recv()
+
+            def stage(rows):
+                total = partial[c * 2 + 1 - q, rows].astype(f32) + dcc_ref[i, 1 - q, rows].astype(f32)
+                dst_ref[i, rows] = total.astype(bf16)
+
+            token_loop(stage)
+
+
+    def staged(i, act, n, step):
+        dest = r + step * n
+        valid = (dest < row_count) if step > 0 else (dest >= 0)
+
+        @pl.when(valid)
+        def _():
+            act(i, dest, step)
 
     def finish_piece(i):
         for hop in range(1, y_count):
@@ -820,15 +906,47 @@
         return last + [local]
 
     finals = []
-    for i in range(pieces - 1):
-        ordered(i, forward)
-        finals += finish_piece(i)
-    ordered(pieces - 1, forward)
-    for i, (source, result) in enumerate(((dh_ref, dh_res_ref), (br_ref, br_res_ref))):
+    for n, step in stages[:2]:
+        staged(0, o_forward, n, step)
+    stage_tokens()
+    for copy in seq_copies:
+        copy.start()
+    for at, (n, step) in enumerate(stages):
+        if at > 1:
+            staged(0, o_forward, n, step)
+        staged(0, forward, n, step)
+        staged(1, forward, n, step)
+    o_settle()
+    for step in range(1, y_count):
+        o_y_copy(step).start()
+    finals += finish_piece(0)
+    finals += finish_piece(1)
+    def o_body(at, carry):
+        rows = pl.ds(pl.multiple_of(at * piece, piece), piece)
+        total = outs_ref[r, y, rows].astype(f32)
+        for step in range(1, y_count):
+            total = total + ylast_ref[step - 1, rows].astype(f32)
+        olast_ref[rows] = total.astype(bf16)
+        return carry
+
+    for n, step in stages:
+        staged(2, forward, n, step)
+    finals += finish_piece(2)
+    for n, step in stages:
+        staged(3, forward, n, step)
+    for step in range(1, y_count):
+        o_y_copy(step).wait_recv()
+    lax.fori_loop(0, depth // piece, o_body, 0)
+    o_last, o_local = t_copies(pieces + 1, olast_ref, out_res_ref, pl.ds(0, olast_ref.shape[1]))
+    for copy in o_last:
+        copy.start()
+    o_local.start()
+    finals += o_last + [o_local]
+    for i, (partial, result) in enumerate(((dh_ref, dh_res_ref), (br_ref, br_res_ref))):
         seq_copies[i].wait_recv()
 
         def settle(rows):
-            total = source[t, rows].astype(f32) + dcc_ref[i, q, rows].astype(f32)
+            total = partial[t, rows].astype(f32) + dcc_ref[i, q, rows].astype(f32)
             result[rows] = total + dseq_ref[i, rows].astype(f32)
 
         token_loop(settle)
@@ -842,7 +960,7 @@
         for block in range(gu_ref.shape[1] // part):
             place = (block * 4 + quarter) * part
             gu_out_ref[:, place : place + part] = gu_res_ref[quarter, :, block * part : (block + 1) * part]
-    finals += finish_piece(pieces - 1)
+    finals += finish_piece(3)
 
     def sent(i, dest, step):
         for hop in range(1, y_count):
@@ -853,6 +971,12 @@
         ordered(i, sent)
         for hop in range(1, y_count):
             y_copy(i, r, hop).wait_send()
+    def o_sent(i, dest, step):
+        o_copy(dest, step).wait_send()
+
+    ordered(0, o_sent)
+    for step in range(1, y_count):
+        o_y_copy(step).wait_send()
     for copy in gu_last + cc_copies + seq_copies:
         copy.wait_send()
     for copy in finals:
@@ -860,39 +984,47 @@
     for quarter in range(4):
         for block in range(4):
             place = block * 4 * features + quarter * features
-            qkvu_res_ref[:, place : place + features] = res_ref[quarter, :, block * features : (block + 1) * features]
-        rest_ref[quarter] = res_ref[quarter, :, 4 * features :]
-
-
-def scatter_last(partial, d_h, branch, gate_up_sum, features, part):
+            at = small + block * features
+            qkvu_res_ref[:, place : place + features] = res_ref[quarter, :, at : at + features]
+        small_out_ref[quarter] = res_ref[quarter, :, :small]
+
+
+def scatter_last(partial, small, out_part, d_h, branch, gate_up_sum, features, part):
     row_count, y_count = lax.axis_size("row"), lax.axis_size("cy")
-    total, cols = partial.shape
+    total, wide = partial.shape
+    cols, out_cols = wide + small.shape[1], out_part.shape[1]
     depth = total // (row_count * y_count)
     half = depth // 2
     tokens, width = d_h.shape[0] // 4, d_h.shape[1]
     vm = pl.BlockSpec(memory_space=pltpu.VMEM)
     dma = pltpu.SemaphoreType.DMA
     block = lambda *lead: pltpu.VMEM(lead + (depth, cols), bf16)
+    slab = lambda *lead: pltpu.VMEM(lead + (depth, out_cols), bf16)
     shape = jax.ShapeDtypeStruct
     gu_cols = gate_up_sum.shape[1]
-    pieces = 2
+    pieces = 4
     return pl.pallas_call(
         functools.partial(scatter_kernel, row_count, y_count, features, part),
-        in_specs=[vm] * 4,
-        out_specs=[vm] * 5,
-        out_shape=[shape((half, 16 * features), bf16), shape((4, half, cols - 4 * features), bf16),
+        in_specs=[vm] * 6,
+        out_specs=[vm] * 6,
+        out_shape=[shape((half, 16 * features), bf16), shape((4, half, small.shape[1]), bf16),
+                   shape((4, half, out_cols), bf16),
                    shape((4, half, gu_cols) if part % 128 else (half, 4 * gu_cols), bf16),
                    shape((tokens, width), f32), shape((tokens, width), f32)],
         scratch_shapes=[block(row_count, y_count - 1), block(row_count), block(row_count), block(row_count),
+                        slab(row_count, y_count), slab(row_count, y_count), slab(row_count, y_count),
+                        slab(y_count - 1), slab(),
                         pltpu.VMEM((4, half, cols), bf16), pltpu.VMEM((4, half, gu_cols), bf16),
                         pltpu.VMEM((2, 2, tokens, width), bf16), pltpu.VMEM((2, tokens, width), bf16),
                         pltpu.VMEM((2, tokens, width), bf16),
                         dma((pieces, row_count, y_count - 1)), dma((pieces, row_count, y_count - 1))]
                        + [dma((pieces, row_count))] * 4
-                       + [dma((pieces + 1, 3)), dma((pieces + 1, 3)), dma((4,)), dma((4,)), dma((pieces + 1,))],
+                       + [dma((pieces + 2, 3)), dma((pieces + 2, 3)), dma((4,)), dma((4,)), dma((pieces + 2,))]
+                       + [dma((row_count,))] * 4 + [dma((y_count - 1,))] * 2,
         compiler_params=pltpu.CompilerParams(collective_id=2, has_side_effects=True, vmem_limit_bytes=60 * 1024 * 1024),
         name="scatter_last",
-    )(partial.reshape(row_count * y_count, depth, cols), d_h.reshape(4, tokens, width),
+    )(partial.reshape(row_count * y_count, depth, wide), small.reshape(row_count * y_count, depth, -1),
+      out_part.reshape(row_count, y_count, depth, out_cols), d_h.reshape(4, tokens, width),
       branch.reshape(4, tokens, width), gate_up_sum)
 
 
@@ -1193,10 +1325,13 @@
                 far, qh, kh, p, s_in, projected, far_keys[head], far_values, d_attn, head, local
             )
         )
+    down_both = in_order(down_sum, swapped(down_sum, "seq"), seq)
+    middle = min(1, local - 1)
+    first, down_both = lax.optimization_barrier((backs[middle][0], down_both))
+    backs[middle] = [first] + list(backs[middle][1:])
     first, out_part = lax.optimization_barrier((backs[-1][0], out_part))
     backs[-1] = [first] + list(backs[-1][1:])
     pieces, logit_rows, kernel_rows = [], [], []
-    down_both = in_order(down_sum, swapped(down_sum, "seq"), seq)
     for head in range(local):
         w, t, _, kh, p, _, _ = prepared[head]
         dqh, dkh, dp, ds, dv, dfars = backs[head]
@@ -1245,8 +1380,8 @@
     )
     used = small_term.shape[1]
     small_term = jnp.pad(small_term, ((0, 0), (0, CH - used)))
-    qkvu_grad, rest, gate_up_grad, d_h_first, branch = scatter_last(
-        jnp.concatenate([qkvu_term, small_term, out_part], axis=1).astype(bf16),
+    qkvu_grad, small_sum, out_sum, gate_up_grad, d_h_first, branch = scatter_last(
+        qkvu_term.astype(bf16), small_term.astype(bf16), out_part.astype(bf16),
         d_h_first.astype(bf16), branch.astype(bf16), gate_up_sum, features, ff_part,
     )
     layer_output = jnp.where(valid, x_mid + branch, 0.0).astype(bf16)[None]
@@ -1256,8 +1391,8 @@
     if ff_part % CH:
         gate_up_grad = gate_up_grad.reshape(group, rows, -1, ff_part).transpose(1, 2, 0, 3).reshape(rows, -1)
     gate_up_grad = gate_up_grad.astype(f32)
-    small_grad = jnp.sum(rest[:, :, :CH].astype(f32), 0)
-    out_grad_own = jnp.concatenate([rest[i, :, CH:] for i in range(group)], axis=1).astype(f32)
+    small_grad = jnp.sum(small_sum.astype(f32), 0)
+    out_grad_own = jnp.concatenate([out_sum[i] for i in range(group)], axis=1).astype(f32)
     down_grad = down_both.astype(f32)
     return (
         layer_output,

time: 617 us -> 592 us (0.959)
  waiting for transfers between devices: 27.7 us -> 20.4 us
  local copies, waits for them, and re-layouts: 55.5 us -> 48.2 us
    unnamed x148 -> x144, local copies, waits for them, and re-layouts: 33.9 us -> 31.8 us
  transfers between devices with their start and end apart: 17 -> 17, of which waited for: 3 -> 3; matrix products, arithmetic and copies ran while one was open for 20% -> 19% of each run, Pallas kernels for 29% -> 30%
where the time goes in v4:
time: 592 us; the launch traced here: 585 us
  Pallas kernels  358 us (60%)
  matrix products  85.9 us (15%)
  local copies, waits for them, and re-layouts  48.2 us (8%)
  other arithmetic  32.7 us (6%)
  starting transfers between devices  24.9 us (4%)
  waiting for transfers between devices  20.4 us (3%)
  between operations  15.5 us (3%)
    pallas_call x1, Pallas kernels, scatter_last(): pl.pallas_call(functools.partial(scatter_kernel, row_count, y_count, feat...  89.6 us
    pallas_call x1, Pallas kernels, gather_first(): pl.pallas_call(functools.partial(gather_kernel, row_count, y_count, featu...  79.3 us
    pallas_call x3, Pallas kernels, attend_back(): pl.pallas_call(attend_back_kernel, grid=(1,), in_specs=[pl.BlockSpec(memo...  42.1 us
    pallas_call x3, Pallas kernels, prep_back(): pl.pallas_call(functools.partial(prep_back_kernel, unroll, head), grid=(1...  41 us
    unnamed x144, local copies, waits for them, and re-layouts  31.8 us
    pallas_call x3, Pallas kernels, prep(): pl.pallas_call(functools.partial(prep_kernel, unroll, head), grid=(1,), i...  25.7 us
    pallas_call x3, Pallas kernels, attend(): pl.pallas_call(attend_kernel, grid=(1,), in_specs=[pl.BlockSpec(memory_sp...  24.8 us
    pallas_call x1, Pallas kernels, group_sum(): pl.pallas_call(group_sum_kernel, in_specs=[pl.BlockSpec(memory_space=pltp...  23 us
  transfers between devices with their start and end apart: 17, of which 3 were waited for; matrix products, arithmetic and copies ran while one was open for 19% of the time, Pallas kernels for 30%

profile of v4, /device:TPU:1, one launch (start us, length us, event | category | flops | bytes accessed | tf_op | source)
XLA Modules:
  0.0 585.1 jit_solution(13102625925273128468)
XLA Ops:
  13.6 79.3 %gather_first.1 = (bf16[4,2,2,96,1536]{4,3,2,1,0:T(8,128)(2,1)}, bf16[4,2,2,32,128]{4,3,2,1,0:T(8,128)(2,1)S(1)}, bf16[4,2,2,96,1536]{4,3,2,1,0:T(8,128)(2,1)}, ...) custom-call(bf16[96,6144]{1,0:T(8,128)(2,1)S(1)} %copy-done.5, ...), custom_call_target="tpu_custom_call" | custom-call | tf_op jit(solution)/shard_map/gather_first/pallas_call | solution.py:653
  115.7 8.6 %prep.5 = (bf16[1024,128]{1,0:T(8,128)(2,1)}, bf16[1024,128]{1,0:T(8,128)(2,1)}, bf16[1024,128]{1,0:T(8,128)(2,1)}, bf16[1024,128]{1,0:T(8,128)(2,1)}, bf16[1024...) custom-call(bf16[1024,1536]{1,0:T(8,128)(2,1)} %copy-done.40, bf16[1024,1536]{1,0:T(8,128)(2,1)} %copy-done.40, ...), custom_call_target="tpu_custom_call" | custom-call | flops 10240000000 | bytes 4194304 | tf_op jit(solution)/shard_map/prep/pallas_call | solution.py:339
  125.6 8.6 %prep.4 = (bf16[1024,128]{1,0:T(8,128)(2,1)}, bf16[1024,128]{1,0:T(8,128)(2,1)}, bf16[1024,128]{1,0:T(8,128)(2,1)}, bf16[1024,128]{1,0:T(8,128)(2,1)}, bf16[1024...) custom-call(bf16[1024,1536]{1,0:T(8,128)(2,1)} %copy-done.40, bf16[1024,1536]{1,0:T(8,128)(2,1)} %copy-done.40, ...), custom_call_target="tpu_custom_call" | custom-call | flops 10240000000 | bytes 4194304 | tf_op jit(solution)/shard_map/prep/pallas_call | solution.py:339
  135.8 8.6 %prep.3 = (bf16[1024,128]{1,0:T(8,128)(2,1)}, bf16[1024,128]{1,0:T(8,128)(2,1)}, bf16[1024,128]{1,0:T(8,128)(2,1)}, bf16[1024,128]{1,0:T(8,128)(2,1)}, bf16[1024...) custom-call(bf16[1024,1536]{1,0:T(8,128)(2,1)} %copy-done.40, bf16[1024,1536]{1,0:T(8,128)(2,1)} %copy-done.40, ...), custom_call_target="tpu_custom_call" | custom-call | flops 10240000000 | bytes 4194304 | tf_op jit(solution)/shard_map/prep/pallas_call | solution.py:339
  146.4 8.2 %attend.5 = bf16[1024,128]{1,0:T(8,128)(2,1)} custom-call(s32[1]{0:T(128)} %bitcast.2.far_ref, bf16[1024,128]{1,0:T(8,128)(2,1)} %get-tuple-element.100.qh_ref, bf16[1024,128]{1,0:T(8,128)(2,1)} %get-tuple-element.101.kh_ref, bf16[1024,128]{1,0:T(8,128)(2,1)} %get-tuple-element.102.p_ref, f32[1024,128]{1,0:T(8,128)} %get-tuple-element.103.s_in_ref, ...), custom_call_target="tpu_custom_call" | custom-call | flops 10240000000 | bytes 4194304 | tf_op jit(solution)/shard_map/attend/pallas_call | solution.py:356
  155.4 8.2 %attend.4 = bf16[1024,128]{1,0:T(8,128)(2,1)} custom-call(s32[1]{0:T(128)} %bitcast.2.far_ref, bf16[1024,128]{1,0:T(8,128)(2,1)} %get-tuple-element.95.qh_ref, bf16[1024,128]{1,0:T(8,128)(2,1)} %get-tuple-element.96.kh_ref, bf16[1024,128]{1,0:T(8,128)(2,1)} %get-tuple-element.97.p_ref, f32[1024,128]{1,0:T(8,128)} %get-tuple-element.98.s_in_ref, ...), custom_call_target="tpu_custom_call" | custom-call | flops 10240000000 | bytes 4194304 | tf_op jit(solution)/shard_map/attend/pallas_call | solution.py:356
  164.3 8.3 %attend.3 = bf16[1024,128]{1,0:T(8,128)(2,1)} custom-call(s32[1]{0:T(128)} %bitcast.2.far_ref, bf16[1024,128]{1,0:T(8,128)(2,1)} %get-tuple-element.90.qh_ref, bf16[1024,128]{1,0:T(8,128)(2,1)} %get-tuple-element.91.kh_ref, bf16[1024,128]{1,0:T(8,128)(2,1)} %get-tuple-element.92.p_ref, f32[1024,128]{1,0:T(8,128)} %get-tuple-element.93.s_in_ref, ...), custom_call_target="tpu_custom_call" | custom-call | flops 10240000000 | bytes 4194304 | tf_op jit(solution)/shard_map/attend/pallas_call | solution.py:356
  194.9 21.8 %group_gather.1 = bf16[4,256,1536]{2,1,0:T(8,128)(2,1)S(1)} custom-call(bf16[256,1536]{1,0:T(8,128)(2,1)S(1)} %multiply_convert_fusion.5.x_ref), custom_call_target="tpu_custom_call" | custom-call | tf_op jit(solution)/shard_map/group_gather/pallas_call | solution.py:1060
  216.7 12.1 %all-gather.3.cloned.1.call-done = bf16[36864,128]{1,0:T(8,128)(2,1)} async-done(((bf16[4608,128]{1,0:T(8,128)(2,1)}), bf16[36864,128]{1,0:T(8,128)(2,1)}) %all-gather.3.cloned.1.call-update) | async-done | bytes 9437200 | tf_op jit(solution)/shard_map/all_gather | solution.py:1239
  228.8 10.3 %unpack.1 = (bf16[1536,2048]{1,0:T(8,128)(2,1)}, bf16[1024,1536]{1,0:T(8,128)(2,1)}) custom-call(bf16[8,4608,128]{2,1,0:T(8,128)(2,1)} %bitcast.121), custom_call_target="tpu_custom_call" | custom-call | bytes 18874368 | tf_op jit(solution)/shard_map/unpack/pallas_call | solution.py:1154
  239.2 9.0 %fusion.38 = f32[1024,2048]{0,1:T(8,128)S(1)} fusion(bf16[1024,1536]{1,0:T(8,128)(2,1)S(1)} %bitcast.108, bf16[1536,2048]{1,0:T(8,128)(2,1)} %get-tuple-element.111), kind=kOutput, calls=%fused_computation.124 | convolution fusion | flops 6442450944 | bytes 17825792 | tf_op jit(solution)/shard_map/dot_general | solution.py:1289
  260.9 10.2 %fusion.1 = f32[1024,1536]{1,0:T(8,128)S(1)} fusion(bf16[1536,2048]{1,0:T(8,128)(2,1)} %get-tuple-element.111, bf16[1024,1024]{0,1:T(8,128)(2,1)} %get-tuple-element.193, bf16[1024,1024]{0,1:T(8,128)(2,1)} %get-tuple-element.192), kind=kOutput, calls=%fused_computation.24 | convolution fusion | flops 6450839552 | bytes 16777216 | tf_op jit(solution)/shard_map/tf,df->td/dot_general | solution.py:1302
  271.2 23.0 %group_sum.1 = f32[256,1536]{1,0:T(8,128)S(1)} custom-call(f32[4,256,1536]{2,1,0:T(8,128)S(1)} %bitcast.107), custom_call_target="tpu_custom_call" | custom-call | tf_op jit(solution)/shard_map/group_sum/pallas_call | solution.py:1126
  307.8 10.9 %convolution_convert_fusion.1 = bf16[1536,2048]{1,0:T(8,128)(2,1)} fusion(bf16[1024,1536]{1,0:T(8,128)(2,1)S(1)} %bitcast.109, bf16[1024,1024]{0,1:T(8,128)(2,1)} %get-tuple-element.193, bf16[1024,1024]{0,1:T(8,128)(2,1)} %get-tuple-element.192), kind=kOutput, calls=%fused_computation.1 | convolution fusion | flops 6453985280 | bytes 13631488 | tf_op jit(solution)/shard_map/td,tf->df/dot_general | solution.py:1305
  320.2 6.9 %convolution_convert_fusion.3 = bf16[1024,1536]{1,0:T(8,128)(2,1)} fusion(bf16[1024,1024]{0,1:T(8,128)(2,1)S(1)} %copy-done.57, bf16[1024,1536]{1,0:T(8,128)(2,1)} %get-tuple-element.110), kind=kOutput, calls=%fused_computation.17 | convolution fusion | flops 3222798336 | bytes 8388608 | tf_op jit(solution)/shard_map/dot_general | solution.py:1295
  332.0 13.9 %attend_back.3 = (f32[1024,128]{1,0:T(8,128)}, f32[1024,128]{1,0:T(8,128)}, f32[1024,128]{1,0:T(8,128)}, bf16[1024,128]{1,0:T(8,128)(2,1)}, f32[1024,128]{1,0:T(8,128)}, /*index=5*/bf16[2,1024,128]{2,1,0:T(8,128)(2,1)}) custom-call(s32[1]{0:T(128)} %bitcast.2.far_ref, bf16[1024,128]{1,0:T(8,128)(2,1)} %get-tuple-element.90.qh_ref, ...), custom_call_target="tpu_custom_call" | custom-call | flops 30720000000 | bytes 8388608 | tf_op jit(solution)/shard_map/attend_back/pallas_call | solution.py:376
  347.3 14.1 %attend_back.4 = (f32[1024,128]{1,0:T(8,128)}, f32[1024,128]{1,0:T(8,128)}, f32[1024,128]{1,0:T(8,128)}, bf16[1024,128]{1,0:T(8,128)(2,1)}, f32[1024,128]{1,0:T(8,128)}, /*index=5*/bf16[2,1024,128]{2,1,0:T(8,128)(2,1)}) custom-call(s32[1]{0:T(128)} %bitcast.2.far_ref, bf16[1024,128]{1,0:T(8,128)(2,1)} %get-tuple-element.95.qh_ref, ...), custom_call_target="tpu_custom_call" | custom-call | flops 30720000000 | bytes 8388608 | tf_op jit(solution)/shard_map/attend_back/pallas_call | solution.py:376
  364.1 14.1 %attend_back.5 = (f32[1024,128]{1,0:T(8,128)}, f32[1024,128]{1,0:T(8,128)}, f32[1024,128]{1,0:T(8,128)}, bf16[1024,128]{1,0:T(8,128)(2,1)}, f32[1024,128]{1,0:T(8,128)}, /*index=5*/bf16[2,1024,128]{2,1,0:T(8,128)(2,1)}) custom-call(s32[1]{0:T(128)} %bitcast.2.far_ref, bf16[1024,128]{1,0:T(8,128)(2,1)} %get-tuple-element.100.qh_ref, ...), custom_call_target="tpu_custom_call" | custom-call | flops 30720000000 | bytes 8388608 | tf_op jit(solution)/shard_map/attend_back/pallas_call | solution.py:376
  380.5 13.9 %prep_back.3 = (bf16[1024,128]{1,0:T(8,128)(2,1)}, bf16[1024,128]{1,0:T(8,128)(2,1)}, bf16[1024,128]{1,0:T(8,128)(2,1)}, f32[1032,128]{1,0:T(8,128)}, f32[8,128]{1,0:T(8,128)}, /*index=5*/f32[8,128]{1,0:T(8,128)}) custom-call(bf16[1024,1536]{1,0:T(8,128)(2,1)} %copy-done.40, bf16[1024,1536]{1,0:T(8,128)(2,1)} %copy-done.40, bf16[1024,1536]{1,0:T(8,128)(2,1)} %copy-done.40, ...), custom_call_target="tpu_custom_call" | custom-call | flops 30720000000 | bytes 8388608 | tf_op jit(solution)/shard_map/prep_back/pallas_call | solution.py:399
  401.9 13.7 %prep_back.5 = (bf16[1024,128]{1,0:T(8,128)(2,1)}, bf16[1024,128]{1,0:T(8,128)(2,1)}, bf16[1024,128]{1,0:T(8,128)(2,1)}, f32[1032,128]{1,0:T(8,128)}, f32[8,128]{1,0:T(8,128)}, /*index=5*/f32[8,128]{1,0:T(8,128)}) custom-call(bf16[1024,1536]{1,0:T(8,128)(2,1)} %copy-done.40, bf16[1024,1536]{1,0:T(8,128)(2,1)} %copy-done.40, bf16[1024,1536]{1,0:T(8,128)(2,1)} %copy-done.40, ...), custom_call_target="tpu_custom_call" | custom-call | flops 30720000000 | bytes 8388608 | tf_op jit(solution)/shard_map/prep_back/pallas_call | solution.py:399
  418.9 13.4 %prep_back.4 = (bf16[1024,128]{1,0:T(8,128)(2,1)}, bf16[1024,128]{1,0:T(8,128)(2,1)}, bf16[1024,128]{1,0:T(8,128)(2,1)}, f32[1032,128]{1,0:T(8,128)}, f32[8,128]{1,0:T(8,128)}, /*index=5*/f32[8,128]{1,0:T(8,128)}) custom-call(bf16[1024,1536]{1,0:T(8,128)(2,1)} %copy-done.40, bf16[1024,1536]{1,0:T(8,128)(2,1)} %copy-done.40, bf16[1024,1536]{1,0:T(8,128)(2,1)} %copy-done.40, ...), custom_call_target="tpu_custom_call" | custom-call | flops 30720000000 | bytes 8388608 | tf_op jit(solution)/shard_map/prep_back/pallas_call | solution.py:399
  454.4 10.3 %fusion.37 = (bf16[1024,1536]{1,0:T(8,128)(2,1)}, bf16[1536]{0:T(1024)(128)(2,1)S(1)}) fusion(f32[1024]{0:T(1024)S(1)} %bitcast.134, bf16[4,256,1536]{2,1,0:T(8,128)(2,1)S(1)} %copy-done.13, f32[1024,1536]{1,0:T(8,128)} %fusion.36, bf16[1024,1536]{1,0:T(8,128)(2,1)} %maximum_dynamic-update-slice_fusion, bf16[1536,1536]{1,0:T(8,128)(2,1)} %bitcast.138), kind=kOutput, calls=%fused_computation.123 | convolution fusion | flops 4841273856 | bytes 20454400 | tf_op jit(solution)/shard_map/tn,dn->td/dot_general | solution.py:1367
  465.9 9.2 %convolution_convert_fusion = bf16[1536,1536]{1,0:T(8,128)(2,1)} fusion(bf16[1024,1536]{1,0:T(8,128)(2,1)} %copy-done.14, bf16[1024,1536]{1,0:T(8,128)(2,1)} %maximum_dynamic-update-slice_fusion), kind=kOutput, calls=%fused_computation | convolution fusion | flops 4834197504 | bytes 11010048 | tf_op jit(solution)/shard_map/td,tn->dn/dot_general | solution.py:1365
  475.2 89.6 %scatter_last.1 = (bf16[96,6144]{1,0:T(8,128)(2,1)}, bf16[4,96,128]{2,1,0:T(8,128)(2,1)}, bf16[4,96,384]{2,1,0:T(8,128)(2,1)}, bf16[96,8192]{1,0:T(8,128)(2,1)},...) custom-call(bf16[8,192,1536]{2,1,0:T(8,128)(2,1)} %bitcast.123, bf16[8,192,128]{2,1,0:T(8,128)(2,1)} %bitcast.129, ...), custom_call_target="tpu_custom_call" | custom-call | tf_op jit(solution)/shard_map/scatter_last/pallas_call | solution.py:1006
  (268 shorter events, 143.4 us)
Async XLA Ops:
  7.2 221.7 %all-gather.3.cloned.1.call-start = ((), (), s32[]{:S(2)}) async-start(), calls=%async_computation.6 | async-start | bytes 10616832 | tf_op jit(solution)/shard_map/all_gather | solution.py:1239
  103.4 11.7 %collective-permute-start = (bf16[8,384]{1,0:T(8,128)(2,1)S(1)}, bf16[8,384]{1,0:T(8,128)(2,1)S(1)}, u32[]{:S(2)}, u32[]{:S(2)}) collective-permute-start(bf16[8,384]{1,0:T(8,128)(2,1)S(1)} %slice.124), channel_id=1, source_target_pairs={{0,4},{1,5},{2,6},{3,7},{8,12},{9,13},{10,14},{11,15},{16,20},{17,... | collective-permute-start | bytes 18440 | tf_op jit(solution)/shard_map/ppermute | solution.py:1171
  106.5 39.2 %collective-permute-start.2 = (bf16[1024,384]{1,0:T(8,128)(2,1)}, bf16[1024,384]{1,0:T(8,128)(2,1)}, u32[]{:S(2)}, u32[]{:S(2)}) collective-permute-start(bf16[1024,384]{1,0:T(8,128)(2,1)} %slice.127), channel_id=1, source_target_pairs={{0,4},{1,5},{2,6},{3,7},{8,12},{9,13},{10,14},{11,15},{16,20},{17,... | collective-permute-start | bytes 2359304 | tf_op jit(solution)/shard_map/ppermute | solution.py:1171
  124.3 21.5 %collective-permute-start.4 = (bf16[1024,128]{1,0:T(8,128)(2,1)}, bf16[1024,128]{1,0:T(8,128)(2,1)S(1)}, u32[]{:S(2)}, u32[]{:S(2)}) collective-permute-start(bf16[1024,128]{1,0:T(8,128)(2,1)} %get-tuple-element.104), channel_id=1, source_target_pairs={{0,4},{1,5},{2,6},{3,7},{8,12},{9,13},{10,14},{11,15},{16,20},{17,... | collective-permute-start | bytes 786440 | tf_op jit(solution)/shard_map/ppermute | solution.py:1171
  134.1 20.5 %collective-permute-start.3 = (bf16[1024,128]{1,0:T(8,128)(2,1)}, bf16[1024,128]{1,0:T(8,128)(2,1)S(1)}, u32[]{:S(2)}, u32[]{:S(2)}) collective-permute-start(bf16[1024,128]{1,0:T(8,128)(2,1)} %get-tuple-element.99), channel_id=1, source_target_pairs={{0,4},{1,5},{2,6},{3,7},{8,12},{9,13},{10,14},{11,15},{16,20},{17,... | collective-permute-start | bytes 786440 | tf_op jit(solution)/shard_map/ppermute | solution.py:1171
  144.4 19.2 %collective-permute-start.1 = (bf16[1024,128]{1,0:T(8,128)(2,1)}, bf16[1024,128]{1,0:T(8,128)(2,1)S(1)}, u32[]{:S(2)}, u32[]{:S(2)}) collective-permute-start(bf16[1024,128]{1,0:T(8,128)(2,1)} %get-tuple-element.94), channel_id=1, source_target_pairs={{0,4},{1,5},{2,6},{3,7},{8,12},{9,13},{10,14},{11,15},{16,20},{17,... | collective-permute-start | bytes 786440 | tf_op jit(solution)/shard_map/ppermute | solution.py:1171
  174.9 14.5 %all-to-all-start = ((bf16[4,256,384]{1,2,0:T(8,128)(2,1)}), bf16[4,256,384]{1,2,0:T(8,128)(2,1)S(1)}, u32[]{:S(2)}, u32[]{:S(2)}) async-start(bf16[4,256,384]{1,2,0:T(8,128)(2,1)} %copy.48), calls=%async_computation | async-start | bytes 1572864 | tf_op jit(solution)/shard_map/all_to_all | solution.py:1285
  178.6 221.9 %reduce-scatter.3.cloned.1.call-start = ((), (), s32[]{:S(2)}) async-start(), calls=%async_computation.4 | async-start | bytes 3538944 | tf_op jit(solution)/shard_map/reduce_scatter | solution.py:1306
  260.9 33.6 %copy-start.47 = (pred[256]{0:T(512)(128)(4,1)}, pred[256]{0:T(512)(128)(4,1)S(1)}, u32[]{:S(2)}) copy-start(pred[256]{0:T(512)(128)(4,1)S(1)} %add_compare_fusion.1) | copy-start | bytes 772
  271.2 23.0 %copy-start.10 = (f32[256,1536]{1,0:T(8,128)S(1)}, f32[256,1536]{1,0:T(8,128)}, u32[]{:S(2)}) copy-start(f32[256,1536]{1,0:T(8,128)} %copy-done.9) | copy-start | bytes 4718596
  299.0 28.1 %collective-permute-start.5 = (bf16[1536,768]{1,0:T(8,128)(2,1)}, bf16[1536,768]{1,0:T(8,128)(2,1)}, u32[]{:S(2)}, u32[]{:S(2)}) collective-permute-start(bf16[1536,768]{1,0:T(8,128)(2,1)} %dynamic-slice_convert_fusion), channel_id=1, source_target_pairs={{0,2},{2,0},{1,3},{3,1},{4,6},{6,4},{5,7},{7,5},{8,10},{10,8},{9,1... | collective-permute-start | bytes 7077896 | tf_op jit(solution)/shard_map/ppermute | solution.py:1165
  302.6 29.4 %all-to-all-start.1 = ((bf16[256,4,384]{2,0,1:T(8,128)(2,1)}), bf16[256,4,384]{2,0,1:T(8,128)(2,1)}, u32[]{:S(2)}, u32[]{:S(2)}) async-start(bf16[256,4,384]{2,0,1:T(8,128)(2,1)} %bitcast.124), calls=%async_computation.1 | async-start | bytes 1572864 | tf_op jit(solution)/shard_map/all_to_all | solution.py:1316
  307.2 168.0 %reduce-scatter.5.cloned.1.call-start = ((), (), s32[]{:S(2)}) async-start(), calls=%async_computation.5 | async-start | bytes 7077888 | tf_op jit(solution)/shard_map/reduce_scatter | solution.py:1307
  346.0 33.7 %collective-permute-start.6 = (bf16[2,1024,128]{2,1,0:T(8,128)(2,1)}, bf16[2,1024,128]{2,1,0:T(8,128)(2,1)S(1)}, u32[]{:S(2)}, u32[]{:S(2)}) collective-permute-start(bf16[2,1024,128]{2,1,0:T(8,128)(2,1)} %get-tuple-element.118), channel_id=1, source_target_pairs={{4,0},{5,1},{6,2},{7,3},{12,8},{13,9},{14,10},{15,11},{20,16},{21,... | collective-permute-start | bytes 1572872 | tf_op jit(solution)/shard_map/ppermute | solution.py:1171
  361.4 57.5 %collective-permute-start.8 = (bf16[2,1024,128]{2,1,0:T(8,128)(2,1)}, bf16[2,1024,128]{2,1,0:T(8,128)(2,1)}, u32[]{:S(2)}, u32[]{:S(2)}) collective-permute-start(bf16[2,1024,128]{2,1,0:T(8,128)(2,1)} %get-tuple-element.128), channel_id=1, source_target_pairs={{4,0},{5,1},{6,2},{7,3},{12,8},{13,9},{14,10},{15,11},{20,16},{21,... | collective-permute-start | bytes 1572872 | tf_op jit(solution)/shard_map/ppermute | solution.py:1171
  362.7 36.6 %collective-permute-start.9 = (bf16[1536,384]{1,0:T(8,128)(2,1)S(1)}, bf16[1536,384]{1,0:T(8,128)(2,1)S(1)}, u32[]{:S(2)}, u32[]{:S(2)}) collective-permute-start(bf16[1536,384]{1,0:T(8,128)(2,1)S(1)} %dynamic-slice_convert_fusion.1), channel_id=1, source_target_pairs={{0,1},{1,0},{2,3},{3,2},{4,5},{5,4},{6,7},{7,6},{8,9},{9,8},{10,11... | collective-permute-start | bytes 3538952 | tf_op jit(solution)/shard_map/ppermute | solution.py:1165
  378.2 23.8 %collective-permute-start.10 = (bf16[2,1024,128]{2,1,0:T(8,128)(2,1)}, bf16[2,1024,128]{2,1,0:T(8,128)(2,1)}, u32[]{:S(2)}, u32[]{:S(2)}) collective-permute-start(bf16[2,1024,128]{2,1,0:T(8,128)(2,1)} %get-tuple-element.139), channel_id=1, source_target_pairs={{4,0},{5,1},{6,2},{7,3},{12,8},{13,9},{14,10},{15,11},{20,16},{21,... | collective-permute-start | bytes 1572872 | tf_op jit(solution)/shard_map/ppermute | solution.py:1171
  396.1 48.5 %copy-start.23 = (f32[1024,128]{1,0:T(8,128)}, f32[1024,128]{1,0:T(8,128)S(1)}, u32[]{:S(2)}) copy-start(f32[1024,128]{1,0:T(8,128)S(1)} %slice.104) | copy-start | bytes 1572868
  400.5 18.3 %collective-permute-start.7 = (bf16[128,1536]{1,0:T(8,128)(2,1)}, bf16[128,1536]{1,0:T(8,128)(2,1)S(1)}, u32[]{:S(2)}, u32[]{:S(2)}) collective-permute-start(bf16[128,1536]{1,0:T(8,128)(2,1)} %reduce-scatter.3.cloned.1.call-done), channel_id=1, source_target_pairs={{0,1},{1,0},{2,3},{3,2},{4,5},{5,4},{6,7},{7,6},{8,9},{9,8},{10,11... | collective-permute-start | bytes 1179656 | tf_op jit(solution)/shard_map/ppermute | solution.py:1165
  417.4 27.2 %copy-start.24 = (f32[1024,128]{1,0:T(8,128)}, f32[1024,128]{1,0:T(8,128)S(1)}, u32[]{:S(2)}) copy-start(f32[1024,128]{1,0:T(8,128)S(1)} %slice.106) | copy-start | bytes 1572868
  418.9 20.0 %copy-start.31 = (bf16[1024,128]{1,0:T(8,128)(2,1)S(1)}, bf16[1024,128]{1,0:T(8,128)(2,1)}, u32[]{:S(2)}) copy-start(bf16[1024,128]{1,0:T(8,128)(2,1)} %get-tuple-element.141) | copy-start | bytes 786436
  434.3 17.3 %collective-permute-start.11 = (f32[8,384]{1,0:T(8,128)S(1)}, f32[8,384]{1,0:T(8,128)S(1)}, u32[]{:S(2)}, u32[]{:S(2)}) collective-permute-start(f32[8,384]{1,0:T(8,128)S(1)} %pad_maximum_fusion.7), channel_id=1, source_target_pairs={{4,0},{5,1},{6,2},{7,3},{12,8},{13,9},{14,10},{15,11},{20,16},{21,... | collective-permute-start | bytes 36872 | tf_op jit(solution)/shard_map/ppermute | solution.py:1171
  475.1 91.5 %copy-start.11 = (f32[256,1536]{1,0:T(8,128)S(1)}, f32[256,1536]{1,0:T(8,128)}, u32[]{:S(2)}) copy-start(f32[256,1536]{1,0:T(8,128)} %copy-done.9) | copy-start | bytes 4718596
  475.2 91.5 %copy-start.48 = (pred[256]{0:T(512)(128)(4,1)S(1)}, pred[256]{0:T(512)(128)(4,1)}, u32[]{:S(2)}) copy-start(pred[256]{0:T(512)(128)(4,1)} %copy-done.47) | copy-start | bytes 772
  (58 other events, 323.1 us)
Sparse Core Ops, SparseCore 0:
  93.0 135.7 all-gather.2
  261.0 74.9 reduce-scatter.2
  339.6 120.9 reduce-scatter.4

commit v5 on v4

--- a/solution.py
+++ b/solution.py
@@ -84,7 +84,7 @@
 
 
 def prep_kernel(unroll, head, q_ref, k_ref, u_ref, rim_ref, kernel_ref, logits_ref,
-                w_ref, t_ref, qh_ref, kh_ref, p_ref, s_ref, kt_ref, ext_ref, mv_ref):
+                w_ref, t_ref, qh_ref, kh_ref, p_ref, s_ref, kt_ref, moved_ref, ext_ref, mv_ref):
     count = q_ref.shape[0]
     chunks = count // CH
     conv, scale = convolved(u_ref, rim_ref, kernel_ref, ext_ref)
@@ -117,7 +117,9 @@
     lax.fori_loop(0, chunks // unroll, step, 0)
     mv_ref[...] = kh_ref[...]
     for m in range(1, chunks):
-        mv_ref[0 : m * CH] = mm(mv_ref[0 : m * CH], p_ref[m * CH : (m + 1) * CH], 1, 1).astype(bf16)
+        cur = mv_ref[0 : m * CH]
+        moved_ref[m, 0 : m * CH] = cur
+        mv_ref[0 : m * CH] = mm(cur, p_ref[m * CH : (m + 1) * CH], 1, 1).astype(bf16)
     kt_ref[...] = mv_ref[...]
 
 
@@ -136,8 +138,7 @@
         rows = slice((m + 1) * CH, count)
         span = slice(m * CH, (m + 1) * CH)
         cur = q_ref[rows, :]
-        if save_ref is not None:
-            save_ref[m, rows, :] = cur
+        save_ref[m, rows, :] = cur
         s_ref[rows, span] = mm(cur, kh_ref[span, :], 1, 1)
         q_ref[rows, :] = mm(cur, p_ref[span, :]).astype(bf16)
 
@@ -155,10 +156,11 @@
     return e_local, e_remote, total
 
 
-def attend_kernel(far_ref, qh_ref, kh_ref, p_ref, s_in_ref, v_ref, kr_ref, vr_ref, o_ref, q_ref, s_ref):
+def attend_kernel(far_ref, qh_ref, kh_ref, p_ref, s_in_ref, v_ref, kr_ref, vr_ref,
+                  o_ref, pl_ref, pr_ref, save_ref, q_ref, s_ref):
     scale = CH ** -0.5
     far = far_ref[0]
-    walk_queries(qh_ref, kh_ref, p_ref, s_in_ref, q_ref, s_ref, None)
+    walk_queries(qh_ref, kh_ref, p_ref, s_in_ref, q_ref, s_ref, save_ref)
 
     count = qh_ref.shape[0]
 
@@ -167,6 +169,9 @@
         e_local, e_remote, total = strip_weights(scale, far, begin, near, q_ref, s_ref, kr_ref)
         summed = mm(e_local, v_ref[:near]) + mm(e_remote, vr_ref[...])
         o_ref[pl.ds(begin, CH), :] = (summed / total).astype(bf16)
+        inverse = 1.0 / total
+        pl_ref[pl.ds(begin, CH), :near] = (e_local * inverse).astype(bf16)
+        pr_ref[pl.ds(begin, CH), :] = (e_remote * inverse).astype(bf16)
         return carry
 
     middle = count // CH // 2
@@ -174,20 +179,17 @@
     lax.fori_loop(middle, count // CH, functools.partial(strip, count), 0)
 
 
-def attend_back_kernel(far_ref, qh_ref, kh_ref, p_ref, s_in_ref, v_ref, kr_ref, vr_ref, do_ref,
+def attend_back_kernel(kh_ref, p_ref, v_ref, kr_ref, vr_ref, do_ref, pl_ref, pr_ref, save_ref, q_ref,
                        dqh_ref, dkh_ref, dp_ref, ds_ref, dv_ref, dfar_ref,
-                       q_ref, s_ref, save_ref, pl_ref, pr_ref, dsl_ref, dsr_ref, dq_ref):
+                       dsl_ref, dsr_ref, dq_ref):
     scale = CH ** -0.5
-    far = far_ref[0]
-    count = qh_ref.shape[0]
+    count = kh_ref.shape[0]
     chunks = count // CH
-    walk_queries(qh_ref, kh_ref, p_ref, s_in_ref, q_ref, s_ref, save_ref)
 
     def strip(near, c, carry):
         begin = pl.multiple_of(c * CH, CH)
-        e_local, e_remote, total = strip_weights(scale, far, begin, near, q_ref, s_ref, kr_ref)
-        inverse = 1.0 / total
-        p_local, p_remote = e_local * inverse, e_remote * inverse
+        p_local = pl_ref[pl.ds(begin, CH), :near].astype(f32)
+        p_remote = pr_ref[pl.ds(begin, CH), :].astype(f32)
         do = do_ref[pl.ds(begin, CH), :]
         dp_local = mm(do, v_ref[:near], 1, 1)
         dp_remote = mm(do, vr_ref[...], 1, 1)
@@ -196,8 +198,6 @@
         )
         d_local = p_local * (dp_local - delta) * scale
         d_remote = (p_remote * (dp_remote - delta) * scale).astype(bf16)
-        pl_ref[pl.ds(begin, CH), :near] = p_local.astype(bf16)
-        pr_ref[pl.ds(begin, CH), :] = p_remote.astype(bf16)
         dsl_ref[pl.ds(begin, CH), :near] = d_local.astype(bf16)
         dsr_ref[pl.ds(begin, CH), :] = d_remote
         dq_ref[pl.ds(begin, CH), :] = mm(d_remote, kr_ref[...])
@@ -233,20 +233,19 @@
 
 
 def prep_back_kernel(unroll, head, q_ref, k_ref, u_ref, rim_ref, kernel_ref, logits_ref,
-                     w_ref, t_ref, kh_ref, p_ref, ds_ref, dqh_ref, dkh_ref, dp_ref, dv_ref,
-                     dfar_ref,
-                     gq_ref, gk_ref, gv_ref, gu_ref, glog_ref, gker_ref,
-                     ext_ref, mv_ref, save_ref, dk_ref, dps_ref, dw_ref, dc_ref):
+                     w_ref, t_ref, save_ref, p_ref, ds_ref, dqh_ref, dkh_ref, dp_ref, dv_ref,
+                     dfar_ref, *rest):
+    (grads_ref, rim_out_ref, tail_ref, glog_ref, gker_ref, gq_ref, gk_ref, gv_ref, gu_ref,
+     ext_ref, dk_ref, dps_ref, dw_ref, dc_ref, sems) = rest[-15:]
+    heads = grads_ref.shape[1] // CH // 4
+
+    def out_copy(kind, ref):
+        place = grads_ref.at[:, pl.ds((kind * heads + head) * CH, CH)]
+        return pltpu.make_async_copy(ref, place, sems.at[kind])
+
     count = q_ref.shape[0]
     chunks = count // CH
     strict, upto = tri(True), tri(False)
-    mv_ref[...] = kh_ref[...]
-    for m in range(1, chunks):
-        rows = slice(0, m * CH)
-        cur = mv_ref[rows, :]
-        save_ref[m, rows, :] = cur
-        if m < chunks - 1:
-            mv_ref[rows, :] = mm(cur, p_ref[m * CH : (m + 1) * CH, :], 1, 1).astype(bf16)
     dk_ref[...] = dfar_ref[0].astype(f32)
     dps_ref[...] = dp_ref[...]
     for m in range(chunks - 1, 0, -1):
@@ -257,6 +256,7 @@
         dk_ref[rows, :] = mm(d_new, p_ref[span, :])
     dk_ref[...] = dk_ref[...] + dkh_ref[...]
     gv_ref[...] = (dv_ref[...] + dfar_ref[1].astype(f32)).astype(bf16)
+    out_copy(2, gv_ref).start()
     ones = jnp.ones((8, CH), f32)
 
     def chunk(start):
@@ -300,6 +300,8 @@
         return carry
 
     lax.fori_loop(0, chunks // unroll, step, 0)
+    out_copy(0, gq_ref).start()
+    out_copy(1, gk_ref).start()
     conv, scale = convolved(u_ref, rim_ref, kernel_ref, ext_ref)
     unit = conv * scale
     dw = dw_ref[...]
@@ -313,7 +315,12 @@
     for lag in range(1, 4):
         total = total + kernel_ref[lag : lag + 1] * dc_ref[pl.ds(lag, count + 8)]
         gker_ref[lag : lag + 1] = jnp.sum(d_conv * ext_ref[pl.ds(8 - lag, count)], 0, keepdims=True)
-    gu_ref[...] = total
+    gu_ref[...] = total[8:].astype(bf16)
+    out_copy(3, gu_ref).start()
+    rim_out_ref[...] = total[:8]
+    tail_ref[...] = total[count:]
+    for kind, ref in enumerate((gq_ref, gk_ref, gv_ref, gu_ref)):
+        out_copy(kind, ref).wait()
 
 
 def params():
@@ -341,8 +348,9 @@
         grid=(1,),
         in_specs=[column(count, head), column(count, heads + head), column(count, 3 * heads + head),
                   column(8, head), column(8, head), whole((count, CH))],
-        out_specs=[whole((count, CH))] * 7,
-        out_shape=[sq, sq, sq, sq, sq, jax.ShapeDtypeStruct((count, CH), f32), sq],
+        out_specs=[whole((count, CH))] * 7 + [whole((count // CH, count, CH))],
+        out_shape=[sq, sq, sq, sq, sq, jax.ShapeDtypeStruct((count, CH), f32), sq,
+                   jax.ShapeDtypeStruct((count // CH, count, CH), bf16)],
         scratch_shapes=[pltpu.VMEM((count + 8, CH), f32), pltpu.VMEM((count, CH), bf16)],
         compiler_params=params(), name="prep",
         cost_estimate=estimate(count * 10**7, count * 4096),
@@ -353,21 +361,24 @@
     count = qh.shape[0]
     fc = kr.shape[0]
     c = whole((count, CH))
+    steps = (count // CH - 1, count, CH)
+    sq = jax.ShapeDtypeStruct((count, CH), bf16)
     return pl.pallas_call(
         attend_kernel,
         grid=(1,),
         in_specs=[pl.BlockSpec(memory_space=pltpu.SMEM), c, c, c, c, column(count, 2 * heads + head),
                   whole((fc, CH)), column(fc, head)],
-        out_specs=c,
-        out_shape=jax.ShapeDtypeStruct((count, CH), bf16),
-        scratch_shapes=[pltpu.VMEM((count, CH), bf16), pltpu.VMEM((count, count), f32)],
+        out_specs=[c, whole((count, count)), whole((count, fc)), whole(steps), c],
+        out_shape=[sq, jax.ShapeDtypeStruct((count, count), bf16), jax.ShapeDtypeStruct((count, fc), bf16),
+                   jax.ShapeDtypeStruct(steps, bf16), sq],
+        scratch_shapes=[pltpu.VMEM((count, count), f32)],
         compiler_params=params(), name="attend",
         cost_estimate=estimate(count * 10**7, count * 4096),
     )(far, qh, kh, p, s_in, projected, kr, vr)
 
 
-def attend_back(far, qh, kh, p, s_in, projected, kr, vr, d_attn, head, heads):
-    count = qh.shape[0]
+def attend_back(kh, p, projected, kr, vr, d_attn, probs, far_probs, walked, q_last, head, heads):
+    count = kh.shape[0]
     fc = kr.shape[0]
     c = whole((count, CH))
     r = whole((fc, CH))
@@ -376,41 +387,42 @@
     return pl.pallas_call(
         attend_back_kernel,
         grid=(1,),
-        in_specs=[pl.BlockSpec(memory_space=pltpu.SMEM), c, c, c, c, column(count, 2 * heads + head),
-                  r, column(fc, head), column(count, head)],
+        in_specs=[c, c, column(count, 2 * heads + head), r, column(fc, head), column(count, head),
+                  whole((count, count)), whole((count, fc)), whole((count // CH - 1, count, CH)), c],
         out_specs=[c, c, c, c, c, whole((2, fc, CH))],
         out_shape=[w32, w32, w32, jax.ShapeDtypeStruct((count, CH), bf16), w32, far16],
-        scratch_shapes=[pltpu.VMEM((count, CH), bf16), pltpu.VMEM((count, count), f32),
-                        pltpu.VMEM((count // CH - 1, count, CH), bf16),
-                        pltpu.VMEM((count, count), bf16), pltpu.VMEM((count, fc), bf16),
-                        pltpu.VMEM((count, count), bf16), pltpu.VMEM((count, fc), bf16),
+        scratch_shapes=[pltpu.VMEM((count, count), bf16), pltpu.VMEM((count, fc), bf16),
                         pltpu.VMEM((count, CH), f32)],
         compiler_params=params(), name="attend_back",
         cost_estimate=estimate(count * 3 * 10**7, count * 8192),
-    )(far, qh, kh, p, s_in, projected, kr, vr, d_attn)
-
-
-def prep_back(projected, rim, kernel, logits, w, t, kh, p, ds, dqh, dkh, dp, dv, dfar, head, heads):
+    )(kh, p, projected, kr, vr, d_attn, probs, far_probs, walked, q_last)
+
+
+def prep_back(projected, rim, kernel, logits, w, t, moved, p, ds, dqh, dkh, dp, dv, dfar, grads, head, heads):
     count = projected.shape[0]
     c = whole((count, CH))
-    sq = jax.ShapeDtypeStruct((count, CH), bf16)
     chunks = count // CH
     unroll = 8 if count % (8 * CH) == 0 else 2
+    anywhere = pl.BlockSpec(memory_space=pl.ANY)
+    shape = jax.ShapeDtypeStruct
+    own = pltpu.VMEM((count, CH), bf16)
+    more = [] if grads is None else [grads]
     return pl.pallas_call(
         functools.partial(prep_back_kernel, unroll, head),
         grid=(1,),
         in_specs=[column(count, head), column(count, heads + head), column(count, 3 * heads + head),
-                  column(8, head), column(8, head), c] + [c] * 9 + [whole((2, count, CH))],
-        out_specs=[c, c, c, whole((count + 8, CH)), whole((chunks, CH)), whole((8, CH))],
-        out_shape=[sq, sq, sq, jax.ShapeDtypeStruct((count + 8, CH), f32),
-                   jax.ShapeDtypeStruct((chunks, CH), f32), jax.ShapeDtypeStruct((8, CH), f32)],
-        scratch_shapes=[pltpu.VMEM((count + 8, CH), f32), pltpu.VMEM((count, CH), bf16),
-                        pltpu.VMEM((chunks, count, CH), bf16), pltpu.VMEM((count, CH), f32),
+                  column(8, head), column(8, head), c, c, c, whole((chunks, count, CH))] + [c] * 6
+                 + [whole((2, count, CH))] + [anywhere] * len(more),
+        out_specs=[anywhere, whole((8, CH)), whole((8, CH)), whole((chunks, CH)), whole((8, CH))],
+        out_shape=[shape((count, 4 * heads * CH), bf16), shape((8, CH), f32), shape((8, CH), f32),
+                   shape((chunks, CH), f32), shape((8, CH), f32)],
+        scratch_shapes=[own, own, own, own, pltpu.VMEM((count + 8, CH), f32), pltpu.VMEM((count, CH), f32),
                         pltpu.VMEM((count, CH), f32), pltpu.VMEM((count, CH), f32),
-                        pltpu.VMEM((count + 16, CH), f32)],
+                        pltpu.VMEM((count + 16, CH), f32), pltpu.SemaphoreType.DMA((4,))],
+        input_output_aliases={16: 0} if more else {},
         compiler_params=params(), name="prep_back",
         cost_estimate=estimate(count * 3 * 10**7, count * 8192),
-    )(projected, projected, projected, rim, kernel, logits, w, t, kh, p, ds, dqh, dkh, dp, dv, dfar)
+    )(projected, projected, projected, rim, kernel, logits, w, t, moved, p, ds, dqh, dkh, dp, dv, dfar, *more)
 
 
 MESH = pl.DeviceIdType.MESH
@@ -1275,13 +1287,13 @@
                 keys = move_keys(keys.astype(f32), transforms.astype(f32)).astype(bf16)
         kept.append(hops)
     far_keys = [jnp.concatenate(hops, 0) for hops in kept]
-    attn = []
+    attended = []
     for head in range(local):
-        _, _, qh, kh, p, s_in, _ = prepared[head]
-        attn.append(
+        _, _, qh, kh, p, s_in, _, _ = prepared[head]
+        attended.append(
             attend(far, qh, kh, p, s_in, projected, far_keys[head], far_values, head, local)
         )
-    attn = jnp.concatenate(attn, axis=1)
+    attn = jnp.concatenate([parts[0] for parts in attended], axis=1)
     back = lax.all_to_all(attn, ("cc", "seq"), split_axis=0, concat_axis=1, tiled=True)
     tokens = own16.astype(f32)
     x_mid = tokens + jnp.dot(back, wide_out, preferred_element_type=f32)
@@ -1315,25 +1327,27 @@
     d_back = jnp.einsum("te,de->td", d_branch, wide_out, preferred_element_type=f32).astype(bf16)
     d_attn = lax.all_to_all(d_back, ("cc", "seq"), split_axis=1, concat_axis=0, tiled=True)
     d_attn, other_part = lax.optimization_barrier((d_attn, other_part))
-    out_part = own_part + swapped(other_part, "seq").astype(f32)
+    upper = other_part.shape[0] // 2
+    late = [swapped(other_part[:upper], "seq"), swapped(other_part[upper:], "seq"), swapped(down_sum, "seq")]
 
     backs = []
     for head in range(local):
-        _, _, qh, kh, p, s_in, _ = prepared[head]
-        backs.append(
-            attend_back(
-                far, qh, kh, p, s_in, projected, far_keys[head], far_values, d_attn, head, local
-            )
-        )
-    down_both = in_order(down_sum, swapped(down_sum, "seq"), seq)
-    middle = min(1, local - 1)
-    first, down_both = lax.optimization_barrier((backs[middle][0], down_both))
-    backs[middle] = [first] + list(backs[middle][1:])
-    first, out_part = lax.optimization_barrier((backs[-1][0], out_part))
-    backs[-1] = [first] + list(backs[-1][1:])
-    pieces, logit_rows, kernel_rows = [], [], []
+        if head:
+            at = min(head, 2) - 1
+            d_attn, dv, late[at] = lax.optimization_barrier((d_attn, backs[-1][4], late[at]))
+            backs[-1] = backs[-1][:4] + [dv] + backs[-1][5:]
+        kh, p = prepared[head][3], prepared[head][4]
+        backs.append(list(
+            attend_back(kh, p, projected, far_keys[head], far_values, d_attn, *attended[head][1:], head, local)
+        ))
+    first, last, late[2] = lax.optimization_barrier((backs[0][0], backs[-1][1], late[2]))
+    backs[-1] = backs[-1][:1] + [last] + backs[-1][2:]
+    backs[0] = [first] + backs[0][1:]
+    out_part = own_part + jnp.concatenate(late[:2], axis=0).astype(f32)
+    down_both = in_order(down_sum, late[2], seq)
+    grads, rims, tails, logit_rows, kernel_rows = None, [], [], [], []
     for head in range(local):
-        w, t, _, kh, p, _, _ = prepared[head]
+        w, t, _, _, p, _, _, moved = prepared[head]
         dqh, dkh, dp, ds, dv, dfars = backs[head]
         outgoing = None
         for hop in reversed(range(1, cy_size)):
@@ -1347,25 +1361,21 @@
                 dp = dp + d_transform
             outgoing = d_both
         dfar = passed_along(outgoing, "cy", -1)
-        gq, gk, gv, gu, glog, gker = prep_back(
-            projected, rim, kernel, logits, w, t, kh, p, ds, dqh, dkh, dp, dv, dfar, head, local
+        grads, rim_part, tail, glog, gker = prep_back(
+            projected, rim, kernel, logits, w, t, moved, p, ds, dqh, dkh, dp, dv, dfar, grads, head, local
         )
-        pieces.append((gq, gk, gv, gu))
+        rims.append(rim_part)
+        tails.append(tail)
         logit_rows.append(glog.reshape(1, span))
         kernel_rows.append(gker[:taps])
-    d_rim = jnp.concatenate([piece[3][:8] for piece in pieces], axis=1)
-    rim_back = passed_along(d_rim, "cy", -1)
-    d_raw = jnp.concatenate([piece[3][8:] for piece in pieces], axis=1)
-    d_raw = jnp.concatenate([d_raw[: span - 8], d_raw[span - 8 :] + rim_back], axis=0).astype(bf16)
-    d_projected = jnp.concatenate(
-        [piece[0] for piece in pieces] + [piece[1] for piece in pieces] + [piece[2] for piece in pieces] + [d_raw],
-        axis=1,
-    )
+    rim_back = passed_along(jnp.concatenate(rims, axis=1), "cy", -1)
+    tail = (jnp.concatenate(tails, axis=1) + rim_back).astype(bf16)
+    d_projected = lax.dynamic_update_slice(grads, tail, (span - 8, 3 * features))
     d_logits = jnp.concatenate(logit_rows, axis=0).astype(bf16)
     qkvu_term = jnp.einsum("td,tn->dn", h_first, d_projected, preferred_element_type=f32)
     beta_term = jnp.einsum("td,ht->dh", h_first, d_logits, preferred_element_type=f32)
     d_h_first = jnp.einsum("tn,dn->td", d_projected, wide_qkvu, preferred_element_type=f32)
-    d_h_first = d_h_first + jnp.einsum("ht,hd->td", d_logits, beta_local, preferred_element_type=f32)
+    d_h_first = d_h_first + jnp.einsum("ht,hd->td", d_logits, beta_local, preferred_element_type=f32).astype(bf16)
     normed = rms_norm(span_input.astype(f32), 1.0)
     gain_one_term = jnp.sum(d_h_first * normed, 0)
 

time: 592 us -> 585 us (0.988)
  local copies, waits for them, and re-layouts: 48.2 us -> 32.7 us
    ppermute x9, waiting for transfers between devices: 1.33 us -> 13.6 us  [passed_along(): lax.ppermute(value, axis, [(source, source + steps) for source in range(l...]
    unnamed x144 -> x133, local copies, waits for them, and re-layouts: 31.8 us -> 22.6 us
    all_gather x1, waiting for transfers between devices: 12.1 us -> 5.77 us  [per_device(): both = lax.all_gather(gate_up_pair, all_axes, axis=0, tiled=False)]
    slice x7 -> x1, local copies, waits for them, and re-layouts: 6.37 us -> 0.12 us  [per_device(): other_part[upper:]]
  transfers between devices with their start and end apart: 17 -> 18, of which waited for: 3 -> 3; matrix products, arithmetic and copies ran while one was open for 19% -> 16% of each run, Pallas kernels for 30% -> 31%
where the time goes in v5:
time: 585 us; the launch traced here: 579 us
  Pallas kernels  362 us (62%)
  matrix products  85 us (15%)
  local copies, waits for them, and re-layouts  32.7 us (6%)
  other arithmetic  31.1 us (5%)
  starting transfers between devices  26.6 us (5%)
  waiting for transfers between devices  26.2 us (4%)
  between operations  15.6 us (3%)
    pallas_call x1, Pallas kernels, scatter_last(): pl.pallas_call(functools.partial(scatter_kernel, row_count, y_count, feat...  90.3 us
    pallas_call x1, Pallas kernels, gather_first(): pl.pallas_call(functools.partial(gather_kernel, row_count, y_count, featu...  79.3 us
    pallas_call x3, Pallas kernels, prep_back(): pl.pallas_call(functools.partial(prep_back_kernel, unroll, head), grid=(1...  41.7 us
    pallas_call x3, Pallas kernels, attend_back(): pl.pallas_call(attend_back_kernel, grid=(1,), in_specs=[c, c, column(coun...  39.1 us
    pallas_call x3, Pallas kernels, attend(): pl.pallas_call(attend_kernel, grid=(1,), in_specs=[pl.BlockSpec(memory_sp...  29.5 us
    pallas_call x3, Pallas kernels, prep(): pl.pallas_call(functools.partial(prep_kernel, unroll, head), grid=(1,), i...  27.3 us
    pallas_call x1, Pallas kernels, group_sum(): pl.pallas_call(group_sum_kernel, in_specs=[pl.BlockSpec(memory_space=pltp...  22.8 us
    unnamed x133, local copies, waits for them, and re-layouts  22.6 us
  transfers between devices with their start and end apart: 18, of which 3 were waited for; matrix products, arithmetic and copies ran while one was open for 16% of the time, Pallas kernels for 31%

profile of v5, /device:TPU:1, one launch (start us, length us, event | category | flops | bytes accessed | tf_op | source)
XLA Modules:
  0.0 579.4 jit_solution(11485756009142245099)
XLA Ops:
  13.6 79.3 %gather_first.1 = (bf16[4,2,2,96,1536]{4,3,2,1,0:T(8,128)(2,1)}, bf16[4,2,2,32,128]{4,3,2,1,0:T(8,128)(2,1)S(1)}, bf16[4,2,2,96,1536]{4,3,2,1,0:T(8,128)(2,1)}, ...) custom-call(bf16[96,6144]{1,0:T(8,128)(2,1)S(1)} %copy-done.5, ...), custom_call_target="tpu_custom_call" | custom-call | tf_op jit(solution)/shard_map/gather_first/pallas_call | solution.py:665
  115.9 9.1 %prep.5 = (bf16[1024,128]{1,0:T(8,128)(2,1)}, bf16[1024,128]{1,0:T(8,128)(2,1)}, bf16[1024,128]{1,0:T(8,128)(2,1)}, bf16[1024,128]{1,0:T(8,128)(2,1)}, bf16[1024...) custom-call(bf16[1024,1536]{1,0:T(8,128)(2,1)} %copy-done.30, ...), custom_call_target="tpu_custom_call" | custom-call | flops 10240000000 | bytes 4194304 | tf_op jit(solution)/shard_map/prep/pallas_call | solution.py:346
  126.3 9.1 %prep.4 = (bf16[1024,128]{1,0:T(8,128)(2,1)}, bf16[1024,128]{1,0:T(8,128)(2,1)}, bf16[1024,128]{1,0:T(8,128)(2,1)}, bf16[1024,128]{1,0:T(8,128)(2,1)}, bf16[1024...) custom-call(bf16[1024,1536]{1,0:T(8,128)(2,1)} %copy-done.30, ...), custom_call_target="tpu_custom_call" | custom-call | flops 10240000000 | bytes 4194304 | tf_op jit(solution)/shard_map/prep/pallas_call | solution.py:346
  136.9 9.1 %prep.3 = (bf16[1024,128]{1,0:T(8,128)(2,1)}, bf16[1024,128]{1,0:T(8,128)(2,1)}, bf16[1024,128]{1,0:T(8,128)(2,1)}, bf16[1024,128]{1,0:T(8,128)(2,1)}, bf16[1024...) custom-call(bf16[1024,1536]{1,0:T(8,128)(2,1)} %copy-done.30, ...), custom_call_target="tpu_custom_call" | custom-call | flops 10240000000 | bytes 4194304 | tf_op jit(solution)/shard_map/prep/pallas_call | solution.py:346
  148.0 10.2 %attend.5 = (bf16[1024,128]{1,0:T(8,128)(2,1)}, bf16[1024,1024]{1,0:T(8,128)(2,1)}, bf16[1024,1024]{1,0:T(8,128)(2,1)}, bf16[7,1024,128]{2,1,0:T(8,128)(2,1)}, bf16[1024,128]{1,0:T(8,128)(2,1)}) custom-call(s32[1]{0:T(128)} %bitcast.2.far_ref, bf16[1024,128]{1,0:T(8,128)(2,1)} %get-tuple-element.122.qh_ref, bf16[1024,128]{1,0:T(8,128)(2,1)} %get-tuple-element.123.kh_ref, ...), custom_call_target="tpu_custom_call" | custom-call | flops 10240000000 | bytes 4194304 | tf_op jit(solution)/shard_map/attend/pallas_call | solution.py:366
  158.9 9.6 %attend.4 = (bf16[1024,128]{1,0:T(8,128)(2,1)}, bf16[1024,1024]{1,0:T(8,128)(2,1)}, bf16[1024,1024]{1,0:T(8,128)(2,1)}, bf16[7,1024,128]{2,1,0:T(8,128)(2,1)}, bf16[1024,128]{1,0:T(8,128)(2,1)}) custom-call(s32[1]{0:T(128)} %bitcast.2.far_ref, bf16[1024,128]{1,0:T(8,128)(2,1)} %get-tuple-element.116.qh_ref, bf16[1024,128]{1,0:T(8,128)(2,1)} %get-tuple-element.117.kh_ref, ...), custom_call_target="tpu_custom_call" | custom-call | flops 10240000000 | bytes 4194304 | tf_op jit(solution)/shard_map/attend/pallas_call | solution.py:366
  169.3 9.7 %attend.3 = (bf16[1024,128]{1,0:T(8,128)(2,1)}, bf16[1024,1024]{1,0:T(8,128)(2,1)}, bf16[1024,1024]{1,0:T(8,128)(2,1)}, bf16[7,1024,128]{2,1,0:T(8,128)(2,1)}, bf16[1024,128]{1,0:T(8,128)(2,1)}) custom-call(s32[1]{0:T(128)} %bitcast.2.far_ref, bf16[1024,128]{1,0:T(8,128)(2,1)} %get-tuple-element.110.qh_ref, bf16[1024,128]{1,0:T(8,128)(2,1)} %get-tuple-element.111.kh_ref, ...), custom_call_target="tpu_custom_call" | custom-call | flops 10240000000 | bytes 4194304 | tf_op jit(solution)/shard_map/attend/pallas_call | solution.py:366
  201.2 21.8 %group_gather.1 = bf16[4,256,1536]{2,1,0:T(8,128)(2,1)S(1)} custom-call(bf16[256,1536]{1,0:T(8,128)(2,1)S(1)} %multiply_convert_fusion.5.x_ref), custom_call_target="tpu_custom_call" | custom-call | tf_op jit(solution)/shard_map/group_gather/pallas_call | solution.py:1072
  228.9 10.3 %unpack.1 = (bf16[1536,2048]{1,0:T(8,128)(2,1)}, bf16[1024,1536]{1,0:T(8,128)(2,1)}) custom-call(bf16[8,4608,128]{2,1,0:T(8,128)(2,1)} %bitcast.123), custom_call_target="tpu_custom_call" | custom-call | bytes 18874368 | tf_op jit(solution)/shard_map/unpack/pallas_call | solution.py:1166
  239.2 9.0 %fusion.39 = f32[1024,2048]{0,1:T(8,128)S(1)} fusion(bf16[1024,1536]{1,0:T(8,128)(2,1)S(1)} %bitcast.110, bf16[1536,2048]{1,0:T(8,128)(2,1)} %get-tuple-element.135), kind=kOutput, calls=%fused_computation.114 | convolution fusion | flops 6442450944 | bytes 17825792 | tf_op jit(solution)/shard_map/dot_general | solution.py:1301
  260.9 10.2 %fusion.2 = f32[1024,1536]{1,0:T(8,128)S(1)} fusion(bf16[1536,2048]{1,0:T(8,128)(2,1)} %get-tuple-element.135, bf16[1024,1024]{0,1:T(8,128)(2,1)} %get-tuple-element.233, bf16[1024,1024]{0,1:T(8,128)(2,1)} %get-tuple-element.232), kind=kOutput, calls=%fused_computation.26 | convolution fusion | flops 6450839552 | bytes 16777216 | tf_op jit(solution)/shard_map/tf,df->td/dot_general | solution.py:1314
  271.1 22.8 %group_sum.1 = f32[256,1536]{1,0:T(8,128)S(1)} custom-call(f32[4,256,1536]{2,1,0:T(8,128)S(1)} %bitcast.109), custom_call_target="tpu_custom_call" | custom-call | tf_op jit(solution)/shard_map/group_sum/pallas_call | solution.py:1138
  307.5 11.0 %convolution_convert_fusion.1 = bf16[1536,2048]{1,0:T(8,128)(2,1)} fusion(bf16[1024,1536]{1,0:T(8,128)(2,1)S(1)} %bitcast.111, bf16[1024,1024]{0,1:T(8,128)(2,1)} %get-tuple-element.233, bf16[1024,1024]{0,1:T(8,128)(2,1)} %get-tuple-element.232), kind=kOutput, calls=%fused_computation.1 | convolution fusion | flops 6453985280 | bytes 13631488 | tf_op jit(solution)/shard_map/td,tf->df/dot_general | solution.py:1317
  320.1 7.1 %convolution_convert_fusion.4 = bf16[1024,1536]{1,0:T(8,128)(2,1)} fusion(bf16[1024,1024]{0,1:T(8,128)(2,1)S(1)} %copy-done.55, bf16[1024,1536]{1,0:T(8,128)(2,1)} %get-tuple-element.134), kind=kOutput, calls=%fused_computation.19 | convolution fusion | flops 3222798336 | bytes 8388608 | tf_op jit(solution)/shard_map/dot_general | solution.py:1307
  333.7 12.9 %attend_back.3 = (f32[1024,128]{1,0:T(8,128)}, f32[1024,128]{1,0:T(8,128)}, f32[1024,128]{1,0:T(8,128)}, bf16[1024,128]{1,0:T(8,128)(2,1)}, f32[1024,128]{1,0:T(8,128)}, /*index=5*/bf16[2,1024,128]{2,1,0:T(8,128)(2,1)}) custom-call(bf16[1024,128]{1,0:T(8,128)(2,1)} %get-tuple-element.111.kh_ref, bf16[1024,128]{1,0:T(8,128)(2,1)} %get-tuple-element.112.p_ref, ...), custom_call_target="tpu_custom_call" | custom-call | flops 30720000000 | bytes 8388608 | tf_op jit(solution)/shard_map/attend_back/pallas_call | solution.py:387
  348.0 13.3 %attend_back.4 = (f32[1024,128]{1,0:T(8,128)}, f32[1024,128]{1,0:T(8,128)}, f32[1024,128]{1,0:T(8,128)}, bf16[1024,128]{1,0:T(8,128)(2,1)}, f32[1024,128]{1,0:T(8,128)}, /*index=5*/bf16[2,1024,128]{2,1,0:T(8,128)(2,1)}) custom-call(bf16[1024,128]{1,0:T(8,128)(2,1)} %get-tuple-element.117.kh_ref, bf16[1024,128]{1,0:T(8,128)(2,1)} %get-tuple-element.118.p_ref, ...), custom_call_target="tpu_custom_call" | custom-call | flops 30720000000 | bytes 8388608 | tf_op jit(solution)/shard_map/attend_back/pallas_call | solution.py:387
  362.7 13.0 %attend_back.5 = (f32[1024,128]{1,0:T(8,128)}, f32[1024,128]{1,0:T(8,128)}, f32[1024,128]{1,0:T(8,128)}, bf16[1024,128]{1,0:T(8,128)(2,1)}, f32[1024,128]{1,0:T(8,128)}, /*index=5*/bf16[2,1024,128]{2,1,0:T(8,128)(2,1)}) custom-call(bf16[1024,128]{1,0:T(8,128)(2,1)} %get-tuple-element.123.kh_ref, bf16[1024,128]{1,0:T(8,128)(2,1)} %get-tuple-element.124.p_ref, ...), custom_call_target="tpu_custom_call" | custom-call | flops 30720000000 | bytes 8388608 | tf_op jit(solution)/shard_map/attend_back/pallas_call | solution.py:387
  380.9 13.8 %prep_back.3 = (bf16[1024,1536]{1,0:T(8,128)(2,1)}, f32[8,128]{1,0:T(8,128)}, f32[8,128]{1,0:T(8,128)}, f32[8,128]{1,0:T(8,128)}, f32[8,128]{1,0:T(8,128)}) custom-call(bf16[1024,1536]{1,0:T(8,128)(2,1)} %copy-done.30, bf16[1024,1536]{1,0:T(8,128)(2,1)} %copy-done.30, bf16[1024,1536]{1,0:T(8,128)(2,1)} %copy-done.30, bf16[8,384]{1,0:T(8,128)(2,1)} %copy-done.53, ...), custom_call_target="tpu_custom_call" | custom-call | flops 30720000000 | bytes 8388608 | tf_op jit(solution)/shard_map/prep_back/pallas_call | solution.py:410
  394.7 13.6 %collective-permute-done.10.dfar_ref = bf16[2,1024,128]{2,1,0:T(8,128)(2,1)} collective-permute-done((bf16[2,1024,128]{2,1,0:T(8,128)(2,1)S(1)}, bf16[2,1024,128]{2,1,0:T(8,128)(2,1)}, u32[]{:S(2)}, u32[]{:S(2)}) %collective-permute-start.10) | collective-permute-done | bytes 524320 | tf_op jit(solution)/shard_map/ppermute | solution.py:1183
  408.3 13.8 %prep_back.4 = (bf16[1024,1536]{1,0:T(8,128)(2,1)}, f32[8,128]{1,0:T(8,128)}, f32[8,128]{1,0:T(8,128)}, f32[8,128]{1,0:T(8,128)}, f32[8,128]{1,0:T(8,128)}) custom-call(bf16[1024,1536]{1,0:T(8,128)(2,1)} %copy-done.30, bf16[1024,1536]{1,0:T(8,128)(2,1)} %copy-done.30, bf16[1024,1536]{1,0:T(8,128)(2,1)} %copy-done.30, ...), custom_call_target="tpu_custom_call", output_to_operand_aliasing={{0}: (16, {})} | custom-call | flops 30720000000 | bytes 8388608 | tf_op jit(solution)/shard_map/prep_back/pallas_call | solution.py:410
  422.9 14.0 %prep_back.5 = (bf16[1024,1536]{1,0:T(8,128)(2,1)}, f32[8,128]{1,0:T(8,128)}, f32[8,128]{1,0:T(8,128)}, f32[8,128]{1,0:T(8,128)}, f32[8,128]{1,0:T(8,128)}) custom-call(bf16[1024,1536]{1,0:T(8,128)(2,1)} %copy-done.30, bf16[1024,1536]{1,0:T(8,128)(2,1)} %copy-done.30, bf16[1024,1536]{1,0:T(8,128)(2,1)} %copy-done.30, ...), custom_call_target="tpu_custom_call", output_to_operand_aliasing={{0}: (16, {})} | custom-call | flops 30720000000 | bytes 8388608 | tf_op jit(solution)/shard_map/prep_back/pallas_call | solution.py:410
  447.7 10.0 %fusion = (bf16[1024,1536]{1,0:T(8,128)(2,1)}, bf16[1536]{0:T(1024)(128)(2,1)S(1)}) fusion(bf16[1024,1536]{1,0:T(8,128)(2,1)} %convolution_convert_fusion.2, f32[1024]{0:T(1024)S(1)} %bitcast.140, bf16[4,256,1536]{2,1,0:T(8,128)(2,1)S(1)} %copy-done.13, bf16[1024,1536]{1,0:T(8,128)(2,1)} %fusion.29, bf16[1536,1536]{1,0:T(8,128)(2,1)} %bitcast.144), kind=kOutput, calls=%fused_computation.10 | convolution fusion | flops 4842846720 | bytes 17308672 | tf_op jit(solution)/shard_map/tn,dn->td/dot_general | solution.py:1377
  458.9 9.3 %convolution_convert_fusion = bf16[1536,1536]{1,0:T(8,128)(2,1)} fusion(bf16[1024,1536]{1,0:T(8,128)(2,1)} %copy-done.14, bf16[1024,1536]{1,0:T(8,128)(2,1)} %fusion.29), kind=kOutput, calls=%fused_computation | convolution fusion | flops 4834197504 | bytes 11010048 | tf_op jit(solution)/shard_map/td,tn->dn/dot_general | solution.py:1375
  468.2 90.3 %scatter_last.1 = (bf16[96,6144]{1,0:T(8,128)(2,1)}, bf16[4,96,128]{2,1,0:T(8,128)(2,1)}, bf16[4,96,384]{2,1,0:T(8,128)(2,1)}, bf16[96,8192]{1,0:T(8,128)(2,1)},...) custom-call(bf16[8,192,1536]{2,1,0:T(8,128)(2,1)} %bitcast.125, bf16[8,192,128]{2,1,0:T(8,128)(2,1)} %bitcast.131, ...), custom_call_target="tpu_custom_call" | custom-call | tf_op jit(solution)/shard_map/scatter_last/pallas_call | solution.py:1018
  (248 shorter events, 131.4 us)
Async XLA Ops:
  7.2 221.7 %all-gather.3.cloned.1.call-start = ((), (), s32[]{:S(2)}) async-start(), calls=%async_computation.6 | async-start | bytes 10616832 | tf_op jit(solution)/shard_map/all_gather | solution.py:1251
  103.4 11.9 %collective-permute-start = (bf16[8,384]{1,0:T(8,128)(2,1)S(1)}, bf16[8,384]{1,0:T(8,128)(2,1)S(1)}, u32[]{:S(2)}, u32[]{:S(2)}) collective-permute-start(bf16[8,384]{1,0:T(8,128)(2,1)S(1)} %slice.99), channel_id=1, source_target_pairs={{0,4},{1,5},{2,6},{3,7},{8,12},{9,13},{10,14},{11,15},{16,20},{17,... | collective-permute-start | bytes 18440 | tf_op jit(solution)/shard_map/ppermute | solution.py:1183
  106.5 40.8 %collective-permute-start.2 = (bf16[1024,384]{1,0:T(8,128)(2,1)}, bf16[1024,384]{1,0:T(8,128)(2,1)}, u32[]{:S(2)}, u32[]{:S(2)}) collective-permute-start(bf16[1024,384]{1,0:T(8,128)(2,1)} %slice.102), channel_id=1, source_target_pairs={{0,4},{1,5},{2,6},{3,7},{8,12},{9,13},{10,14},{11,15},{16,20},{17,... | collective-permute-start | bytes 2359304 | tf_op jit(solution)/shard_map/ppermute | solution.py:1183
  125.0 22.3 %collective-permute-start.4 = (bf16[1024,128]{1,0:T(8,128)(2,1)}, bf16[1024,128]{1,0:T(8,128)(2,1)S(1)}, u32[]{:S(2)}, u32[]{:S(2)}) collective-permute-start(bf16[1024,128]{1,0:T(8,128)(2,1)} %get-tuple-element.126), channel_id=1, source_target_pairs={{0,4},{1,5},{2,6},{3,7},{8,12},{9,13},{10,14},{11,15},{16,20},{17,... | collective-permute-start | bytes 786440 | tf_op jit(solution)/shard_map/ppermute | solution.py:1183
  135.4 22.8 %collective-permute-start.3 = (bf16[1024,128]{1,0:T(8,128)(2,1)}, bf16[1024,128]{1,0:T(8,128)(2,1)S(1)}, u32[]{:S(2)}, u32[]{:S(2)}) collective-permute-start(bf16[1024,128]{1,0:T(8,128)(2,1)} %get-tuple-element.120), channel_id=1, source_target_pairs={{0,4},{1,5},{2,6},{3,7},{8,12},{9,13},{10,14},{11,15},{16,20},{17,... | collective-permute-start | bytes 786440 | tf_op jit(solution)/shard_map/ppermute | solution.py:1183
  146.0 22.6 %collective-permute-start.1 = (bf16[1024,128]{1,0:T(8,128)(2,1)}, bf16[1024,128]{1,0:T(8,128)(2,1)S(1)}, u32[]{:S(2)}, u32[]{:S(2)}) collective-permute-start(bf16[1024,128]{1,0:T(8,128)(2,1)} %get-tuple-element.114), channel_id=1, source_target_pairs={{0,4},{1,5},{2,6},{3,7},{8,12},{9,13},{10,14},{11,15},{16,20},{17,... | collective-permute-start | bytes 786440 | tf_op jit(solution)/shard_map/ppermute | solution.py:1183
  181.2 14.5 %all-to-all-start = ((bf16[4,256,384]{1,2,0:T(8,128)(2,1)}), bf16[4,256,384]{1,2,0:T(8,128)(2,1)S(1)}, u32[]{:S(2)}, u32[]{:S(2)}) async-start(bf16[4,256,384]{1,2,0:T(8,128)(2,1)} %copy.50), calls=%async_computation | async-start | bytes 1572864 | tf_op jit(solution)/shard_map/all_to_all | solution.py:1297
  184.9 176.4 %reduce-scatter.3.cloned.1.call-start = ((), (), s32[]{:S(2)}) async-start(), calls=%async_computation.4 | async-start | bytes 3538944 | tf_op jit(solution)/shard_map/reduce_scatter | solution.py:1318
  260.9 33.4 %copy-start.43 = (pred[256]{0:T(512)(128)(4,1)}, pred[256]{0:T(512)(128)(4,1)S(1)}, u32[]{:S(2)}) copy-start(pred[256]{0:T(512)(128)(4,1)S(1)} %add_compare_fusion.1) | copy-start | bytes 772
  271.1 22.8 %copy-start.10 = (f32[256,1536]{1,0:T(8,128)S(1)}, f32[256,1536]{1,0:T(8,128)}, u32[]{:S(2)}) copy-start(f32[256,1536]{1,0:T(8,128)} %copy-done.9) | copy-start | bytes 4718596
  298.7 28.5 %collective-permute-start.5 = (bf16[1536,768]{1,0:T(8,128)(2,1)}, bf16[1536,768]{1,0:T(8,128)(2,1)}, u32[]{:S(2)}, u32[]{:S(2)}) collective-permute-start(bf16[1536,768]{1,0:T(8,128)(2,1)} %dynamic-slice_convert_fusion), channel_id=1, source_target_pairs={{0,2},{2,0},{1,3},{3,1},{4,6},{6,4},{5,7},{7,5},{8,10},{10,8},{9,1... | collective-permute-start | bytes 7077896 | tf_op jit(solution)/shard_map/ppermute | solution.py:1177
  302.3 29.8 %all-to-all-start.1 = ((bf16[256,4,384]{2,0,1:T(8,128)(2,1)}), bf16[256,4,384]{2,0,1:T(8,128)(2,1)}, u32[]{:S(2)}, u32[]{:S(2)}) async-start(bf16[256,4,384]{2,0,1:T(8,128)(2,1)} %bitcast.126), calls=%async_computation.1 | async-start | bytes 1572864 | tf_op jit(solution)/shard_map/all_to_all | solution.py:1328
  306.9 161.3 %reduce-scatter.5.cloned.1.call-start = ((), (), s32[]{:S(2)}) async-start(), calls=%async_computation.5 | async-start | bytes 7077888 | tf_op jit(solution)/shard_map/reduce_scatter | solution.py:1319
  332.2 15.8 %collective-permute-start.6 = (bf16[768,384]{1,0:T(8,128)(2,1)S(1)}, bf16[768,384]{1,0:T(8,128)(2,1)S(1)}, u32[]{:S(2)}, u32[]{:S(2)}) collective-permute-start(bf16[768,384]{1,0:T(8,128)(2,1)S(1)} %get-tuple-element.238), channel_id=1, source_target_pairs={{0,1},{1,0},{2,3},{3,2},{4,5},{5,4},{6,7},{7,6},{8,9},{9,8},{10,11... | collective-permute-start | bytes 1769480 | tf_op jit(solution)/shard_map/ppermute | solution.py:1177
  333.6 27.7 %collective-permute-start.7 = (bf16[768,384]{1,0:T(8,128)(2,1)S(1)}, bf16[768,384]{1,0:T(8,128)(2,1)S(1)}, u32[]{:S(2)}, u32[]{:S(2)}) collective-permute-start(bf16[768,384]{1,0:T(8,128)(2,1)S(1)} %get-tuple-element.237), channel_id=1, source_target_pairs={{0,1},{1,0},{2,3},{3,2},{4,5},{5,4},{6,7},{7,6},{8,9},{9,8},{10,11... | collective-permute-start | bytes 1769480 | tf_op jit(solution)/shard_map/ppermute | solution.py:1177
  346.7 33.4 %collective-permute-start.11 = (bf16[2,1024,128]{2,1,0:T(8,128)(2,1)}, bf16[2,1024,128]{2,1,0:T(8,128)(2,1)S(1)}, u32[]{:S(2)}, u32[]{:S(2)}) collective-permute-start(bf16[2,1024,128]{2,1,0:T(8,128)(2,1)} %get-tuple-element.179), channel_id=1, source_target_pairs={{4,0},{5,1},{6,2},{7,3},{12,8},{13,9},{14,10},{15,11},{20,16},{21,... | collective-permute-start | bytes 1572872 | tf_op jit(solution)/shard_map/ppermute | solution.py:1183
  348.0 30.8 %slice-start.5 = ((s8[4718592]{0:T(1024)(128)(4,1)}), s8[524288]{0:T(1024)(128)(4,1)S(1)}, s32[]{:S(2)}) async-start(s8[4718592]{0:T(1024)(128)(4,1)} %bitcast.119), calls=%async_computation.12 | async-start | bytes 1048576
  361.3 18.8 %collective-permute-start.8 = (bf16[128,1536]{1,0:T(8,128)(2,1)}, bf16[128,1536]{1,0:T(8,128)(2,1)S(1)}, u32[]{:S(2)}, u32[]{:S(2)}) collective-permute-start(bf16[128,1536]{1,0:T(8,128)(2,1)} %reduce-scatter.3.cloned.1.call-done), channel_id=1, source_target_pairs={{0,1},{1,0},{2,3},{3,2},{4,5},{5,4},{6,7},{7,6},{8,9},{9,8},{10,11... | collective-permute-start | bytes 1179656 | tf_op jit(solution)/shard_map/ppermute | solution.py:1177
  375.7 46.4 %collective-permute-start.9 = (bf16[2,1024,128]{2,1,0:T(8,128)(2,1)}, bf16[2,1024,128]{2,1,0:T(8,128)(2,1)S(1)}, u32[]{:S(2)}, u32[]{:S(2)}) collective-permute-start(bf16[2,1024,128]{2,1,0:T(8,128)(2,1)} %get-tuple-element.161), channel_id=1, source_target_pairs={{4,0},{5,1},{6,2},{7,3},{12,8},{13,9},{14,10},{15,11},{20,16},{21,... | collective-permute-start | bytes 1572872 | tf_op jit(solution)/shard_map/ppermute | solution.py:1183
  377.0 31.3 %collective-permute-start.10 = (bf16[2,1024,128]{2,1,0:T(8,128)(2,1)S(1)}, bf16[2,1024,128]{2,1,0:T(8,128)(2,1)}, u32[]{:S(2)}, u32[]{:S(2)}) collective-permute-start(bf16[2,1024,128]{2,1,0:T(8,128)(2,1)S(1)} %copy-done.49), channel_id=1, source_target_pairs={{4,0},{5,1},{6,2},{7,3},{12,8},{13,9},{14,10},{15,11},{20,16},{21,... | collective-permute-start | bytes 1572872 | tf_op jit(solution)/shard_map/ppermute | solution.py:1183
  422.9 19.1 %copy-start.24 = (bf16[128,1536]{1,0:T(8,128)(2,1)S(1)}, bf16[128,1536]{1,0:T(8,128)(2,1)}, u32[]{:S(2)}) copy-start(bf16[128,1536]{1,0:T(8,128)(2,1)} %reduce-scatter.3.cloned.1.call-done) | copy-start | bytes 1179652
  437.8 9.2 %collective-permute-start.12 = (f32[8,384]{1,0:T(8,128)S(1)}, f32[8,384]{1,0:T(8,128)S(1)}, u32[]{:S(2)}, u32[]{:S(2)}) collective-permute-start(f32[8,384]{1,0:T(8,128)S(1)} %pad_maximum_fusion.5), channel_id=1, source_target_pairs={{4,0},{5,1},{6,2},{7,3},{12,8},{13,9},{14,10},{15,11},{20,16},{21,... | collective-permute-start | bytes 36872 | tf_op jit(solution)/shard_map/ppermute | solution.py:1183
  468.1 92.2 %copy-start.2 = (bf16[1,256,1536]{2,1,0:T(8,128)(2,1)S(1)}, bf16[1,256,1536]{2,1,0:T(8,128)(2,1)}, u32[]{:S(2)}) copy-start(bf16[1,256,1536]{2,1,0:T(8,128)(2,1)} %param.11) | copy-start | bytes 2359300
  468.2 92.2 %copy-start.29 = (f32[1536]{0:T(1024)S(1)}, f32[1536]{0:T(1024)}, u32[]{:S(2)}) copy-start(f32[1536]{0:T(1024)} %copy-done.28) | copy-start | bytes 18436
  (57 other events, 296.2 us)
Sparse Core Ops, SparseCore 0:
  93.0 135.7 all-gather.2
  261.0 76.3 reduce-scatter.2
  341.0 122.7 reduce-scatter.4

commit v6 on v5

--- a/solution.py
+++ b/solution.py
@@ -342,7 +342,7 @@
 def prep(projected, rim, kernel, logits, head, heads):
     count = projected.shape[0]
     sq = jax.ShapeDtypeStruct((count, CH), bf16)
-    unroll = 8 if count % (8 * CH) == 0 else 4
+    unroll = 4
     return pl.pallas_call(
         functools.partial(prep_kernel, unroll, head),
         grid=(1,),

time: 585 us -> 592 us (1.012)
  Pallas kernels: 362 us -> 370 us
    pallas_call x3, Pallas kernels: 27.3 us -> 34 us  [prep(): pl.pallas_call(functools.partial(prep_kernel, unroll, head), grid=(1,), i...]
  transfers between devices with their start and end apart: 18 -> 18, of which waited for: 3 -> 2; matrix products, arithmetic and copies ran while one was open for 16% -> 16% of each run, Pallas kernels for 31% -> 32%
where the time goes in v6:
time: 592 us; the launch traced here: 583 us
  Pallas kernels  370 us (62%)
  matrix products  85 us (14%)
  local copies, waits for them, and re-layouts  32.7 us (6%)
  other arithmetic  31.1 us (5%)
  starting transfers between devices  26.1 us (4%)
  waiting for transfers between devices  23 us (4%)
  between operations  15.6 us (3%)
    pallas_call x1, Pallas kernels, scatter_last(): pl.pallas_call(functools.partial(scatter_kernel, row_count, y_count, feat...  91.5 us
    pallas_call x1, Pallas kernels, gather_first(): pl.pallas_call(functools.partial(gather_kernel, row_count, y_count, featu...  79.3 us
    pallas_call x3, Pallas kernels, prep_back(): pl.pallas_call(functools.partial(prep_back_kernel, unroll, head), grid=(1...  41.7 us
    pallas_call x3, Pallas kernels, attend_back(): pl.pallas_call(attend_back_kernel, grid=(1,), in_specs=[c, c, column(coun...  39.5 us
    pallas_call x3, Pallas kernels, prep(): pl.pallas_call(functools.partial(prep_kernel, unroll, head), grid=(1,), i...  34 us
    pallas_call x3, Pallas kernels, attend(): pl.pallas_call(attend_kernel, grid=(1,), in_specs=[pl.BlockSpec(memory_sp...  29 us
    pallas_call x1, Pallas kernels, group_sum(): pl.pallas_call(group_sum_kernel, in_specs=[pl.BlockSpec(memory_space=pltp...  22.6 us
    unnamed x133, local copies, waits for them, and re-layouts  22.5 us
  transfers between devices with their start and end apart: 18, of which 2 were waited for; matrix products, arithmetic and copies ran while one was open for 16% of the time, Pallas kernels for 32%

profile of v6, /device:TPU:1, one launch (start us, length us, event | category | flops | bytes accessed | tf_op | source)
XLA Modules:
  0.0 583.2 jit_solution(2686224731035814530)
XLA Ops:
  13.6 79.3 %gather_first.1 = (bf16[4,2,2,96,1536]{4,3,2,1,0:T(8,128)(2,1)}, bf16[4,2,2,32,128]{4,3,2,1,0:T(8,128)(2,1)S(1)}, bf16[4,2,2,96,1536]{4,3,2,1,0:T(8,128)(2,1)}, ...) custom-call(bf16[96,6144]{1,0:T(8,128)(2,1)S(1)} %copy-done.5, ...), custom_call_target="tpu_custom_call" | custom-call | tf_op jit(solution)/shard_map/gather_first/pallas_call | solution.py:665
  115.4 11.3 %prep.5 = (bf16[1024,128]{1,0:T(8,128)(2,1)}, bf16[1024,128]{1,0:T(8,128)(2,1)}, bf16[1024,128]{1,0:T(8,128)(2,1)}, bf16[1024,128]{1,0:T(8,128)(2,1)}, bf16[1024...) custom-call(bf16[1024,1536]{1,0:T(8,128)(2,1)} %copy-done.30, ...), custom_call_target="tpu_custom_call" | custom-call | flops 10240000000 | bytes 4194304 | tf_op jit(solution)/shard_map/prep/pallas_call | solution.py:346
  128.2 11.3 %prep.4 = (bf16[1024,128]{1,0:T(8,128)(2,1)}, bf16[1024,128]{1,0:T(8,128)(2,1)}, bf16[1024,128]{1,0:T(8,128)(2,1)}, bf16[1024,128]{1,0:T(8,128)(2,1)}, bf16[1024...) custom-call(bf16[1024,1536]{1,0:T(8,128)(2,1)} %copy-done.30, ...), custom_call_target="tpu_custom_call" | custom-call | flops 10240000000 | bytes 4194304 | tf_op jit(solution)/shard_map/prep/pallas_call | solution.py:346
  140.9 11.3 %prep.3 = (bf16[1024,128]{1,0:T(8,128)(2,1)}, bf16[1024,128]{1,0:T(8,128)(2,1)}, bf16[1024,128]{1,0:T(8,128)(2,1)}, bf16[1024,128]{1,0:T(8,128)(2,1)}, bf16[1024...) custom-call(bf16[1024,1536]{1,0:T(8,128)(2,1)} %copy-done.30, ...), custom_call_target="tpu_custom_call" | custom-call | flops 10240000000 | bytes 4194304 | tf_op jit(solution)/shard_map/prep/pallas_call | solution.py:346
  154.2 9.7 %attend.5 = (bf16[1024,128]{1,0:T(8,128)(2,1)}, bf16[1024,1024]{1,0:T(8,128)(2,1)}, bf16[1024,1024]{1,0:T(8,128)(2,1)}, bf16[7,1024,128]{2,1,0:T(8,128)(2,1)}, bf16[1024,128]{1,0:T(8,128)(2,1)}) custom-call(s32[1]{0:T(128)} %bitcast.2.far_ref, bf16[1024,128]{1,0:T(8,128)(2,1)} %get-tuple-element.122.qh_ref, bf16[1024,128]{1,0:T(8,128)(2,1)} %get-tuple-element.123.kh_ref, ...), custom_call_target="tpu_custom_call" | custom-call | flops 10240000000 | bytes 4194304 | tf_op jit(solution)/shard_map/attend/pallas_call | solution.py:366
  164.6 9.7 %attend.4 = (bf16[1024,128]{1,0:T(8,128)(2,1)}, bf16[1024,1024]{1,0:T(8,128)(2,1)}, bf16[1024,1024]{1,0:T(8,128)(2,1)}, bf16[7,1024,128]{2,1,0:T(8,128)(2,1)}, bf16[1024,128]{1,0:T(8,128)(2,1)}) custom-call(s32[1]{0:T(128)} %bitcast.2.far_ref, bf16[1024,128]{1,0:T(8,128)(2,1)} %get-tuple-element.116.qh_ref, bf16[1024,128]{1,0:T(8,128)(2,1)} %get-tuple-element.117.kh_ref, ...), custom_call_target="tpu_custom_call" | custom-call | flops 10240000000 | bytes 4194304 | tf_op jit(solution)/shard_map/attend/pallas_call | solution.py:366
  175.0 9.7 %attend.3 = (bf16[1024,128]{1,0:T(8,128)(2,1)}, bf16[1024,1024]{1,0:T(8,128)(2,1)}, bf16[1024,1024]{1,0:T(8,128)(2,1)}, bf16[7,1024,128]{2,1,0:T(8,128)(2,1)}, bf16[1024,128]{1,0:T(8,128)(2,1)}) custom-call(s32[1]{0:T(128)} %bitcast.2.far_ref, bf16[1024,128]{1,0:T(8,128)(2,1)} %get-tuple-element.110.qh_ref, bf16[1024,128]{1,0:T(8,128)(2,1)} %get-tuple-element.111.kh_ref, ...), custom_call_target="tpu_custom_call" | custom-call | flops 10240000000 | bytes 4194304 | tf_op jit(solution)/shard_map/attend/pallas_call | solution.py:366
  207.1 21.8 %group_gather.1 = bf16[4,256,1536]{2,1,0:T(8,128)(2,1)S(1)} custom-call(bf16[256,1536]{1,0:T(8,128)(2,1)S(1)} %multiply_convert_fusion.5.x_ref), custom_call_target="tpu_custom_call" | custom-call | tf_op jit(solution)/shard_map/group_gather/pallas_call | solution.py:1072
  229.0 10.3 %unpack.1 = (bf16[1536,2048]{1,0:T(8,128)(2,1)}, bf16[1024,1536]{1,0:T(8,128)(2,1)}) custom-call(bf16[8,4608,128]{2,1,0:T(8,128)(2,1)} %bitcast.123), custom_call_target="tpu_custom_call" | custom-call | bytes 18874368 | tf_op jit(solution)/shard_map/unpack/pallas_call | solution.py:1166
  239.3 9.0 %fusion.39 = f32[1024,2048]{0,1:T(8,128)S(1)} fusion(bf16[1024,1536]{1,0:T(8,128)(2,1)S(1)} %bitcast.110, bf16[1536,2048]{1,0:T(8,128)(2,1)} %get-tuple-element.135), kind=kOutput, calls=%fused_computation.114 | convolution fusion | flops 6442450944 | bytes 17825792 | tf_op jit(solution)/shard_map/dot_general | solution.py:1301
  261.0 10.2 %fusion.2 = f32[1024,1536]{1,0:T(8,128)S(1)} fusion(bf16[1536,2048]{1,0:T(8,128)(2,1)} %get-tuple-element.135, bf16[1024,1024]{0,1:T(8,128)(2,1)} %get-tuple-element.233, bf16[1024,1024]{0,1:T(8,128)(2,1)} %get-tuple-element.232), kind=kOutput, calls=%fused_computation.26 | convolution fusion | flops 6450839552 | bytes 16777216 | tf_op jit(solution)/shard_map/tf,df->td/dot_general | solution.py:1314
  271.2 22.6 %group_sum.1 = f32[256,1536]{1,0:T(8,128)S(1)} custom-call(f32[4,256,1536]{2,1,0:T(8,128)S(1)} %bitcast.109), custom_call_target="tpu_custom_call" | custom-call | tf_op jit(solution)/shard_map/group_sum/pallas_call | solution.py:1138
  307.4 11.1 %convolution_convert_fusion.1 = bf16[1536,2048]{1,0:T(8,128)(2,1)} fusion(bf16[1024,1536]{1,0:T(8,128)(2,1)S(1)} %bitcast.111, bf16[1024,1024]{0,1:T(8,128)(2,1)} %get-tuple-element.233, bf16[1024,1024]{0,1:T(8,128)(2,1)} %get-tuple-element.232), kind=kOutput, calls=%fused_computation.1 | convolution fusion | flops 6453985280 | bytes 13631488 | tf_op jit(solution)/shard_map/td,tf->df/dot_general | solution.py:1317
  320.1 6.9 %convolution_convert_fusion.4 = bf16[1024,1536]{1,0:T(8,128)(2,1)} fusion(bf16[1024,1024]{0,1:T(8,128)(2,1)S(1)} %copy-done.55, bf16[1024,1536]{1,0:T(8,128)(2,1)} %get-tuple-element.134), kind=kOutput, calls=%fused_computation.19 | convolution fusion | flops 3222798336 | bytes 8388608 | tf_op jit(solution)/shard_map/dot_general | solution.py:1307
  333.5 13.0 %attend_back.3 = (f32[1024,128]{1,0:T(8,128)}, f32[1024,128]{1,0:T(8,128)}, f32[1024,128]{1,0:T(8,128)}, bf16[1024,128]{1,0:T(8,128)(2,1)}, f32[1024,128]{1,0:T(8,128)}, /*index=5*/bf16[2,1024,128]{2,1,0:T(8,128)(2,1)}) custom-call(bf16[1024,128]{1,0:T(8,128)(2,1)} %get-tuple-element.111.kh_ref, bf16[1024,128]{1,0:T(8,128)(2,1)} %get-tuple-element.112.p_ref, ...), custom_call_target="tpu_custom_call" | custom-call | flops 30720000000 | bytes 8388608 | tf_op jit(solution)/shard_map/attend_back/pallas_call | solution.py:387
  347.8 13.6 %attend_back.4 = (f32[1024,128]{1,0:T(8,128)}, f32[1024,128]{1,0:T(8,128)}, f32[1024,128]{1,0:T(8,128)}, bf16[1024,128]{1,0:T(8,128)(2,1)}, f32[1024,128]{1,0:T(8,128)}, /*index=5*/bf16[2,1024,128]{2,1,0:T(8,128)(2,1)}) custom-call(bf16[1024,128]{1,0:T(8,128)(2,1)} %get-tuple-element.117.kh_ref, bf16[1024,128]{1,0:T(8,128)(2,1)} %get-tuple-element.118.p_ref, ...), custom_call_target="tpu_custom_call" | custom-call | flops 30720000000 | bytes 8388608 | tf_op jit(solution)/shard_map/attend_back/pallas_call | solution.py:387
  362.9 13.0 %attend_back.5 = (f32[1024,128]{1,0:T(8,128)}, f32[1024,128]{1,0:T(8,128)}, f32[1024,128]{1,0:T(8,128)}, bf16[1024,128]{1,0:T(8,128)(2,1)}, f32[1024,128]{1,0:T(8,128)}, /*index=5*/bf16[2,1024,128]{2,1,0:T(8,128)(2,1)}) custom-call(bf16[1024,128]{1,0:T(8,128)(2,1)} %get-tuple-element.123.kh_ref, bf16[1024,128]{1,0:T(8,128)(2,1)} %get-tuple-element.124.p_ref, ...), custom_call_target="tpu_custom_call" | custom-call | flops 30720000000 | bytes 8388608 | tf_op jit(solution)/shard_map/attend_back/pallas_call | solution.py:387
  381.0 13.8 %prep_back.3 = (bf16[1024,1536]{1,0:T(8,128)(2,1)}, f32[8,128]{1,0:T(8,128)}, f32[8,128]{1,0:T(8,128)}, f32[8,128]{1,0:T(8,128)}, f32[8,128]{1,0:T(8,128)}) custom-call(bf16[1024,1536]{1,0:T(8,128)(2,1)} %copy-done.30, bf16[1024,1536]{1,0:T(8,128)(2,1)} %copy-done.30, bf16[1024,1536]{1,0:T(8,128)(2,1)} %copy-done.30, bf16[8,384]{1,0:T(8,128)(2,1)} %copy-done.53, ...), custom_call_target="tpu_custom_call" | custom-call | flops 30720000000 | bytes 8388608 | tf_op jit(solution)/shard_map/prep_back/pallas_call | solution.py:410
  394.8 16.1 %collective-permute-done.10.dfar_ref = bf16[2,1024,128]{2,1,0:T(8,128)(2,1)} collective-permute-done((bf16[2,1024,128]{2,1,0:T(8,128)(2,1)S(1)}, bf16[2,1024,128]{2,1,0:T(8,128)(2,1)}, u32[]{:S(2)}, u32[]{:S(2)}) %collective-permute-start.10) | collective-permute-done | bytes 524320 | tf_op jit(solution)/shard_map/ppermute | solution.py:1183
  410.9 13.8 %prep_back.4 = (bf16[1024,1536]{1,0:T(8,128)(2,1)}, f32[8,128]{1,0:T(8,128)}, f32[8,128]{1,0:T(8,128)}, f32[8,128]{1,0:T(8,128)}, f32[8,128]{1,0:T(8,128)}) custom-call(bf16[1024,1536]{1,0:T(8,128)(2,1)} %copy-done.30, bf16[1024,1536]{1,0:T(8,128)(2,1)} %copy-done.30, bf16[1024,1536]{1,0:T(8,128)(2,1)} %copy-done.30, ...), custom_call_target="tpu_custom_call", output_to_operand_aliasing={{0}: (16, {})} | custom-call | flops 30720000000 | bytes 8388608 | tf_op jit(solution)/shard_map/prep_back/pallas_call | solution.py:410
  425.6 14.0 %prep_back.5 = (bf16[1024,1536]{1,0:T(8,128)(2,1)}, f32[8,128]{1,0:T(8,128)}, f32[8,128]{1,0:T(8,128)}, f32[8,128]{1,0:T(8,128)}, f32[8,128]{1,0:T(8,128)}) custom-call(bf16[1024,1536]{1,0:T(8,128)(2,1)} %copy-done.30, bf16[1024,1536]{1,0:T(8,128)(2,1)} %copy-done.30, bf16[1024,1536]{1,0:T(8,128)(2,1)} %copy-done.30, ...), custom_call_target="tpu_custom_call", output_to_operand_aliasing={{0}: (16, {})} | custom-call | flops 30720000000 | bytes 8388608 | tf_op jit(solution)/shard_map/prep_back/pallas_call | solution.py:410
  450.3 10.1 %fusion = (bf16[1024,1536]{1,0:T(8,128)(2,1)}, bf16[1536]{0:T(1024)(128)(2,1)S(1)}) fusion(bf16[1024,1536]{1,0:T(8,128)(2,1)} %convolution_convert_fusion.2, f32[1024]{0:T(1024)S(1)} %bitcast.140, bf16[4,256,1536]{2,1,0:T(8,128)(2,1)S(1)} %copy-done.13, bf16[1024,1536]{1,0:T(8,128)(2,1)} %fusion.29, bf16[1536,1536]{1,0:T(8,128)(2,1)} %bitcast.144), kind=kOutput, calls=%fused_computation.10 | convolution fusion | flops 4842846720 | bytes 17308672 | tf_op jit(solution)/shard_map/tn,dn->td/dot_general | solution.py:1377
  461.5 9.3 %convolution_convert_fusion = bf16[1536,1536]{1,0:T(8,128)(2,1)} fusion(bf16[1024,1536]{1,0:T(8,128)(2,1)} %copy-done.14, bf16[1024,1536]{1,0:T(8,128)(2,1)} %fusion.29), kind=kOutput, calls=%fused_computation | convolution fusion | flops 4834197504 | bytes 11010048 | tf_op jit(solution)/shard_map/td,tn->dn/dot_general | solution.py:1375
  470.8 91.5 %scatter_last.1 = (bf16[96,6144]{1,0:T(8,128)(2,1)}, bf16[4,96,128]{2,1,0:T(8,128)(2,1)}, bf16[4,96,384]{2,1,0:T(8,128)(2,1)}, bf16[96,8192]{1,0:T(8,128)(2,1)},...) custom-call(bf16[8,192,1536]{2,1,0:T(8,128)(2,1)} %bitcast.125, bf16[8,192,128]{2,1,0:T(8,128)(2,1)} %bitcast.131, ...), custom_call_target="tpu_custom_call" | custom-call | tf_op jit(solution)/shard_map/scatter_last/pallas_call | solution.py:1018
  (248 shorter events, 125.3 us)
Async XLA Ops:
  7.2 221.8 %all-gather.3.cloned.1.call-start = ((), (), s32[]{:S(2)}) async-start(), calls=%async_computation.6 | async-start | bytes 10616832 | tf_op jit(solution)/shard_map/all_gather | solution.py:1251
  103.4 11.4 %collective-permute-start = (bf16[8,384]{1,0:T(8,128)(2,1)S(1)}, bf16[8,384]{1,0:T(8,128)(2,1)S(1)}, u32[]{:S(2)}, u32[]{:S(2)}) collective-permute-start(bf16[8,384]{1,0:T(8,128)(2,1)S(1)} %slice.99), channel_id=1, source_target_pairs={{0,4},{1,5},{2,6},{3,7},{8,12},{9,13},{10,14},{11,15},{16,20},{17,... | collective-permute-start | bytes 18440 | tf_op jit(solution)/shard_map/ppermute | solution.py:1183
  106.5 47.0 %collective-permute-start.2 = (bf16[1024,384]{1,0:T(8,128)(2,1)}, bf16[1024,384]{1,0:T(8,128)(2,1)}, u32[]{:S(2)}, u32[]{:S(2)}) collective-permute-start(bf16[1024,384]{1,0:T(8,128)(2,1)} %slice.102), channel_id=1, source_target_pairs={{0,4},{1,5},{2,6},{3,7},{8,12},{9,13},{10,14},{11,15},{16,20},{17,... | collective-permute-start | bytes 2359304 | tf_op jit(solution)/shard_map/ppermute | solution.py:1183
  126.8 26.7 %collective-permute-start.4 = (bf16[1024,128]{1,0:T(8,128)(2,1)}, bf16[1024,128]{1,0:T(8,128)(2,1)S(1)}, u32[]{:S(2)}, u32[]{:S(2)}) collective-permute-start(bf16[1024,128]{1,0:T(8,128)(2,1)} %get-tuple-element.126), channel_id=1, source_target_pairs={{0,4},{1,5},{2,6},{3,7},{8,12},{9,13},{10,14},{11,15},{16,20},{17,... | collective-permute-start | bytes 786440 | tf_op jit(solution)/shard_map/ppermute | solution.py:1183
  139.6 24.3 %collective-permute-start.3 = (bf16[1024,128]{1,0:T(8,128)(2,1)}, bf16[1024,128]{1,0:T(8,128)(2,1)S(1)}, u32[]{:S(2)}, u32[]{:S(2)}) collective-permute-start(bf16[1024,128]{1,0:T(8,128)(2,1)} %get-tuple-element.120), channel_id=1, source_target_pairs={{0,4},{1,5},{2,6},{3,7},{8,12},{9,13},{10,14},{11,15},{16,20},{17,... | collective-permute-start | bytes 786440 | tf_op jit(solution)/shard_map/ppermute | solution.py:1183
  152.2 22.1 %collective-permute-start.1 = (bf16[1024,128]{1,0:T(8,128)(2,1)}, bf16[1024,128]{1,0:T(8,128)(2,1)S(1)}, u32[]{:S(2)}, u32[]{:S(2)}) collective-permute-start(bf16[1024,128]{1,0:T(8,128)(2,1)} %get-tuple-element.114), channel_id=1, source_target_pairs={{0,4},{1,5},{2,6},{3,7},{8,12},{9,13},{10,14},{11,15},{16,20},{17,... | collective-permute-start | bytes 786440 | tf_op jit(solution)/shard_map/ppermute | solution.py:1183
  186.9 14.5 %all-to-all-start = ((bf16[4,256,384]{1,2,0:T(8,128)(2,1)}), bf16[4,256,384]{1,2,0:T(8,128)(2,1)S(1)}, u32[]{:S(2)}, u32[]{:S(2)}) async-start(bf16[4,256,384]{1,2,0:T(8,128)(2,1)} %copy.50), calls=%async_computation | async-start | bytes 1572864 | tf_op jit(solution)/shard_map/all_to_all | solution.py:1297
  190.6 170.9 %reduce-scatter.3.cloned.1.call-start = ((), (), s32[]{:S(2)}) async-start(), calls=%async_computation.4 | async-start | bytes 3538944 | tf_op jit(solution)/shard_map/reduce_scatter | solution.py:1318
  261.0 33.3 %copy-start.43 = (pred[256]{0:T(512)(128)(4,1)}, pred[256]{0:T(512)(128)(4,1)S(1)}, u32[]{:S(2)}) copy-start(pred[256]{0:T(512)(128)(4,1)S(1)} %add_compare_fusion.1) | copy-start | bytes 772
  271.2 22.6 %copy-start.10 = (f32[256,1536]{1,0:T(8,128)S(1)}, f32[256,1536]{1,0:T(8,128)}, u32[]{:S(2)}) copy-start(f32[256,1536]{1,0:T(8,128)} %copy-done.9) | copy-start | bytes 4718596
  298.6 28.3 %collective-permute-start.5 = (bf16[1536,768]{1,0:T(8,128)(2,1)}, bf16[1536,768]{1,0:T(8,128)(2,1)}, u32[]{:S(2)}, u32[]{:S(2)}) collective-permute-start(bf16[1536,768]{1,0:T(8,128)(2,1)} %dynamic-slice_convert_fusion), channel_id=1, source_target_pairs={{0,2},{2,0},{1,3},{3,1},{4,6},{6,4},{5,7},{7,5},{8,10},{10,8},{9,1... | collective-permute-start | bytes 7077896 | tf_op jit(solution)/shard_map/ppermute | solution.py:1177
  302.2 29.6 %all-to-all-start.1 = ((bf16[256,4,384]{2,0,1:T(8,128)(2,1)}), bf16[256,4,384]{2,0,1:T(8,128)(2,1)}, u32[]{:S(2)}, u32[]{:S(2)}) async-start(bf16[256,4,384]{2,0,1:T(8,128)(2,1)} %bitcast.126), calls=%async_computation.1 | async-start | bytes 1572864 | tf_op jit(solution)/shard_map/all_to_all | solution.py:1328
  306.8 164.0 %reduce-scatter.5.cloned.1.call-start = ((), (), s32[]{:S(2)}) async-start(), calls=%async_computation.5 | async-start | bytes 7077888 | tf_op jit(solution)/shard_map/reduce_scatter | solution.py:1319
  332.0 15.8 %collective-permute-start.6 = (bf16[768,384]{1,0:T(8,128)(2,1)S(1)}, bf16[768,384]{1,0:T(8,128)(2,1)S(1)}, u32[]{:S(2)}, u32[]{:S(2)}) collective-permute-start(bf16[768,384]{1,0:T(8,128)(2,1)S(1)} %get-tuple-element.238), channel_id=1, source_target_pairs={{0,1},{1,0},{2,3},{3,2},{4,5},{5,4},{6,7},{7,6},{8,9},{9,8},{10,11... | collective-permute-start | bytes 1769480 | tf_op jit(solution)/shard_map/ppermute | solution.py:1177
  333.4 28.0 %collective-permute-start.7 = (bf16[768,384]{1,0:T(8,128)(2,1)S(1)}, bf16[768,384]{1,0:T(8,128)(2,1)S(1)}, u32[]{:S(2)}, u32[]{:S(2)}) collective-permute-start(bf16[768,384]{1,0:T(8,128)(2,1)S(1)} %get-tuple-element.237), channel_id=1, source_target_pairs={{0,1},{1,0},{2,3},{3,2},{4,5},{5,4},{6,7},{7,6},{8,9},{9,8},{10,11... | collective-permute-start | bytes 1769480 | tf_op jit(solution)/shard_map/ppermute | solution.py:1177
  346.5 33.7 %collective-permute-start.11 = (bf16[2,1024,128]{2,1,0:T(8,128)(2,1)}, bf16[2,1024,128]{2,1,0:T(8,128)(2,1)S(1)}, u32[]{:S(2)}, u32[]{:S(2)}) collective-permute-start(bf16[2,1024,128]{2,1,0:T(8,128)(2,1)} %get-tuple-element.179), channel_id=1, source_target_pairs={{4,0},{5,1},{6,2},{7,3},{12,8},{13,9},{14,10},{15,11},{20,16},{21,... | collective-permute-start | bytes 1572872 | tf_op jit(solution)/shard_map/ppermute | solution.py:1183
  347.8 31.1 %slice-start.5 = ((s8[4718592]{0:T(1024)(128)(4,1)}), s8[524288]{0:T(1024)(128)(4,1)S(1)}, s32[]{:S(2)}) async-start(s8[4718592]{0:T(1024)(128)(4,1)} %bitcast.119), calls=%async_computation.12 | async-start | bytes 1048576
  361.5 18.7 %collective-permute-start.8 = (bf16[128,1536]{1,0:T(8,128)(2,1)}, bf16[128,1536]{1,0:T(8,128)(2,1)S(1)}, u32[]{:S(2)}, u32[]{:S(2)}) collective-permute-start(bf16[128,1536]{1,0:T(8,128)(2,1)} %reduce-scatter.3.cloned.1.call-done), channel_id=1, source_target_pairs={{0,1},{1,0},{2,3},{3,2},{4,5},{5,4},{6,7},{7,6},{8,9},{9,8},{10,11... | collective-permute-start | bytes 1179656 | tf_op jit(solution)/shard_map/ppermute | solution.py:1177
  375.8 48.9 %collective-permute-start.9 = (bf16[2,1024,128]{2,1,0:T(8,128)(2,1)}, bf16[2,1024,128]{2,1,0:T(8,128)(2,1)S(1)}, u32[]{:S(2)}, u32[]{:S(2)}) collective-permute-start(bf16[2,1024,128]{2,1,0:T(8,128)(2,1)} %get-tuple-element.161), channel_id=1, source_target_pairs={{4,0},{5,1},{6,2},{7,3},{12,8},{13,9},{14,10},{15,11},{20,16},{21,... | collective-permute-start | bytes 1572872 | tf_op jit(solution)/shard_map/ppermute | solution.py:1183
  377.1 33.8 %collective-permute-start.10 = (bf16[2,1024,128]{2,1,0:T(8,128)(2,1)S(1)}, bf16[2,1024,128]{2,1,0:T(8,128)(2,1)}, u32[]{:S(2)}, u32[]{:S(2)}) collective-permute-start(bf16[2,1024,128]{2,1,0:T(8,128)(2,1)S(1)} %copy-done.49), channel_id=1, source_target_pairs={{4,0},{5,1},{6,2},{7,3},{12,8},{13,9},{14,10},{15,11},{20,16},{21,... | collective-permute-start | bytes 1572872 | tf_op jit(solution)/shard_map/ppermute | solution.py:1183
  425.6 19.1 %copy-start.24 = (bf16[128,1536]{1,0:T(8,128)(2,1)S(1)}, bf16[128,1536]{1,0:T(8,128)(2,1)}, u32[]{:S(2)}) copy-start(bf16[128,1536]{1,0:T(8,128)(2,1)} %reduce-scatter.3.cloned.1.call-done) | copy-start | bytes 1179652
  440.5 9.2 %collective-permute-start.12 = (f32[8,384]{1,0:T(8,128)S(1)}, f32[8,384]{1,0:T(8,128)S(1)}, u32[]{:S(2)}, u32[]{:S(2)}) collective-permute-start(f32[8,384]{1,0:T(8,128)S(1)} %pad_maximum_fusion.5), channel_id=1, source_target_pairs={{4,0},{5,1},{6,2},{7,3},{12,8},{13,9},{14,10},{15,11},{20,16},{21,... | collective-permute-start | bytes 36872 | tf_op jit(solution)/shard_map/ppermute | solution.py:1183
  470.8 93.4 %copy-start.2 = (bf16[1,256,1536]{2,1,0:T(8,128)(2,1)S(1)}, bf16[1,256,1536]{2,1,0:T(8,128)(2,1)}, u32[]{:S(2)}) copy-start(bf16[1,256,1536]{2,1,0:T(8,128)(2,1)} %param.11) | copy-start | bytes 2359300
  470.8 93.4 %copy-start.29 = (f32[1536]{0:T(1024)S(1)}, f32[1536]{0:T(1024)}, u32[]{:S(2)}) copy-start(f32[1536]{0:T(1024)} %copy-done.28) | copy-start | bytes 18436
  (57 other events, 295.3 us)
Sparse Core Ops, SparseCore 0:
  93.0 135.7 all-gather.2
  261.1 78.3 reduce-scatter.2
  343.0 122.8 reduce-scatter.4
